TPU v7x, 32 devices: a whole 2x2x4 slice. The times are simulated.
32 devices in a mesh: grp: 4 (over x, core), fsdp: 8 (over z, y).
Axes of the slice: x: 2, y: 2, z: 4, core: 2. Of those that a mesh axis runs over, the one named last changes fastest.
Arguments:
- expert_momentum: float32 [96, 512, 2048], P('grp', 'fsdp'), may hold values from -1500 to 1500
- expert_grad: float32 [96, 512, 2048], P('grp', 'fsdp'), may hold values from -3000 to 3000
- wide_momentum: float32 [4, 2048, 4096], P('grp', None, 'fsdp'), may hold values from -1500 to 1500
- wide_grad: float32 [4, 2048, 4096], P('grp', None, 'fsdp'), may hold values from -3000 to 3000
- assignment: int32 [96], replicated, may hold values from 0 to 7, as said below
- expert_tokens: int32 [96], replicated, may hold values from 16 to 1023
Outputs:
- expert_updates: float32 [96, 512, 2048], P('grp', 'fsdp')
- wide_updates: float32 [4, 2048, 4096], P('grp', None, 'fsdp')
- worker_updates: float32 [32, 6, 512, 2048], P(('grp', 'fsdp'))
Inputs may be any that keep to these rules, and one draw needn't show every extreme that they name: `assignment`: within each group of 24 consecutive experts no worker gets more than 6 experts; at least one worker, and possibly several, gets exactly 6.
All inputs are finite; a program needn't handle non-finite values.
Results may differ from a plain program's by a relative error of at most 0.012.
Values may be sent and summed in bfloat16 or wider, within the bound.
No kernel may reach another device: no remote copies, remote signals or barrier semaphores. Data moves between devices by JAX's collectives and lax.ppermute only.
A program may use at most 256 MiB of HBM per device.

v0:
```python
import math

import jax
import jax.numpy as jnp
from jax import lax
from jax.sharding import PartitionSpec as P

D = 2048
AW = 4096
ITERS = 2


COEF_A = 3.4445
COEF_B = -4.775
COEF_C = 2.0315
BETA = 0.95
EPS = 1e-06


def polish(current, gram):
    gram_low = gram.astype(jnp.bfloat16)
    first = jnp.dot(gram_low, current.astype(jnp.bfloat16), preferred_element_type=jnp.float32)
    second = jnp.dot(gram_low, first.astype(jnp.bfloat16), preferred_element_type=jnp.float32)
    return COEF_A * current + COEF_B * first + COEF_C * second


def whole_gram(matrix):
    low = matrix.astype(jnp.bfloat16)
    return jnp.dot(low, low.T, preferred_element_type=jnp.float32)


def summed_gram(matrix):
    low = matrix.astype(jnp.bfloat16)
    part = jnp.dot(low, low.T, preferred_element_type=jnp.float32)
    return lax.psum(part.astype(jnp.bfloat16), "fsdp").astype(jnp.float32)


def newton_schulz(merged, gram_fn):
    current = merged
    for step in range(ITERS):
        if step == 0:
            summed = gram_fn(merged)
            norm_sq = jnp.trace(summed) + EPS
            current = merged / jnp.sqrt(norm_sq)
            gram = summed / norm_sq
        else:
            gram = gram_fn(current)
        current = polish(current, gram)
    return current


def solve_one(matrix):
    return newton_schulz(matrix, whole_gram)


def solve_items(items):
    return lax.map(solve_one, items)


def on_device(expert_momentum, expert_grad, wide_momentum, wide_grad, assignment, expert_tokens):
    members = lax.axis_size("fsdp")
    expert_merged = BETA * expert_momentum + expert_grad
    wide_merged = BETA * wide_momentum[0] + wide_grad[0]
    wide_out = newton_schulz(wide_merged, summed_gram) * math.sqrt(AW)
    per_group = expert_merged.shape[0]
    rows = expert_merged.shape[1]
    group_index = lax.axis_index("grp")
    workers = lax.dynamic_slice_in_dim(assignment, group_index * per_group, per_group)
    tokens = expert_tokens.astype(jnp.float32)
    own_tokens = lax.dynamic_slice_in_dim(tokens, group_index * per_group, per_group)
    factor = jnp.sqrt(own_tokens / jnp.mean(tokens)) * math.sqrt(D)
    order = jnp.arange(per_group, dtype=jnp.int32)
    earlier = (workers[:, None] == workers[None, :]) & (order[None, :] < order[:, None])
    rank = jnp.sum(earlier.astype(jnp.int32), axis=1)
    most = 2 * -(-per_group // members)
    slot_ids = jnp.arange(most, dtype=jnp.int32)
    peer_ids = jnp.arange(members, dtype=jnp.int32)
    picks = (
        (rank[None, None, :] == slot_ids[:, None, None])
        & (workers[None, None, :] == peer_ids[None, :, None])
    ).astype(jnp.float32)
    hold = -(-per_group // members)
    holder = order % members
    place = order // members
    hold_ids = jnp.arange(hold, dtype=jnp.int32)
    spread = (
        (place[None, None, :] == hold_ids[:, None, None])
        & (holder[None, None, :] == peer_ids[None, :, None])
    ).astype(jnp.float32)
    outgoing = jnp.einsum("skj,jrd->skrd", spread, expert_merged, precision=lax.Precision.HIGHEST)
    outgoing = outgoing.reshape(hold, members * rows, D)
    results = solve_items(lax.all_to_all(outgoing, "fsdp", split_axis=1, concat_axis=1, tiled=True))
    returned = lax.all_to_all(results, "fsdp", split_axis=1, concat_axis=1, tiled=True)
    returned = returned.reshape(hold, members, rows, D)
    expert_out = returned[place, holder] * factor[:, None, None]
    sending = jnp.einsum("skj,jrd->skrd", picks, expert_out, precision=lax.Precision.HIGHEST)
    sending = sending.reshape(most, members * rows, D)
    worker_out = lax.all_to_all(sending, "fsdp", split_axis=1, concat_axis=1, tiled=True)
    return (expert_out, wide_out[None], worker_out[None])


def solution(mesh):
    placed = (
        P("grp", "fsdp", None),
        P("grp", "fsdp", None),
        P("grp", None, "fsdp"),
        P("grp", None, "fsdp"),
        P(),
        P(),
    )
    return jax.shard_map(
        on_device,
        mesh=mesh,
        in_specs=placed,
        out_specs=(
            P("grp", "fsdp", None),
            P("grp", None, "fsdp"),
            P(("grp", "fsdp"), None, None, None),
        ),
        check_vma=False,
    )
```

profile of v0, /device:TPU:0, one launch (start us, length us, event | category | flops | bytes accessed | tf_op | source)
XLA Modules:
  0.0 2587.8 jit_solution(11304797851966336031)
XLA Ops:
  7.2 9.3 multiply_add_fusion
  16.6 13.9 fusion.16
  30.5 16.6 copy.26
  47.1 18.1 copy.27
  65.1 7.3 all-to-all-start
  72.5 363.0 %all-to-all-done = f32[3,512,2048]{2,0,1:T(4,128)} async-done(((f32[3,512,2048]{2,0,1:T(4,128)}), f32[3,512,2048]{2,0,1:T(4,128)}, u32[]{:S(2)}, u32[]{:S(2)}) %all-to-all-start) | async-done | bytes 12582944 | tf_op jit(solution)/shard_map/all_to_all | solution.py:92
  435.4 317.5 %while.10 = (s32[]{:T(128)}, f32[3,512,2048]{2,0,1:T(4,128)}, f32[3,512,2048]{2,0,1:T(4,128)}, s32[]{:T(128)}, f32[]{:T(128)}, /*index=5*/s32[]{:T(128)}) while((s32[]{:T(128)}, f32[3,512,2048]{2,0,1:T(4,128)}, f32[3,512,2048]{2,0,1:T(4,128)}, s32[]{:T(128)}, f32[]{:T(128)}, /*index=5*/s32[]{:T(128)}) %tuple.29), condition=%wide.region_2.3_spmd, body=%wide.region_0.2_spmd.sunk | while | flops 6462373888 | bytes 113770680 | solution.py:57
  435.8 7.4 constant_dynamic-slice_fusion.2
  443.3 2.0 copy-done
  445.3 3.0 select_reduce_fusion.2
  448.9 4.0 fusion.69
  453.0 2.8 fusion.70
  455.7 1.3 convolution_convert_fusion.4
  457.0 1.3 fusion.71
  458.3 1.8 add_bitcast_fusion.2
  460.1 6.3 copy.69
  466.5 75.0 %dynamic_update_slice.5 = f32[3,512,2048]{2,0,1:T(4,128)} dynamic-update-slice(f32[3,512,2048]{2,0,1:T(4,128)} %get-tuple-element.71, f32[1,512,2048]{2,0,1:T(1,128)} %copy.69, s32[]{:T(128)S(6)} %copy.73, s32[]{:T(128)} %constant.78.clone.1..sunk, s32[]{:T(128)} %constant.78.clone.1..sunk) | dynamic-update-slice | bytes 8388612 | tf_op jit(solution)/shard_map/while/body/jit(dynamic_update_index_in_dim)/dynamic_update_slice | solution.py:57
  541.5 7.4 constant_dynamic-slice_fusion.2
  548.9 2.0 copy-done
  550.9 3.0 select_reduce_fusion.2
  554.6 4.0 fusion.69
  558.6 2.8 fusion.70
  561.4 1.3 convolution_convert_fusion.4
  562.7 1.3 fusion.71
  563.9 1.8 add_bitcast_fusion.2
  565.8 6.3 copy.69
  572.1 75.0 %dynamic_update_slice.5 = f32[3,512,2048]{2,0,1:T(4,128)} dynamic-update-slice(f32[3,512,2048]{2,0,1:T(4,128)} %get-tuple-element.71, f32[1,512,2048]{2,0,1:T(1,128)} %copy.69, s32[]{:T(128)S(6)} %copy.73, s32[]{:T(128)} %constant.78.clone.1..sunk, s32[]{:T(128)} %constant.78.clone.1..sunk) | dynamic-update-slice | bytes 8388612 | tf_op jit(solution)/shard_map/while/body/jit(dynamic_update_index_in_dim)/dynamic_update_slice | solution.py:57
  647.1 7.4 constant_dynamic-slice_fusion.2
  654.6 2.0 copy-done
  656.6 3.0 select_reduce_fusion.2
  660.2 4.0 fusion.69
  664.3 2.8 fusion.70
  667.0 1.3 convolution_convert_fusion.4
  668.3 1.3 fusion.71
  669.6 1.8 add_bitcast_fusion.2
  671.4 6.3 copy.69
  677.8 75.0 %dynamic_update_slice.5 = f32[3,512,2048]{2,0,1:T(4,128)} dynamic-update-slice(f32[3,512,2048]{2,0,1:T(4,128)} %get-tuple-element.71, f32[1,512,2048]{2,0,1:T(1,128)} %copy.69, s32[]{:T(128)S(6)} %copy.73, s32[]{:T(128)} %constant.78.clone.1..sunk, s32[]{:T(128)} %constant.78.clone.1..sunk) | dynamic-update-slice | bytes 8388612 | tf_op jit(solution)/shard_map/while/body/jit(dynamic_update_index_in_dim)/dynamic_update_slice | solution.py:57
  753.0 5.7 all-to-all-start.1
  758.7 0.6 convert_reduce_fusion.1
  760.0 0.1 dynamic_slice.11
  760.1 0.1 sqrt_multiply_fusion
  760.2 0.2 convert_reduce_fusion
  760.4 360.4 %all-to-all-done.1 = f32[3,512,2048]{2,0,1:T(4,128)} async-done(((f32[3,512,2048]{2,0,1:T(4,128)}), f32[3,512,2048]{2,0,1:T(4,128)}, u32[]{:S(2)}, u32[]{:S(2)}) %all-to-all-start.1) | async-done | bytes 12582944 | tf_op jit(solution)/shard_map/all_to_all | solution.py:93
  1120.8 17.8 copy.30
  1138.6 12.1 gather_fusion
  1150.7 12.3 broadcast_multiply_fusion
  1163.0 28.1 %fusion.14 = f32[6,8,64,2048]{3,1,2,0:T(8,128)} fusion(f32[24,64,2048]{2,1,0:T(8,128)} %broadcast_multiply_fusion, pred[8,24]{1,0:T(8,128)(4,1)S(1)} %iota_compare_fusion.3, pred[6,24]{1,0:T(8,128)(4,1)S(1)} %iota_compare_fusion.4), kind=kOutput, calls=%fused_computation.26 | convolution fusion | flops 1811940480 | bytes 37749072 | tf_op jit(solution)/shard_map/skj,jrd->skrd/dot_general | solution.py:96
  1191.1 22.1 copy.32
  1213.2 37.9 %copy.33 = f32[6,512,2048]{2,0,1:T(8,128)} copy(f32[6,512,2048]{2,1,0:T(8,128)S(1)} %bitcast.64) | data formatting | bytes 50331648 | tf_op jit(solution)/shard_map/reshape | solution.py:97
  1251.1 7.1 all-to-all-start.2
  1258.1 0.2 all-reduce.3.cloned.1.call-start
  1258.4 13.9 convolution_convert_fusion.2
  1272.3 0.0 all-reduce.3.cloned.1.call-update
  1272.3 0.0 all-reduce.5.cloned.1.call-start
  1272.4 956.6 %all-reduce.3.cloned.1.call-done = bf16[2048,2048]{1,0:T(8,128)(2,1)} async-done(((bf16[2048,2048]{1,0:T(8,128)(2,1)}), bf16[2048,2048]{1,0:T(8,128)(2,1)}) %all-reduce.3.cloned.1.call-update) | async-done | bytes 8388624 | tf_op jit(solution)/shard_map/psum | solution.py:35
  2229.0 4.3 fusion.12
  2234.0 12.6 fusion.21
  2246.6 11.6 fusion.20
  2258.2 11.4 convolution_convert_fusion.1
  2269.6 0.0 all-reduce.5.cloned.1.call-update
  2269.6 269.2 %all-reduce.5.cloned.1.call-done = bf16[2048,2048]{1,0:T(8,128)(2,1)} async-done(((bf16[2048,2048]{1,0:T(8,128)(2,1)}), bf16[2048,2048]{1,0:T(8,128)(2,1)}) %all-reduce.5.cloned.1.call-update) | async-done | bytes 8388624 | tf_op jit(solution)/shard_map/psum | solution.py:35
  2538.9 8.3 fusion.28
  2547.2 7.0 multiply_bitcast_fusion
  2554.2 26.5 %copy.34 = f32[1,6,512,2048]{3,2,1,0:T(8,128)} copy(f32[1,6,512,2048]{3,1,2,0:T(8,128)} %bitcast.18) | data formatting | bytes 50331648
  (31 shorter events, 0.1 us)
Async XLA Ops:
  65.1 370.3 %all-to-all-start = ((f32[3,512,2048]{2,0,1:T(4,128)}), f32[3,512,2048]{2,0,1:T(4,128)}, u32[]{:S(2)}, u32[]{:S(2)}) async-start(f32[3,512,2048]{2,0,1:T(4,128)} %copy.27), calls=%async_computation | async-start | bytes 33554432 | tf_op jit(solution)/shard_map/all_to_all | solution.py:92
  443.3 2.0 copy-start
  448.9 4.1 copy-start.1
  548.9 2.0 copy-start
  554.5 4.1 copy-start.1
  654.5 2.0 copy-start
  660.2 4.1 copy-start.1
  752.9 5.8 copy-start.5
  752.9 7.0 copy-start.6
  753.0 367.8 %all-to-all-start.1 = ((f32[3,512,2048]{2,0,1:T(4,128)}), f32[3,512,2048]{2,0,1:T(4,128)}, u32[]{:S(2)}, u32[]{:S(2)}) async-start(f32[3,512,2048]{2,0,1:T(4,128)} %get-tuple-element.20), calls=%async_computation.1 | async-start | bytes 33554432 | tf_op jit(solution)/shard_map/all_to_all | solution.py:93
  1251.1 1303.1 %all-to-all-start.2 = ((f32[6,512,2048]{2,0,1:T(8,128)}), f32[6,512,2048]{2,0,1:T(8,128)}, u32[]{:S(2)}, u32[]{:S(2)}) async-start(f32[6,512,2048]{2,0,1:T(8,128)} %copy.33), calls=%async_computation.2 | async-start | bytes 67108864 | tf_op jit(solution)/shard_map/all_to_all | solution.py:98
  1258.1 970.9 %all-reduce.3.cloned.1.call-start = ((), (), s32[]{:S(2)}) async-start(), calls=%async_computation.3 | async-start | bytes 16777216 | tf_op jit(solution)/shard_map/psum | solution.py:35
  1272.3 1266.5 %all-reduce.5.cloned.1.call-start = ((), (), s32[]{:S(2)}) async-start(), calls=%async_computation.4 | async-start | bytes 16777216 | tf_op jit(solution)/shard_map/psum | solution.py:35
  2234.0 12.6 copy-start.2
  2234.0 12.6 copy-start.4
  2538.9 8.3 copy-start.3
  2538.9 8.3 copy-start.7
Sparse Core Ops, SparseCore 0:
  1272.4 956.5 all-reduce.2
  2269.7 269.0 all-reduce.4
where the time goes:
time: 2600 us; the launch traced here: 2590 us
  waiting for transfers between devices  1950 us (75%)
  local copies, waits for them, and re-layouts  424 us (16%)
  matrix products  149 us (6%)
  other arithmetic  26.8 us (1%)
    psum x2, waiting for transfers between devices, summed_gram(): return lax.psum(part.astype(jnp.bfloat16), 'fsdp').astype(jnp.float32)  1230 us
    all_to_all x1, waiting for transfers between devices, on_device(): lax.all_to_all(outgoing, 'fsdp', split_axis=1, concat_axis=1, tiled=True)  363 us
    all_to_all x1, waiting for transfers between devices, on_device(): lax.all_to_all(results, 'fsdp', split_axis=1, concat_axis=1, tiled=True)  360 us
    dynamic_update_slice x6, local copies, waits for them, and re-layouts, solve_items(): return lax.map(solve_one, items)  244 us
  transfers between devices with their start and end apart: 5, of which 4 were waited for; matrix products, arithmetic and copies ran while one was open for 3% of the time, Pallas kernels for 0%

commit v1 on v0

v1 whole, which is shorter than its diff:
```python
import functools
import math

import jax
import jax.numpy as jnp
from jax import lax
from jax.experimental import pallas as pl
from jax.experimental.pallas import tpu as pltpu
from jax.sharding import PartitionSpec as P

COEF_A = 3.4445
COEF_B = -4.775
COEF_C = 2.0315
BETA = 0.95
EPS = 1e-06

F16_TOP = 32768.0
SMALLEST = 1e-30
BLOCK = 256

F32 = jnp.float32
BF16 = jnp.bfloat16

SMEM_SPEC = pl.BlockSpec(memory_space=pltpu.SMEM)
ANY_SPEC = pl.BlockSpec(memory_space=pl.ANY)


def dot(left, right):
    return jnp.dot(left, right, preferred_element_type=F32)


def dot_nt(left, right):
    return lax.dot_general(left, right, (((1,), (1,)), ((), ())), preferred_element_type=F32)


def cost(flops, bytes_accessed):
    return pl.CostEstimate(flops=int(flops), bytes_accessed=int(bytes_accessed), transcendentals=0)


def route_kernel(members, most, per_group, base_ref, assign_ref, table_ref, count_ref):
    half_members = members // 2
    base = base_ref[0]
    for i in range(members * most):
        table_ref[i] = per_group - 1
    for j in range(members):
        count_ref[j] = 0

    def own(e, carry):
        worker = assign_ref[base + e]
        rank = count_ref[worker]
        table_ref[worker * most + rank] = e
        count_ref[worker] = rank + 1
        return carry

    lax.fori_loop(0, per_group, own, 0)
    for half in range(2):
        first = half * half_members
        last = first + half_members - 1

        def other(e, carry):
            holder, slot = carry
            worker = assign_ref[base + e]
            mine = jnp.logical_and(worker >= first, worker <= last)
            for _ in range(half_members - 1):
                full = slot >= most
                following = jnp.minimum(holder + 1, last)
                slot = jnp.where(full, count_ref[following], slot)
                holder = jnp.where(full, following, holder)

            @pl.when(jnp.logical_not(mine))
            def _():
                table_ref[holder * most + slot] = e

            return holder, jnp.where(mine, slot, slot + 1)

        lax.fori_loop(0, per_group, other, (jnp.int32(first), count_ref[first]))


def route(base, assignment, members, most, per_group):
    return pl.pallas_call(
        functools.partial(route_kernel, members, most, per_group),
        out_shape=(
            jax.ShapeDtypeStruct((members * most,), jnp.int32),
            jax.ShapeDtypeStruct((members,), jnp.int32),
        ),
        in_specs=[SMEM_SPEC, SMEM_SPEC],
        out_specs=(SMEM_SPEC, SMEM_SPEC),
        name="route",
    )(base, assignment)


def merge_kernel(momentum_ref, grad_ref, scaled_ref, top_ref):
    merged = BETA * momentum_ref[...] + grad_ref[...]
    top = jnp.maximum(jnp.max(jnp.abs(merged), axis=(1, 2), keepdims=True), SMALLEST)
    scaled_ref[...] = merged * (F16_TOP / top)
    top_ref[...] = jnp.broadcast_to(top, top_ref.shape)


def merge(momentum, grad):
    per_group, rows, width = momentum.shape
    spec = pl.BlockSpec((1, rows, width), lambda i: (i, 0, 0))
    return pl.pallas_call(
        merge_kernel,
        grid=(per_group,),
        out_shape=(
            jax.ShapeDtypeStruct(momentum.shape, F32),
            jax.ShapeDtypeStruct((per_group, 8, 128), F32),
        ),
        in_specs=[spec, spec],
        out_specs=(spec, pl.BlockSpec((1, 8, 128), lambda i: (i, 0, 0))),
        name="merge",
        cost_estimate=cost(5 * momentum.size, momentum.size * 12),
    )(momentum, grad)


def solve_kernel(
    members, half_members, first_slot,
    row_ref, scale_ref, keep_ref, factor_ref, data_ref, *rest,
):
    work_ref, back_ref, whole, low = rest[-4:]
    rows = data_ref.shape[2]
    size, width = whole.shape
    slot = first_slot + pl.program_id(0)
    tile = min(512, width)

    for member in range(members):
        part = data_ref[member, 0] * scale_ref[slot * members + member]
        whole[pl.ds(member * rows, rows), :] = part
        low[pl.ds(member * rows, rows), :] = part.astype(BF16)

    gram = jnp.zeros((size, size), F32)
    for k in range(width // tile):
        block = low[:, k * tile:(k + 1) * tile]
        gram = gram + dot_nt(block, block)
    row_ids = lax.broadcasted_iota(jnp.int32, (size, size), 0)
    col_ids = lax.broadcasted_iota(jnp.int32, (size, size), 1)
    norm_sq = jnp.sum(jnp.where(row_ids == col_ids, gram, 0.0), keepdims=True) + EPS
    inverse = lax.rsqrt(norm_sq)
    g0 = gram / norm_sq
    g0_low = g0.astype(BF16)
    square = dot(g0_low, g0_low)
    cube = dot(g0_low, square.astype(BF16))
    u = COEF_B * g0 + COEF_C * square
    t = COEF_B * square + COEF_C * cube
    u_low = u.astype(BF16)
    g1 = (COEF_A * COEF_A) * g0 + (2 * COEF_A) * t + dot(u_low, t.astype(BF16))
    g1_low = g1.astype(BF16)
    v = COEF_B * g1 + COEF_C * dot(g1_low, g1_low)
    mix = (COEF_A * (u + v) + dot(v.astype(BF16), u_low)).astype(BF16)
    factor = factor_ref[slot]
    keep = keep_ref[slot]
    for k in range(width // tile):
        cols = slice(k * tile, (k + 1) * tile)
        moved = dot(mix, low[:, cols])
        result = ((COEF_A * COEF_A) * whole[:, cols] + moved) * inverse
        work_ref[0, :, cols] = result * factor
        whole[:, cols] = result * keep
    first_row = pl.multiple_of(row_ref[0], half_members * rows)
    for member in range(half_members):
        back_ref[member, 0] = whole[pl.ds(first_row + member * rows, rows), :]


def solve(first_row, scale, keep, factor, data, work, first_slot, most, half_members):
    members, chunk, rows, width = data.shape
    size = members * rows
    inputs = [first_row, scale, keep, factor, data]
    specs = [SMEM_SPEC] * 4 + [pl.BlockSpec((members, 1, rows, width), lambda i: (0, i, 0, 0))]
    aliases = {}
    if work is not None:
        inputs.append(work)
        specs.append(ANY_SPEC)
        aliases = {5: 0}
    flops = chunk * (4 * size * size * width + 10 * size ** 3)
    return pl.pallas_call(
        functools.partial(solve_kernel, members, half_members, first_slot),
        grid=(chunk,),
        out_shape=(
            jax.ShapeDtypeStruct((most, size, width), F32),
            jax.ShapeDtypeStruct((half_members, chunk, rows, width), F32),
        ),
        in_specs=specs,
        out_specs=(
            pl.BlockSpec((1, size, width), lambda i: (first_slot + i, 0, 0)),
            pl.BlockSpec((half_members, 1, rows, width), lambda i: (0, i, 0, 0)),
        ),
        scratch_shapes=[pltpu.VMEM((size, width), F32), pltpu.VMEM((size, width), BF16)],
        input_output_aliases=aliases,
        name=f"solve{first_slot}",
        cost_estimate=cost(flops, data.size * 12),
    )(*inputs)


def home_kernel(ids_ref, factor_ref, data_ref, *rest):
    rest[-1][...] = data_ref[0] * factor_ref[pl.program_id(0)]


def home(ids, factor, data, out, per_group):
    half_members, chunk, rows, width = data.shape
    inputs = [ids, factor, data]
    specs = [
        SMEM_SPEC,
        pl.BlockSpec((1, 1, rows, width), lambda i, ids: (i // chunk, i % chunk, 0, 0)),
    ]
    aliases = {}
    if out is not None:
        inputs.append(out)
        specs.append(ANY_SPEC)
        aliases = {3: 0}
    return pl.pallas_call(
        home_kernel,
        grid_spec=pltpu.PrefetchScalarGridSpec(
            num_scalar_prefetch=1,
            grid=(half_members * chunk,),
            in_specs=specs,
            out_specs=pl.BlockSpec((1, rows, width), lambda i, ids: (ids[i], 0, 0)),
        ),
        out_shape=jax.ShapeDtypeStruct((per_group, rows, width), F32),
        input_output_aliases=aliases,
        name="home",
        cost_estimate=cost(1e8, data.size * 8),
    )(*inputs)


def wide_gram_kernel(momentum_ref, grad_ref, merged_ref, packed_ref, sum_ref, low):
    i = pl.program_id(0)
    merged = BETA * momentum_ref[...] + grad_ref[...]
    merged_ref[...] = merged
    rounded = merged.astype(BF16)
    low[pl.ds(pl.multiple_of(i * BLOCK, BLOCK), BLOCK), :] = rounded

    @pl.when(i == 0)
    def _():
        sum_ref[...] = jnp.zeros_like(sum_ref)

    squares = jnp.square(rounded.astype(F32))
    sum_ref[...] += jnp.sum(squares, axis=(0, 1), keepdims=True)
    start = i * (i + 1) // 2

    def column(j, carry):
        other = low[pl.ds(pl.multiple_of(j * BLOCK, BLOCK), BLOCK), :]
        place = pl.multiple_of((start + j) * BLOCK, BLOCK)
        packed_ref[pl.ds(place, BLOCK), :] = dot_nt(rounded, other).astype(BF16)
        return carry

    lax.fori_loop(0, i + 1, column, 0)


def wide_gram(momentum, grad):
    height, width = momentum.shape
    number = height // BLOCK
    packed = number * (number + 1) // 2 * BLOCK
    row_spec = pl.BlockSpec((BLOCK, width), lambda i: (i, 0))
    return pl.pallas_call(
        wide_gram_kernel,
        grid=(number,),
        out_shape=(
            jax.ShapeDtypeStruct((height, width), F32),
            jax.ShapeDtypeStruct((packed, BLOCK), BF16),
            jax.ShapeDtypeStruct((8, 128), F32),
        ),
        in_specs=[row_spec, row_spec],
        out_specs=(
            row_spec,
            pl.BlockSpec((packed, BLOCK), lambda i: (0, 0)),
            pl.BlockSpec((8, 128), lambda i: (0, 0)),
        ),
        scratch_shapes=[pltpu.VMEM((height, width), BF16)],
        name="wide_gram",
        cost_estimate=cost(packed * BLOCK * width * 2, height * width * 12 + packed * BLOCK * 2),
    )(momentum, grad)


def wide_solve_kernel(coef_ref, packed_ref, merged_ref, out_ref, gram, first, second, one, two):
    height, width = out_ref.shape
    number = height // BLOCK
    inverse, inverse_sq, outer = coef_ref[0], coef_ref[1], coef_ref[2]

    def assemble(i, carry):
        rows = pl.ds(pl.multiple_of(i * BLOCK, BLOCK), BLOCK)

        def column(j, inner):
            cols = pl.ds(pl.multiple_of(j * BLOCK, BLOCK), BLOCK)
            place = pl.multiple_of((i * (i + 1) // 2 + j) * BLOCK, BLOCK)
            block = packed_ref[pl.ds(place, BLOCK), :]
            gram[cols, rows] = block.T
            gram[rows, cols] = block
            return inner

        return lax.fori_loop(0, i + 1, column, carry)

    lax.fori_loop(0, number, assemble, 0)

    def sweep(source, step):
        def body(i, carry):
            rows = pl.ds(pl.multiple_of(i * BLOCK, BLOCK), BLOCK)
            step(rows, dot(gram[rows, :], source[...]) * inverse_sq)
            return carry

        lax.fori_loop(0, number, body, 0)

    def prepare(i, carry):
        rows = pl.ds(pl.multiple_of(i * BLOCK, BLOCK), BLOCK)
        value = merged_ref[rows, :] * inverse
        first[rows, :] = value
        one[rows, :] = value.astype(BF16)
        return carry

    lax.fori_loop(0, number, prepare, 0)

    def inner_of(base, target):
        def step(rows, product):
            target[rows, :] = (COEF_B * base[rows, :] + COEF_C * product).astype(BF16)
        return step

    def outer_of(base, wide, target):
        def step(rows, product):
            value = COEF_A * base[rows, :] + product
            if wide is not None:
                wide[rows, :] = value
            target[rows, :] = value.astype(BF16)
        return step

    def plain(wide, target):
        def step(rows, product):
            wide[rows, :] = product
            target[rows, :] = product.astype(BF16)
        return step

    sweep(one, inner_of(first, two))
    sweep(two, outer_of(first, first, one))
    sweep(one, inner_of(first, two))
    sweep(two, outer_of(first, None, one))
    sweep(one, plain(second, two))
    sweep(two, inner_of(second, one))

    def turn(rows, product):
        turned = COEF_A * second[rows, :] + product
        value = COEF_B * first[rows, :] + COEF_C * turned
        second[rows, :] = value
        two[rows, :] = value.astype(BF16)

    sweep(one, turn)
    sweep(two, inner_of(second, one))
    sweep(one, outer_of(second, None, two))
    sweep(two, plain(second, one))
    sweep(one, inner_of(second, two))

    def finish(rows, product):
        value = COEF_A * first[rows, :] + COEF_A * second[rows, :] + product
        out_ref[rows, :] = value * outer

    sweep(two, finish)


def wide_solve(coef, packed, merged):
    height, width = merged.shape
    return pl.pallas_call(
        wide_solve_kernel,
        out_shape=jax.ShapeDtypeStruct((height, width), F32),
        in_specs=[SMEM_SPEC] + [pl.BlockSpec(memory_space=pltpu.VMEM)] * 2,
        out_specs=pl.BlockSpec(memory_space=pltpu.VMEM),
        scratch_shapes=[
            pltpu.VMEM((height, height), BF16),
            pltpu.VMEM((height, width), F32),
            pltpu.VMEM((height, width), F32),
            pltpu.VMEM((height, width), BF16),
            pltpu.VMEM((height, width), BF16),
        ],
        name="wide_solve",
        cost_estimate=cost(24 * height * height * width, height * width * 8),
    )(coef, packed, merged)


def on_device(expert_momentum, expert_grad, wide_momentum, wide_grad, assignment, expert_tokens):
    members = lax.axis_size("fsdp")
    half_members = members // 2
    per_group, rows, width = expert_momentum.shape
    wide_height, wide_width = wide_momentum.shape[1:]
    most = 2 * -(-per_group // members)
    chunk = 2
    group_index = lax.axis_index("grp")
    me = lax.axis_index("fsdp")
    half = me // half_members
    halves = [list(range(half_members)), list(range(half_members, members))]
    mirror = [(i, (i + half_members) % members) for i in range(members)]

    def across(value):
        return lax.all_to_all(value, "fsdp", split_axis=0, concat_axis=0, tiled=True)

    def within(value):
        return lax.all_to_all(
            value, "fsdp", split_axis=0, concat_axis=0, tiled=True, axis_index_groups=halves
        )

    base = (group_index * per_group).astype(jnp.int32).reshape(1)
    table, count = route(base, assignment, members, most, per_group)

    wide_merged, packed, squares = wide_gram(wide_momentum[0], wide_grad[0])
    packed_rows = packed.shape[0] // half_members
    parts = within(packed.reshape(half_members, packed_rows, BLOCK))

    scaled, top = merge(expert_momentum, expert_grad)
    slots = table.reshape(members, most)
    outgoing = []
    for start in range(0, most, chunk):
        picked = scaled[slots[:, start:start + chunk].reshape(-1)].astype(jnp.float16)
        outgoing.append(picked.reshape(members, chunk, rows, width))

    notes = jnp.concatenate([top[:, 0, 0], squares[0, :1]])
    notes = jnp.pad(notes, (0, -notes.shape[0] % 128))
    notes = jnp.broadcast_to(notes[None, None, :], (members, 1, notes.shape[0]))
    notes = across(notes)[:, 0]
    arrived = [across(piece) for piece in outgoing]

    part = jnp.sum(parts.astype(F32), axis=0).astype(BF16)
    other = lax.ppermute(part, "fsdp", mirror)
    part = (part.astype(F32) + other.astype(F32)).astype(BF16)
    packed = within(jnp.broadcast_to(part[None], (half_members,) + part.shape))
    packed = packed.reshape(half_members * packed_rows, BLOCK)
    wide_norm = jnp.sum(notes[:, per_group]) + EPS
    coef = jnp.stack(
        [lax.rsqrt(wide_norm), 1.0 / wide_norm, jnp.float32(math.sqrt(wide_width * members))]
    )
    wide_out = wide_solve(coef, packed, wide_merged)

    tops = notes[:, :per_group]
    keep = F16_TOP / jnp.minimum(2.0, jnp.max(tops, axis=0) * 2e7)
    tokens = expert_tokens.astype(F32)
    own_tokens = lax.dynamic_slice_in_dim(tokens, group_index * per_group, per_group)
    factor = jnp.sqrt(own_tokens / jnp.mean(tokens)) * math.sqrt(width)
    own_slots = lax.dynamic_index_in_dim(slots, me, 0, keepdims=False)
    half_slots = lax.dynamic_slice_in_dim(slots, half * half_members, half_members)
    own_count = lax.dynamic_index_in_dim(count, me, 0, keepdims=False)
    own_pick = own_slots[:, None] == jnp.arange(per_group, dtype=jnp.int32)[None, :]
    half_pick = half_slots[:, :, None] == jnp.arange(per_group, dtype=jnp.int32)
    slot_scale = jnp.sum(jnp.where(own_pick[:, None, :], tops[None], 0.0), axis=2) / F16_TOP
    slot_keep = jnp.sum(jnp.where(own_pick, keep[None], 0.0), axis=1)
    slot_factor = jnp.sum(jnp.where(own_pick, factor[None], 0.0), axis=1)
    slot_factor = jnp.where(jnp.arange(most) < own_count, slot_factor, 0.0)
    home_factor = jnp.sum(jnp.where(half_pick, (factor / keep)[None, None], 0.0), axis=2)
    slot_scale = slot_scale.reshape(-1)
    first_row = (half * half_members * rows).astype(jnp.int32).reshape(1)

    work = None
    expert_out = None
    for index, piece in enumerate(arrived):
        start = index * chunk
        work, back = solve(
            first_row, slot_scale, slot_keep, slot_factor, piece.astype(F32), work,
            start, most, half_members,
        )
        back = within(back.astype(jnp.float16)).astype(F32)
        expert_out = home(
            half_slots[:, start:start + chunk].reshape(-1),
            home_factor[:, start:start + chunk].reshape(-1),
            back, expert_out, per_group,
        )
    return (expert_out, wide_out[None], work[None])


def solution(mesh):
    placed = (
        P("grp", "fsdp", None),
        P("grp", "fsdp", None),
        P("grp", None, "fsdp"),
        P("grp", None, "fsdp"),
        P(),
        P(),
    )
    return jax.shard_map(
        on_device,
        mesh=mesh,
        in_specs=placed,
        out_specs=(
            P("grp", "fsdp", None),
            P("grp", None, "fsdp"),
            P(("grp", "fsdp"), None, None, None),
        ),
        check_vma=False,
    )
```

time: 2600 us -> 696 us (0.27)
  waiting for transfers between devices: 1950 us -> 260 us
  local copies, waits for them, and re-layouts: 424 us -> 40.3 us
  Pallas kernels: 0 us -> 184 us
  matrix products: 149 us -> 0 us
  blocking collectives: 0 us -> 97.3 us
  other arithmetic: 26.8 us -> 67.6 us
    psum x2 -> x0, waiting for transfers between devices: 1230 us -> none  [summed_gram(): return lax.psum(part.astype(jnp.bfloat16), 'fsdp').astype(jnp.float32)]
    all_to_all x3 -> x8, waiting for transfers between devices: 723 us -> 208 us  [the longest x3 155 us: across(): lax.all_to_all(value, 'fsdp', split_axis=0, concat_axis=0, tiled=True)]
    dynamic_update_slice x6 -> x0, local copies, waits for them, and re-layouts: 244 us -> none  [solve_items(): return lax.map(solve_one, items)]
    pallas_call x0 -> x10, Pallas kernels: none -> 184 us  [the longest x1 78.4 us: wide_solve(): pl.pallas_call(wide_solve_kernel, out_shape=jax.ShapeDtypeStruct((height,...]
    dot_general x26 -> x0, matrix products: 149 us -> none  [the longest x8 36.8 us: polish(): jnp.dot(gram_low, current.astype(jnp.bfloat16), preferred_element_type=jn...]
    all_to_all x0 -> x1, blocking collectives: none -> 97.3 us  [across(): lax.all_to_all(value, 'fsdp', split_axis=0, concat_axis=0, tiled=True)]
    convert_element_type x1 -> x14, other arithmetic: 0.01 us -> 58.8 us  [the longest x6 21.8 us: on_device(): back = within(back.astype(jnp.float16)).astype(F32)]
    ppermute x0 -> x1, waiting for transfers between devices: none -> 52 us  [on_device(): other = lax.ppermute(part, 'fsdp', mirror)]
  transfers between devices with their start and end apart: 5 -> 9, of which waited for: 4 -> 6; matrix products, arithmetic and copies ran while one was open for 3% -> 14% of each run, Pallas kernels for 0% -> 10%
where the time goes in v1:
time: 696 us; the launch traced here: 694 us
  waiting for transfers between devices  260 us (37%)
  Pallas kernels  184 us (26%)
  blocking collectives  97.3 us (14%)
  other arithmetic  67.6 us (10%)
  starting transfers between devices  42.3 us (6%)
  local copies, waits for them, and re-layouts  40.3 us (6%)
    all_to_all x3, waiting for transfers between devices, across(): lax.all_to_all(value, 'fsdp', split_axis=0, concat_axis=0, tiled=True)  155 us
    all_to_all x1, blocking collectives, across(): lax.all_to_all(value, 'fsdp', split_axis=0, concat_axis=0, tiled=True)  97.3 us
    pallas_call x1, Pallas kernels, wide_solve(): pl.pallas_call(wide_solve_kernel, out_shape=jax.ShapeDtypeStruct((height,...  78.4 us
    all_to_all x5, waiting for transfers between devices, within(): lax.all_to_all(value, 'fsdp', split_axis=0, concat_axis=0, tiled=True, ax...  53.5 us
    ppermute x1, waiting for transfers between devices, on_device(): other = lax.ppermute(part, 'fsdp', mirror)  52 us
    pallas_call x3, Pallas kernels, solve(): pl.pallas_call(functools.partial(solve_kernel, members, half_members, fir...  43.2 us
    gather x3, local copies, waits for them, and re-layouts, on_device(): scaled[slots[:, start:start + chunk].reshape(-1)].astype(jnp.float16)  27.2 us
    all_to_all x5, starting transfers between devices, within(): lax.all_to_all(value, 'fsdp', split_axis=0, concat_axis=0, tiled=True, ax...  23.3 us
  transfers between devices with their start and end apart: 9, of which 6 were waited for; matrix products, arithmetic and copies ran while one was open for 14% of the time, Pallas kernels for 10%

profile of v1, /device:TPU:0, one launch (start us, length us, event | category | flops | bytes accessed | tf_op | source)
XLA Modules:
  0.0 693.8 jit_solution(12663078254586588940)
XLA Ops:
  0.6 16.4 %wide_gram.1 = (f32[2048,512]{1,0:T(8,128)}, bf16[9216,256]{1,0:T(8,128)(2,1)}, f32[8,128]{1,0:T(8,128)}) custom-call(f32[2048,512]{1,0:T(8,128)} %bitcast.31, f32[2048,512]{1,0:T(8,128)} %bitcast.32), custom_call_target="tpu_custom_call" | custom-call | flops 2415919104 | bytes 17301504 | tf_op jit(solution)/shard_map/wide_gram/pallas_call | solution.py:253
  17.0 1.2 slice.41
  18.2 21.4 %merge.1 = (f32[24,64,2048]{2,1,0:T(8,128)}, f32[24,8,128]{2,1,0:T(8,128)}) custom-call(f32[24,64,2048]{2,1,0:T(8,128)} %momentum_ref.1, f32[24,64,2048]{2,1,0:T(8,128)} %grad_ref.1), custom_call_target="tpu_custom_call" | custom-call | flops 15728640 | bytes 37748736 | tf_op jit(solution)/shard_map/merge/pallas_call | solution.py:102
  39.6 1.2 slice_reduce_fusion
  40.8 0.7 fusion
  41.5 0.6 broadcast_in_dim.84
  42.1 7.3 %all-to-all-start = ((f32[8,1,128]{2,1,0:T(1,128)}), f32[8,1,128]{2,1,0:T(1,128)S(1)}, u32[]{:S(2)}, u32[]{:S(2)}) async-start(f32[8,1,128]{2,1,0:T(1,128)} %broadcast_in_dim.84), calls=%async_computation | async-start | bytes 8192 | tf_op jit(solution)/shard_map/all_to_all | solution.py:388
  49.4 2.5 route.1
  51.9 0.7 reshape.180
  52.8 9.1 %gather_fusion.2 = f32[16,64,2048]{2,1,0:T(8,128)} fusion(f32[24,64,2048]{2,1,0:T(8,128)} %get-tuple-element.20, s32[1024]{0:T(1024)S(1)} %pad_clamp_fusion), kind=kCustom, calls=%fused_computation.2 | custom fusion | bytes 16777280 | tf_op jit(solution)/shard_map/gather | solution.py:406
  61.9 6.0 convert_element_type.71
  67.9 6.0 all-to-all-start.3
  74.1 9.1 %gather_fusion = f32[16,64,2048]{2,1,0:T(8,128)} fusion(f32[24,64,2048]{2,1,0:T(8,128)} %get-tuple-element.20, s32[1024]{0:T(1024)S(1)} %pad_clamp_fusion.2), kind=kCustom, calls=%fused_computation | custom fusion | bytes 16777280 | tf_op jit(solution)/shard_map/gather | solution.py:406
  83.2 6.1 convert_element_type.65
  89.3 77.4 %all-to-all-done.3 = f16[8,2,64,2048]{3,2,1,0:T(8,128)(2,1)} async-done(((f16[8,2,64,2048]{3,2,1,0:T(8,128)(2,1)}), f16[8,2,64,2048]{3,2,1,0:T(8,128)(2,1)}, u32[]{:S(2)}, u32[]{:S(2)}) %all-to-all-start.3) | async-done | bytes 4194336 | tf_op jit(solution)/shard_map/all_to_all | solution.py:388
  166.6 4.5 all-to-all-start.1
  171.2 9.1 %gather_fusion.1 = f32[16,64,2048]{2,1,0:T(8,128)} fusion(f32[24,64,2048]{2,1,0:T(8,128)} %get-tuple-element.20, s32[1024]{0:T(1024)S(1)} %pad_clamp_fusion.1), kind=kCustom, calls=%fused_computation.1 | custom fusion | bytes 16777280 | tf_op jit(solution)/shard_map/gather | solution.py:406
  180.3 6.1 convert_element_type.68
  186.4 77.4 %all-to-all-done.1 = f16[8,2,64,2048]{3,2,1,0:T(8,128)(2,1)} async-done(((f16[8,2,64,2048]{3,2,1,0:T(8,128)(2,1)}), f16[8,2,64,2048]{3,2,1,0:T(8,128)(2,1)}, u32[]{:S(2)}, u32[]{:S(2)}) %all-to-all-start.1) | async-done | bytes 4194336 | tf_op jit(solution)/shard_map/all_to_all | solution.py:388
  263.8 97.3 %all_to_all.45 = f16[8,2,64,2048]{3,2,1,0:T(8,128)(2,1)} all-to-all(f16[8,2,64,2048]{3,2,1,0:T(8,128)(2,1)} %bitcast.27), channel_id=1, replica_groups=mesh['grp'=4,'fsdp'=8] {'fsdp'}, dimensions={0} | all-to-all | bytes 8388608 | tf_op jit(solution)/shard_map/all_to_all | solution.py:388
  361.1 5.3 all-to-all-start.7
  366.4 0.6 convert_reduce_fusion
  367.7 0.6 dynamic_slice.17
  368.5 0.6 div.47.scale_ref
  369.2 0.7 select_reduce_fusion.2
  369.9 1.2 compare_select_fusion.3.factor_ref
  371.1 6.6 convert_element_type.73.data_ref
  377.7 4.2 convert_element_type.70.data_ref
  381.9 6.6 convert_element_type.67.data_ref
  388.4 14.3 %solve0.1 = (f32[6,512,2048]{2,1,0:T(8,128)}, f32[4,2,64,2048]{3,2,1,0:T(8,128)}) custom-call(s32[1]{0:T(128)} %bitcast.5.row_ref, f32[48]{0:T(128)} %div.47.scale_ref, f32[6]{0:T(128)} %get-tuple-element.30.keep_ref, f32[6]{0:T(128)} %compare_select_fusion.3.factor_ref, f32[8,2,64,2048]{3,2,1,0:T(8,128)} %convert_element_type.73.data_ref), custom_call_target="tpu_custom_call" | custom-call | flops 6979321856 | bytes 25165824 | tf_op jit(solution)/shard_map/solve0/pallas_call | solution.py:174
  402.8 14.3 %solve2.1 = (f32[6,512,2048]{2,1,0:T(8,128)}, f32[4,2,64,2048]{3,2,1,0:T(8,128)}) custom-call(s32[1]{0:T(128)} %bitcast.5.row_ref, f32[48]{0:T(128)} %div.47.scale_ref, f32[6]{0:T(128)} %get-tuple-element.30.keep_ref, f32[6]{0:T(128)} %compare_select_fusion.3.factor_ref, ...), custom_call_target="tpu_custom_call", output_to_operand_aliasing={{0}: (5, {})} | custom-call | flops 6979321856 | bytes 25165824 | tf_op jit(solution)/shard_map/solve2/pallas_call | solution.py:174
  417.1 14.6 %solve4.1 = (f32[6,512,2048]{2,1,0:T(8,128)}, f32[4,2,64,2048]{3,2,1,0:T(8,128)}) custom-call(s32[1]{0:T(128)} %bitcast.5.row_ref, f32[48]{0:T(128)} %div.47.scale_ref, f32[6]{0:T(128)} %get-tuple-element.30.keep_ref, f32[6]{0:T(128)} %compare_select_fusion.3.factor_ref, ...), custom_call_target="tpu_custom_call", output_to_operand_aliasing={{0}: (5, {})} | custom-call | flops 6979321856 | bytes 25165824 | tf_op jit(solution)/shard_map/solve4/pallas_call | solution.py:174
  431.6 3.8 convert_element_type.74
  435.5 3.9 all-to-all-start.4
  439.4 3.8 convert_element_type.76
  443.2 19.7 %all-to-all-done.4 = f16[4,2,64,2048]{3,2,1,0:T(8,128)(2,1)S(1)} async-done(((f16[4,2,64,2048]{3,2,1,0:T(8,128)(2,1)}), f16[4,2,64,2048]{3,2,1,0:T(8,128)(2,1)S(1)}, u32[]{:S(2)}, u32[]{:S(2)}) %all-to-all-start.4) | async-done | bytes 2097184 | tf_op jit(solution)/shard_map/all_to_all | solution.py:391
  462.9 4.4 all-to-all-start.5
  467.4 3.8 convert_element_type.78
  471.2 21.3 %all-to-all-done.5 = f16[4,2,64,2048]{3,2,1,0:T(8,128)(2,1)} async-done(((f16[4,2,64,2048]{3,2,1,0:T(8,128)(2,1)}), f16[4,2,64,2048]{3,2,1,0:T(8,128)(2,1)}, u32[]{:S(2)}, u32[]{:S(2)}) %all-to-all-start.5) | async-done | bytes 2097184 | tf_op jit(solution)/shard_map/all_to_all | solution.py:391
  492.5 4.5 all-to-all-start.6
  496.9 3.8 reduce_sum.72
  500.7 1.1 collective-permute-start
  501.8 52.0 %collective-permute-done = bf16[2304,256]{1,0:T(8,128)(2,1)S(1)} collective-permute-done((bf16[2304,256]{1,0:T(8,128)(2,1)S(1)}, bf16[2304,256]{1,0:T(8,128)(2,1)S(1)}, u32[]{:S(2)}, u32[]{:S(2)}) %collective-permute-start) | collective-permute-done | bytes 1179680 | tf_op jit(solution)/shard_map/ppermute | solution.py:416
  553.8 1.3 add_convert_fusion
  555.1 3.7 broadcast_in_dim.94
  558.9 5.2 all-to-all-start.8
  564.3 0.6 reshape.189.ids_ref
  564.9 0.6 reshape.187.ids_ref
  565.5 0.6 reshape.181.ids_ref
  566.1 0.7 slice_reduce_fusion.1
  567.5 0.2 select_reduce_fusion.1
  567.7 0.1 copy.22
  567.8 0.7 reshape.190.factor_ref
  568.5 0.6 reshape.188.factor_ref
  569.3 0.6 reshape.182.factor_ref
  569.9 0.7 pad_maximum_fusion.coef_ref
  570.5 2.4 convert_element_type.75.data_ref
  572.9 4.0 convert_element_type.77.data_ref
  577.0 3.9 convert_element_type.79.data_ref
  580.9 7.3 %home.3.rest_0_ = f32[24,64,2048]{2,1,0:T(8,128)} custom-call(s32[8]{0:T(128)} %reshape.189.ids_ref, f32[8]{0:T(128)} %reshape.190.factor_ref, f32[4,2,64,2048]{3,2,1,0:T(8,128)} %convert_element_type.79.data_ref), custom_call_target="tpu_custom_call" | custom-call | flops 100000000 | bytes 8388608 | tf_op jit(solution)/shard_map/home/pallas_call | solution.py:209
  588.2 7.3 %home.4.rest_0_ = f32[24,64,2048]{2,1,0:T(8,128)} custom-call(s32[8]{0:T(128)} %reshape.187.ids_ref, f32[8]{0:T(128)} %reshape.188.factor_ref, f32[4,2,64,2048]{3,2,1,0:T(8,128)} %convert_element_type.77.data_ref, f32[24,64,2048]{2,1,0:T(8,128)} %home.3.rest_0_), custom_call_target="tpu_custom_call", output_to_operand_aliasing={{}: (3, {})} | custom-call | flops 100000000 | bytes 8388608 | tf_op jit(solution)/shard_map/home/pallas_call | solution.py:209
  595.5 7.3 %home.5 = f32[24,64,2048]{2,1,0:T(8,128)} custom-call(s32[8]{0:T(128)} %reshape.181.ids_ref, f32[8]{0:T(128)} %reshape.182.factor_ref, f32[4,2,64,2048]{3,2,1,0:T(8,128)} %convert_element_type.75.data_ref, f32[24,64,2048]{2,1,0:T(8,128)} %home.4.rest_0_), custom_call_target="tpu_custom_call", output_to_operand_aliasing={{}: (3, {})} | custom-call | flops 100000000 | bytes 8388608 | tf_op jit(solution)/shard_map/home/pallas_call | solution.py:209
  602.9 12.6 %all-to-all-done.8 = bf16[4,2304,256]{2,1,0:T(8,128)(2,1)} async-done(((bf16[4,2304,256]{2,1,0:T(8,128)(2,1)}), bf16[4,2304,256]{2,1,0:T(8,128)(2,1)}, u32[]{:S(2)}, u32[]{:S(2)}) %all-to-all-start.8) | async-done | bytes 4718624 | tf_op jit(solution)/shard_map/all_to_all | solution.py:391
  615.4 78.4 %wide_solve.1 = f32[2048,512]{1,0:T(8,128)} custom-call(f32[3]{0:T(128)} %pad_maximum_fusion.coef_ref, bf16[9216,256]{1,0:T(8,128)(2,1)} %bitcast.17.packed_ref, f32[2048,512]{1,0:T(8,128)} %get-tuple-element.27.merged_ref), custom_call_target="tpu_custom_call" | custom-call | flops 51539607552 | bytes 8388608 | tf_op jit(solution)/shard_map/wide_solve/pallas_call | solution.py:357
  (31 shorter events, 1.0 us)
Async XLA Ops:
  42.1 25.8 %all-to-all-start = ((f32[8,1,128]{2,1,0:T(1,128)}), f32[8,1,128]{2,1,0:T(1,128)S(1)}, u32[]{:S(2)}, u32[]{:S(2)}) async-start(f32[8,1,128]{2,1,0:T(1,128)} %broadcast_in_dim.84), calls=%async_computation | async-start | bytes 8192 | tf_op jit(solution)/shard_map/all_to_all | solution.py:388
  67.9 98.7 %all-to-all-start.3 = ((f16[8,2,64,2048]{3,2,1,0:T(8,128)(2,1)}), f16[8,2,64,2048]{3,2,1,0:T(8,128)(2,1)}, u32[]{:S(2)}, u32[]{:S(2)}) async-start(f16[8,2,64,2048]{3,2,1,0:T(8,128)(2,1)} %bitcast.25), calls=%async_computation.3 | async-start | bytes 8388608 | tf_op jit(solution)/shard_map/all_to_all | solution.py:388
  166.6 97.1 %all-to-all-start.1 = ((f16[8,2,64,2048]{3,2,1,0:T(8,128)(2,1)}), f16[8,2,64,2048]{3,2,1,0:T(8,128)(2,1)}, u32[]{:S(2)}, u32[]{:S(2)}) async-start(f16[8,2,64,2048]{3,2,1,0:T(8,128)(2,1)} %bitcast.26), calls=%async_computation.1 | async-start | bytes 8388608 | tf_op jit(solution)/shard_map/all_to_all | solution.py:388
  361.1 5.3 copy-start.1
  361.1 6.6 copy-start.2
  361.1 74.4 %all-to-all-start.7 = ((bf16[4,2304,256]{2,1,0:T(8,128)(2,1)}), bf16[4,2304,256]{2,1,0:T(8,128)(2,1)}, u32[]{:S(2)}, u32[]{:S(2)}) async-start(bf16[4,2304,256]{2,1,0:T(8,128)(2,1)} %bitcast.28), calls=%async_computation.7 | async-start | bytes 9437184 | tf_op jit(solution)/shard_map/all_to_all | solution.py:391
  371.1 6.6 copy-start
  435.5 27.5 %all-to-all-start.4 = ((f16[4,2,64,2048]{3,2,1,0:T(8,128)(2,1)}), f16[4,2,64,2048]{3,2,1,0:T(8,128)(2,1)S(1)}, u32[]{:S(2)}, u32[]{:S(2)}) async-start(f16[4,2,64,2048]{3,2,1,0:T(8,128)(2,1)} %convert_element_type.74), calls=%async_computation.4 | async-start | bytes 4194304 | tf_op jit(solution)/shard_map/all_to_all | solution.py:391
  462.9 29.6 %all-to-all-start.5 = ((f16[4,2,64,2048]{3,2,1,0:T(8,128)(2,1)}), f16[4,2,64,2048]{3,2,1,0:T(8,128)(2,1)}, u32[]{:S(2)}, u32[]{:S(2)}) async-start(f16[4,2,64,2048]{3,2,1,0:T(8,128)(2,1)} %convert_element_type.76), calls=%async_computation.5 | async-start | bytes 4194304 | tf_op jit(solution)/shard_map/all_to_all | solution.py:391
  492.5 62.7 %all-to-all-start.6 = ((f16[4,2,64,2048]{3,2,1,0:T(8,128)(2,1)}), f16[4,2,64,2048]{3,2,1,0:T(8,128)(2,1)}, u32[]{:S(2)}, u32[]{:S(2)}) async-start(f16[4,2,64,2048]{3,2,1,0:T(8,128)(2,1)} %convert_element_type.78), calls=%async_computation.6 | async-start | bytes 4194304 | tf_op jit(solution)/shard_map/all_to_all | solution.py:391
  500.7 53.1 %collective-permute-start = (bf16[2304,256]{1,0:T(8,128)(2,1)S(1)}, bf16[2304,256]{1,0:T(8,128)(2,1)S(1)}, u32[]{:S(2)}, u32[]{:S(2)}) collective-permute-start(bf16[2304,256]{1,0:T(8,128)(2,1)S(1)} %reduce_sum.72), channel_id=1, source_target_pairs={{0,4},{1,5},{2,6},{3,7},{4,0},{5,1},{6,2},{7,3},{8,12},{9,13},{10,... | collective-permute-start | bytes 3538952 | tf_op jit(solution)/shard_map/ppermute | solution.py:416
  558.9 56.5 %all-to-all-start.8 = ((bf16[4,2304,256]{2,1,0:T(8,128)(2,1)}), bf16[4,2304,256]{2,1,0:T(8,128)(2,1)}, u32[]{:S(2)}, u32[]{:S(2)}) async-start(bf16[4,2304,256]{2,1,0:T(8,128)(2,1)} %broadcast_in_dim.94), calls=%async_computation.8 | async-start | bytes 9437184 | tf_op jit(solution)/shard_map/all_to_all | solution.py:391

commit v2 on v1

--- a/solution.py
+++ b/solution.py
@@ -8,6 +8,7 @@
 from jax.experimental.pallas import tpu as pltpu
 from jax.sharding import PartitionSpec as P
 
+
 COEF_A = 3.4445
 COEF_B = -4.775
 COEF_C = 2.0315
@@ -17,6 +18,8 @@
 F16_TOP = 32768.0
 SMALLEST = 1e-30
 BLOCK = 256
+PIECE = 128
+SWEEP = 512
 
 F32 = jnp.float32
 BF16 = jnp.bfloat16
@@ -90,24 +93,26 @@
 
 
 def merge_kernel(momentum_ref, grad_ref, scaled_ref, top_ref):
-    merged = BETA * momentum_ref[...] + grad_ref[...]
-    top = jnp.maximum(jnp.max(jnp.abs(merged), axis=(1, 2), keepdims=True), SMALLEST)
-    scaled_ref[...] = merged * (F16_TOP / top)
-    top_ref[...] = jnp.broadcast_to(top, top_ref.shape)
+    for i in range(momentum_ref.shape[0]):
+        merged = BETA * momentum_ref[i] + grad_ref[i]
+        top = jnp.maximum(jnp.max(jnp.abs(merged), keepdims=True), SMALLEST)
+        scaled_ref[i] = merged * (F16_TOP / top)
+        top_ref[i] = jnp.broadcast_to(top, top_ref.shape[1:])
 
 
 def merge(momentum, grad):
     per_group, rows, width = momentum.shape
-    spec = pl.BlockSpec((1, rows, width), lambda i: (i, 0, 0))
+    step = 4
+    spec = pl.BlockSpec((step, rows, width), lambda i: (i, 0, 0))
     return pl.pallas_call(
         merge_kernel,
-        grid=(per_group,),
+        grid=(per_group // step,),
         out_shape=(
             jax.ShapeDtypeStruct(momentum.shape, F32),
             jax.ShapeDtypeStruct((per_group, 8, 128), F32),
         ),
         in_specs=[spec, spec],
-        out_specs=(spec, pl.BlockSpec((1, 8, 128), lambda i: (i, 0, 0))),
+        out_specs=(spec, pl.BlockSpec((step, 8, 128), lambda i: (i, 0, 0))),
         name="merge",
         cost_estimate=cost(5 * momentum.size, momentum.size * 12),
     )(momentum, grad)
@@ -117,7 +122,7 @@
     members, half_members, first_slot,
     row_ref, scale_ref, keep_ref, factor_ref, data_ref, *rest,
 ):
-    work_ref, back_ref, whole, low = rest[-4:]
+    work_ref, back_ref, whole, low, held, mixed = rest[-6:]
     rows = data_ref.shape[2]
     size, width = whole.shape
     slot = first_slot + pl.program_id(0)
@@ -128,10 +133,15 @@
         whole[pl.ds(member * rows, rows), :] = part
         low[pl.ds(member * rows, rows), :] = part.astype(BF16)
 
-    gram = jnp.zeros((size, size), F32)
-    for k in range(width // tile):
-        block = low[:, k * tile:(k + 1) * tile]
-        gram = gram + dot_nt(block, block)
+    held[...] = jnp.zeros_like(held)
+
+    def add_gram(k, carry):
+        block = low[:, pl.ds(pl.multiple_of(k * tile, tile), tile)]
+        held[...] += dot_nt(block, block)
+        return carry
+
+    lax.fori_loop(0, width // tile, add_gram, 0)
+    gram = held[...]
     row_ids = lax.broadcasted_iota(jnp.int32, (size, size), 0)
     col_ids = lax.broadcasted_iota(jnp.int32, (size, size), 1)
     norm_sq = jnp.sum(jnp.where(row_ids == col_ids, gram, 0.0), keepdims=True) + EPS
@@ -149,21 +159,26 @@
     mix = (COEF_A * (u + v) + dot(v.astype(BF16), u_low)).astype(BF16)
     factor = factor_ref[slot]
     keep = keep_ref[slot]
-    for k in range(width // tile):
-        cols = slice(k * tile, (k + 1) * tile)
-        moved = dot(mix, low[:, cols])
+    mixed[...] = mix
+
+    def apply(k, carry):
+        cols = pl.ds(pl.multiple_of(k * tile, tile), tile)
+        moved = dot(mixed[...], low[:, cols])
         result = ((COEF_A * COEF_A) * whole[:, cols] + moved) * inverse
         work_ref[0, :, cols] = result * factor
         whole[:, cols] = result * keep
-    first_row = pl.multiple_of(row_ref[0], half_members * rows)
-    for member in range(half_members):
-        back_ref[member, 0] = whole[pl.ds(first_row + member * rows, rows), :]
-
-
-def solve(first_row, scale, keep, factor, data, work, first_slot, most, half_members):
+        return carry
+
+    lax.fori_loop(0, width // tile, apply, 0)
+    for turn in range(half_members):
+        start = pl.multiple_of(row_ref[turn], rows)
+        back_ref[turn, 0] = whole[pl.ds(start, rows), :]
+
+
+def solve(row_starts, scale, keep, factor, data, work, first_slot, most, half_members):
     members, chunk, rows, width = data.shape
     size = members * rows
-    inputs = [first_row, scale, keep, factor, data]
+    inputs = [row_starts, scale, keep, factor, data]
     specs = [SMEM_SPEC] * 4 + [pl.BlockSpec((members, 1, rows, width), lambda i: (0, i, 0, 0))]
     aliases = {}
     if work is not None:
@@ -183,9 +198,13 @@
             pl.BlockSpec((1, size, width), lambda i: (first_slot + i, 0, 0)),
             pl.BlockSpec((half_members, 1, rows, width), lambda i: (0, i, 0, 0)),
         ),
-        scratch_shapes=[pltpu.VMEM((size, width), F32), pltpu.VMEM((size, width), BF16)],
+        scratch_shapes=[
+            pltpu.VMEM((size, width), F32),
+            pltpu.VMEM((size, width), BF16),
+            pltpu.VMEM((size, size), F32),
+            pltpu.VMEM((size, size), BF16),
+        ],
         input_output_aliases=aliases,
-        name=f"solve{first_slot}",
         cost_estimate=cost(flops, data.size * 12),
     )(*inputs)
 
@@ -234,15 +253,15 @@
 
     squares = jnp.square(rounded.astype(F32))
     sum_ref[...] += jnp.sum(squares, axis=(0, 1), keepdims=True)
-    start = i * (i + 1) // 2
-
-    def column(j, carry):
-        other = low[pl.ds(pl.multiple_of(j * BLOCK, BLOCK), BLOCK), :]
-        place = pl.multiple_of((start + j) * BLOCK, BLOCK)
-        packed_ref[pl.ds(place, BLOCK), :] = dot_nt(rounded, other).astype(BF16)
-        return carry
-
-    lax.fori_loop(0, i + 1, column, 0)
+    for k in range(low.shape[0] // BLOCK):
+
+        @pl.when(i == k)
+        def _(k=k):
+            product = dot_nt(rounded, low[:(k + 1) * BLOCK, :]).astype(BF16)
+            start = k * (k + 1) // 2
+            for j in range(k + 1):
+                rows = slice((start + j) * BLOCK, (start + j + 1) * BLOCK)
+                packed_ref[rows, :] = product[:, j * BLOCK:(j + 1) * BLOCK]
 
 
 def wide_gram(momentum, grad):
@@ -270,9 +289,12 @@
     )(momentum, grad)
 
 
-def wide_solve_kernel(coef_ref, packed_ref, merged_ref, out_ref, gram, first, second, one, two):
-    height, width = out_ref.shape
+def wide_solve_kernel(
+    coef_ref, turn_ref, table_ref, packed_ref, merged_ref, out_ref, gram, first, second, low
+):
+    height, _ = out_ref.shape
     number = height // BLOCK
+    pieces = packed_ref.shape[1] // PIECE
     inverse, inverse_sq, outer = coef_ref[0], coef_ref[1], coef_ref[2]
 
     def assemble(i, carry):
@@ -280,8 +302,12 @@
 
         def column(j, inner):
             cols = pl.ds(pl.multiple_of(j * BLOCK, BLOCK), BLOCK)
-            place = pl.multiple_of((i * (i + 1) // 2 + j) * BLOCK, BLOCK)
-            block = packed_ref[pl.ds(place, BLOCK), :]
+            found = []
+            for p in range(BLOCK // PIECE):
+                piece = (i * (i + 1) // 2 + j) * (BLOCK // PIECE) + p
+                place = pl.multiple_of((piece % pieces) * PIECE, PIECE)
+                found.append(packed_ref[turn_ref[piece // pieces], pl.ds(place, PIECE), :])
+            block = jnp.concatenate(found, axis=0)
             gram[cols, rows] = block.T
             gram[rows, cols] = block
             return inner
@@ -289,139 +315,128 @@
         return lax.fori_loop(0, i + 1, column, carry)
 
     lax.fori_loop(0, number, assemble, 0)
-
-    def sweep(source, step):
-        def body(i, carry):
-            rows = pl.ds(pl.multiple_of(i * BLOCK, BLOCK), BLOCK)
-            step(rows, dot(gram[rows, :], source[...]) * inverse_sq)
-            return carry
-
-        lax.fori_loop(0, number, body, 0)
 
     def prepare(i, carry):
         rows = pl.ds(pl.multiple_of(i * BLOCK, BLOCK), BLOCK)
         value = merged_ref[rows, :] * inverse
         first[rows, :] = value
-        one[rows, :] = value.astype(BF16)
+        second[rows, :] = jnp.zeros_like(value)
+        low[0, rows, :] = value.astype(BF16)
         return carry
 
     lax.fori_loop(0, number, prepare, 0)
 
-    def inner_of(base, target):
-        def step(rows, product):
-            target[rows, :] = (COEF_B * base[rows, :] + COEF_C * product).astype(BF16)
-        return step
-
-    def outer_of(base, wide, target):
-        def step(rows, product):
-            value = COEF_A * base[rows, :] + product
-            if wide is not None:
-                wide[rows, :] = value
-            target[rows, :] = value.astype(BF16)
-        return step
-
-    def plain(wide, target):
-        def step(rows, product):
-            wide[rows, :] = product
-            target[rows, :] = product.astype(BF16)
-        return step
-
-    sweep(one, inner_of(first, two))
-    sweep(two, outer_of(first, first, one))
-    sweep(one, inner_of(first, two))
-    sweep(two, outer_of(first, None, one))
-    sweep(one, plain(second, two))
-    sweep(two, inner_of(second, one))
-
-    def turn(rows, product):
-        turned = COEF_A * second[rows, :] + product
-        value = COEF_B * first[rows, :] + COEF_C * turned
-        second[rows, :] = value
-        two[rows, :] = value.astype(BF16)
-
-    sweep(one, turn)
-    sweep(two, inner_of(second, one))
-    sweep(one, outer_of(second, None, two))
-    sweep(two, plain(second, one))
-    sweep(one, inner_of(second, two))
-
-    def finish(rows, product):
-        value = COEF_A * first[rows, :] + COEF_A * second[rows, :] + product
-        out_ref[rows, :] = value * outer
-
-    sweep(two, finish)
-
-
-def wide_solve(coef, packed, merged):
+    def sweep(step, carry):
+        from_first, from_second, from_product = table_ref[step], table_ref[12 + step], table_ref[24 + step]
+        now = step % 2
+
+        def body(i, inner):
+            rows = pl.ds(pl.multiple_of(i * SWEEP, SWEEP), SWEEP)
+            product = dot(gram[rows, :], low[now]) * (inverse_sq * from_product)
+            value = product + from_first * first[rows, :] + from_second * second[rows, :]
+
+            @pl.when(step == 1)
+            def _():
+                first[rows, :] = value
+
+            @pl.when(jnp.logical_or(step == 4, jnp.logical_or(step == 6, step == 9)))
+            def _():
+                second[rows, :] = value
+
+            @pl.when(step == 11)
+            def _():
+                out_ref[rows, :] = value * outer
+
+            low[1 - now, rows, :] = value.astype(BF16)
+            return inner
+
+        return lax.fori_loop(0, height // SWEEP, body, carry)
+
+    lax.fori_loop(0, 12, sweep, 0)
+
+
+A, B, C = COEF_A, COEF_B, COEF_C
+SWEEP_FIRST = (B, A, B, A, 0, 0, B, 0, 0, 0, 0, A)
+SWEEP_SECOND = (0, 0, 0, 0, 0, B, C * A, B, A, 0, B, A)
+SWEEP_PRODUCT = (C, 1, C, 1, 1, C, C, C, 1, 1, C, 1)
+
+
+def wide_solve(coef, turns, packed, merged):
     height, width = merged.shape
+    table = jnp.asarray(SWEEP_FIRST + SWEEP_SECOND + SWEEP_PRODUCT, F32)
     return pl.pallas_call(
         wide_solve_kernel,
         out_shape=jax.ShapeDtypeStruct((height, width), F32),
-        in_specs=[SMEM_SPEC] + [pl.BlockSpec(memory_space=pltpu.VMEM)] * 2,
+        in_specs=[SMEM_SPEC] * 3 + [pl.BlockSpec(memory_space=pltpu.VMEM)] * 2,
         out_specs=pl.BlockSpec(memory_space=pltpu.VMEM),
         scratch_shapes=[
             pltpu.VMEM((height, height), BF16),
             pltpu.VMEM((height, width), F32),
             pltpu.VMEM((height, width), F32),
-            pltpu.VMEM((height, width), BF16),
-            pltpu.VMEM((height, width), BF16),
+            pltpu.VMEM((2, height, width), BF16),
         ],
         name="wide_solve",
         cost_estimate=cost(24 * height * height * width, height * width * 8),
-    )(coef, packed, merged)
+    )(coef, turns, table, packed, merged)
 
 
 def on_device(expert_momentum, expert_grad, wide_momentum, wide_grad, assignment, expert_tokens):
     members = lax.axis_size("fsdp")
     half_members = members // 2
     per_group, rows, width = expert_momentum.shape
-    wide_height, wide_width = wide_momentum.shape[1:]
+    _, wide_width = wide_momentum.shape[1:]
     most = 2 * -(-per_group // members)
-    chunk = 2
+    sizes = [1] + [2] * ((most - 2) // 2) + [1]
+    starts = [sum(sizes[:i]) for i in range(len(sizes))]
     group_index = lax.axis_index("grp")
     me = lax.axis_index("fsdp")
     half = me // half_members
-    halves = [list(range(half_members)), list(range(half_members, members))]
+    place = me % half_members
     mirror = [(i, (i + half_members) % members) for i in range(members)]
+    steps = jnp.arange(half_members, dtype=jnp.int32)
+    onward = (place + steps) % half_members
+    origin = (place + half_members - steps) % half_members
 
     def across(value):
         return lax.all_to_all(value, "fsdp", split_axis=0, concat_axis=0, tiled=True)
 
-    def within(value):
-        return lax.all_to_all(
-            value, "fsdp", split_axis=0, concat_axis=0, tiled=True, axis_index_groups=halves
-        )
+    def shifted(value, turn):
+        pairs = [
+            (i, i // half_members * half_members + (i + turn) % half_members)
+            for i in range(members)
+        ]
+        return lax.ppermute(value, "fsdp", pairs)
 
     base = (group_index * per_group).astype(jnp.int32).reshape(1)
     table, count = route(base, assignment, members, most, per_group)
-
+    slots = table.reshape(members, most)
+
+    scaled, top = merge(expert_momentum, expert_grad)
     wide_merged, packed, squares = wide_gram(wide_momentum[0], wide_grad[0])
-    packed_rows = packed.shape[0] // half_members
-    parts = within(packed.reshape(half_members, packed_rows, BLOCK))
-
-    scaled, top = merge(expert_momentum, expert_grad)
-    slots = table.reshape(members, most)
-    outgoing = []
-    for start in range(0, most, chunk):
-        picked = scaled[slots[:, start:start + chunk].reshape(-1)].astype(jnp.float16)
-        outgoing.append(picked.reshape(members, chunk, rows, width))
-
     notes = jnp.concatenate([top[:, 0, 0], squares[0, :1]])
     notes = jnp.pad(notes, (0, -notes.shape[0] % 128))
     notes = jnp.broadcast_to(notes[None, None, :], (members, 1, notes.shape[0]))
     notes = across(notes)[:, 0]
-    arrived = [across(piece) for piece in outgoing]
-
-    part = jnp.sum(parts.astype(F32), axis=0).astype(BF16)
+    arrived = []
+    for start, chunk in zip(starts, sizes):
+        picked = scaled[slots[:, start:start + chunk].reshape(-1)].astype(jnp.float16)
+        arrived.append(across(picked.reshape(members, chunk, rows, width)))
+
+    packed_rows = packed.shape[0] // half_members
+    packed = packed.reshape(half_members, packed_rows, BLOCK)
+    total = lax.dynamic_index_in_dim(packed, place, 0, keepdims=False).astype(F32)
+    for turn in range(1, half_members):
+        part = lax.dynamic_index_in_dim(packed, onward[turn], 0, keepdims=False)
+        total = total + shifted(part, turn).astype(F32)
+    part = total.astype(BF16)
     other = lax.ppermute(part, "fsdp", mirror)
     part = (part.astype(F32) + other.astype(F32)).astype(BF16)
-    packed = within(jnp.broadcast_to(part[None], (half_members,) + part.shape))
-    packed = packed.reshape(half_members * packed_rows, BLOCK)
+    packed = jnp.stack([part] + [shifted(part, turn) for turn in range(1, half_members)])
     wide_norm = jnp.sum(notes[:, per_group]) + EPS
     coef = jnp.stack(
         [lax.rsqrt(wide_norm), 1.0 / wide_norm, jnp.float32(math.sqrt(wide_width * members))]
     )
-    wide_out = wide_solve(coef, packed, wide_merged)
+    wide_out = wide_solve(coef, origin, packed, wide_merged)
 
     tops = notes[:, :per_group]
     keep = F16_TOP / jnp.minimum(2.0, jnp.max(tops, axis=0) * 2e7)
@@ -429,7 +444,7 @@
     own_tokens = lax.dynamic_slice_in_dim(tokens, group_index * per_group, per_group)
     factor = jnp.sqrt(own_tokens / jnp.mean(tokens)) * math.sqrt(width)
     own_slots = lax.dynamic_index_in_dim(slots, me, 0, keepdims=False)
-    half_slots = lax.dynamic_slice_in_dim(slots, half * half_members, half_members)
+    half_slots = slots[half * half_members + origin]
     own_count = lax.dynamic_index_in_dim(count, me, 0, keepdims=False)
     own_pick = own_slots[:, None] == jnp.arange(per_group, dtype=jnp.int32)[None, :]
     half_pick = half_slots[:, :, None] == jnp.arange(per_group, dtype=jnp.int32)
@@ -439,17 +454,20 @@
     slot_factor = jnp.where(jnp.arange(most) < own_count, slot_factor, 0.0)
     home_factor = jnp.sum(jnp.where(half_pick, (factor / keep)[None, None], 0.0), axis=2)
     slot_scale = slot_scale.reshape(-1)
-    first_row = (half * half_members * rows).astype(jnp.int32).reshape(1)
+    row_starts = ((half * half_members + onward) * rows).astype(jnp.int32)
 
     work = None
     expert_out = None
     for index, piece in enumerate(arrived):
-        start = index * chunk
+        start, chunk = starts[index], sizes[index]
         work, back = solve(
-            first_row, slot_scale, slot_keep, slot_factor, piece.astype(F32), work,
+            row_starts, slot_scale, slot_keep, slot_factor, piece.astype(F32), work,
             start, most, half_members,
         )
-        back = within(back.astype(jnp.float16)).astype(F32)
+        pieces = [back[0]]
+        for turn in range(1, half_members):
+            pieces.append(shifted(back[turn].astype(jnp.float16), turn).astype(F32))
+        back = jnp.stack(pieces)
         expert_out = home(
             half_slots[:, start:start + chunk].reshape(-1),
             home_factor[:, start:start + chunk].reshape(-1),

time: 696 us -> 686 us (0.986)
  blocking collectives: 97.3 us -> 0 us
  waiting for transfers between devices: 260 us -> 308 us
  starting transfers between devices: 42.3 us -> 58.5 us
  local copies, waits for them, and re-layouts: 40.3 us -> 54.7 us
    ppermute x0 -> x18, waiting for transfers between devices: none -> 193 us  [shifted(): return lax.ppermute(value, 'fsdp', pairs)]
    all_to_all x1 -> x0, blocking collectives: 97.3 us -> none  [across(): lax.all_to_all(value, 'fsdp', split_axis=0, concat_axis=0, tiled=True)]
    all_to_all x3 -> x5, waiting for transfers between devices: 155 us -> 69.4 us  [across(): lax.all_to_all(value, 'fsdp', split_axis=0, concat_axis=0, tiled=True)]
    all_to_all x5 -> x0, waiting for transfers between devices: 53.5 us -> none  [within(): lax.all_to_all(value, 'fsdp', split_axis=0, concat_axis=0, tiled=True, ax...]
    ppermute x0 -> x18, starting transfers between devices: none -> 29.8 us  [shifted(): return lax.ppermute(value, 'fsdp', pairs)]
    all_to_all x5 -> x0, starting transfers between devices: 23.3 us -> none  [within(): lax.all_to_all(value, 'fsdp', split_axis=0, concat_axis=0, tiled=True, ax...]
    convert_element_type x6 -> x1, other arithmetic: 21.8 us -> 2.91 us  [on_device(): part = total.astype(BF16)]
    another operation x0 -> x21, other arithmetic: none -> 16.5 us  [the longest x16 8.19 us: on_device(): back = jnp.stack(pieces)]
  transfers between devices with their start and end apart: 9 -> 24, of which waited for: 6 -> 16; matrix products, arithmetic and copies ran while one was open for 14% -> 15% of each run, Pallas kernels for 10% -> 17%
where the time goes in v2:
time: 686 us; the launch traced here: 684 us
  waiting for transfers between devices  308 us (45%)
  Pallas kernels  189 us (28%)
  other arithmetic  65.1 us (9%)
  starting transfers between devices  58.5 us (9%)
  local copies, waits for them, and re-layouts  54.7 us (8%)
  between operations  8.11 us (1%)
    ppermute x18, waiting for transfers between devices, shifted(): return lax.ppermute(value, 'fsdp', pairs)  193 us
    pallas_call x1, Pallas kernels, wide_solve(): pl.pallas_call(wide_solve_kernel, out_shape=jax.ShapeDtypeStruct((height,...  77.3 us
    all_to_all x5, waiting for transfers between devices, across(): lax.all_to_all(value, 'fsdp', split_axis=0, concat_axis=0, tiled=True)  69.4 us
    pallas_call x4, Pallas kernels, solve(): pl.pallas_call(functools.partial(solve_kernel, members, half_members, fir...  59.5 us
    ppermute x1, waiting for transfers between devices, on_device(): other = lax.ppermute(part, 'fsdp', mirror)  46.1 us
    gather x4, local copies, waits for them, and re-layouts, on_device(): scaled[slots[:, start:start + chunk].reshape(-1)].astype(jnp.float16)  32.9 us
    ppermute x18, starting transfers between devices, shifted(): return lax.ppermute(value, 'fsdp', pairs)  29.8 us
    all_to_all x5, starting transfers between devices, across(): lax.all_to_all(value, 'fsdp', split_axis=0, concat_axis=0, tiled=True)  26.1 us
  transfers between devices with their start and end apart: 24, of which 16 were waited for; matrix products, arithmetic and copies ran while one was open for 15% of the time, Pallas kernels for 17%

profile of v2, /device:TPU:0, one launch (start us, length us, event | category | flops | bytes accessed | tf_op | source)
XLA Modules:
  0.0 683.7 jit_solution(7146356536925890342)
XLA Ops:
  0.6 12.2 %wide_gram.1 = (f32[2048,512]{1,0:T(8,128)}, bf16[9216,256]{1,0:T(8,128)(2,1)}, f32[8,128]{1,0:T(8,128)}) custom-call(f32[2048,512]{1,0:T(8,128)} %bitcast.113, f32[2048,512]{1,0:T(8,128)} %bitcast.114), custom_call_target="tpu_custom_call" | custom-call | flops 2415919104 | bytes 17301504 | tf_op jit(solution)/shard_map/wide_gram/pallas_call | solution.py:272
  14.0 13.9 %merge.1 = (f32[24,64,2048]{2,1,0:T(8,128)}, f32[24,8,128]{2,1,0:T(8,128)}) custom-call(f32[24,64,2048]{2,1,0:T(8,128)} %momentum_ref.1, f32[24,64,2048]{2,1,0:T(8,128)} %grad_ref.1), custom_call_target="tpu_custom_call" | custom-call | flops 15728640 | bytes 37748736 | tf_op jit(solution)/shard_map/merge/pallas_call | solution.py:107
  30.4 7.3 %all-to-all-start = ((f32[8,1,128]{2,1,0:T(1,128)}), f32[8,1,128]{2,1,0:T(1,128)S(1)}, u32[]{:S(2)}, u32[]{:S(2)}) async-start(f32[8,1,128]{2,1,0:T(1,128)} %broadcast_in_dim.80), calls=%async_computation | async-start | bytes 8192 | tf_op jit(solution)/shard_map/all_to_all | solution.py:401
  37.7 2.5 route.1
  41.1 7.4 %gather_fusion.4 = f32[8,64,2048]{2,1,0:T(8,128)} fusion(f32[24,64,2048]{2,1,0:T(8,128)} %get-tuple-element.22, s32[1024]{0:T(1024)S(1)} %get-tuple-element.72), kind=kCustom, calls=%fused_computation.4 | custom fusion | bytes 8388640 | tf_op jit(solution)/shard_map/gather | solution.py:422
  48.5 3.8 convert_bitcast_fusion
  52.3 6.0 all-to-all-start.4
  58.3 7.4 %gather_fusion.1 = f32[8,64,2048]{2,1,0:T(8,128)} fusion(f32[24,64,2048]{2,1,0:T(8,128)} %get-tuple-element.22, s32[1024]{0:T(1024)S(1)} %get-tuple-element.73), kind=kCustom, calls=%fused_computation.1 | custom fusion | bytes 8388640 | tf_op jit(solution)/shard_map/gather | solution.py:422
  65.7 3.9 convert_bitcast_fusion.1
  69.6 36.4 %all-to-all-done.4 = f16[8,1,64,2048]{3,2,1,0:T(8,128)(2,1)S(1)} async-done(((f16[8,1,64,2048]{3,2,1,0:T(8,128)(2,1)}), f16[8,1,64,2048]{3,2,1,0:T(8,128)(2,1)S(1)}, u32[]{:S(2)}, u32[]{:S(2)}) %all-to-all-start.4) | async-done | bytes 2097184 | tf_op jit(solution)/shard_map/all_to_all | solution.py:401
  107.4 3.6 all-to-all-start.1
  111.3 9.1 %gather_fusion.3 = f32[16,64,2048]{2,1,0:T(8,128)} fusion(f32[24,64,2048]{2,1,0:T(8,128)} %get-tuple-element.22, s32[1024]{0:T(1024)S(1)} %pad_clamp_fusion.1), kind=kCustom, calls=%fused_computation.3 | custom fusion | bytes 16777280 | tf_op jit(solution)/shard_map/gather | solution.py:422
  120.3 6.1 convert_element_type.199
  126.4 33.0 %all-to-all-done.1 = f16[8,1,64,2048]{3,2,1,0:T(8,128)(2,1)S(1)} async-done(((f16[8,1,64,2048]{3,2,1,0:T(8,128)(2,1)}), f16[8,1,64,2048]{3,2,1,0:T(8,128)(2,1)S(1)}, u32[]{:S(2)}, u32[]{:S(2)}) %all-to-all-start.1) | async-done | bytes 2097184 | tf_op jit(solution)/shard_map/all_to_all | solution.py:401
  159.4 4.6 all-to-all-start.3
  170.4 3.9 dynamic-slice_bitcast_fusion.2
  174.3 1.9 collective-permute-start.12
  177.2 1.9 collective-permute-start.13
  181.1 9.1 %gather_fusion.2 = f32[16,64,2048]{2,1,0:T(8,128)} fusion(f32[24,64,2048]{2,1,0:T(8,128)} %get-tuple-element.22, s32[1024]{0:T(1024)S(1)} %pad_clamp_fusion.2), kind=kCustom, calls=%fused_computation.2 | custom fusion | bytes 16777280 | tf_op jit(solution)/shard_map/gather | solution.py:422
  190.2 6.0 convert_element_type.196
  198.6 60.1 %collective-permute-done.12 = bf16[2304,256]{1,0:T(8,128)(2,1)S(1)} collective-permute-done((bf16[2304,256]{1,0:T(8,128)(2,1)}, bf16[2304,256]{1,0:T(8,128)(2,1)S(1)}, u32[]{:S(2)}, u32[]{:S(2)}) %collective-permute-start.12) | collective-permute-done | bytes 1179680 | tf_op jit(solution)/shard_map/ppermute | solution.py:408
  258.7 2.6 collective-permute-done.14
  261.3 22.6 %collective-permute-done.13 = bf16[2304,256]{1,0:T(8,128)(2,1)} collective-permute-done((bf16[2304,256]{1,0:T(8,128)(2,1)}, bf16[2304,256]{1,0:T(8,128)(2,1)}, u32[]{:S(2)}, u32[]{:S(2)}) %collective-permute-start.13) | collective-permute-done | bytes 1179680 | tf_op jit(solution)/shard_map/ppermute | solution.py:408
  283.8 2.9 fusion.2
  286.7 2.6 collective-permute-start.15
  292.9 46.1 %collective-permute-done.15 = bf16[2304,256]{1,0:T(8,128)(2,1)} collective-permute-done((bf16[2304,256]{1,0:T(8,128)(2,1)S(1)}, bf16[2304,256]{1,0:T(8,128)(2,1)}, u32[]{:S(2)}, u32[]{:S(2)}) %collective-permute-start.15) | collective-permute-done | bytes 1179680 | tf_op jit(solution)/shard_map/ppermute | solution.py:432
  339.1 1.9 add_convert_fusion
  341.0 7.9 %collective-permute-start.18 = (bf16[2304,256]{1,0:T(8,128)(2,1)S(1)}, bf16[2304,256]{1,0:T(8,128)(2,1)}, u32[]{:S(2)}, u32[]{:S(2)}) collective-permute-start(bf16[2304,256]{1,0:T(8,128)(2,1)S(1)} %add_convert_fusion), channel_id=1, source_target_pairs={{0,3},{1,0},{2,1},{3,2},{4,7},{5,4},{6,5},{7,6},{8,11},{9,8},{10,9... | collective-permute-start | bytes 3538952 | tf_op jit(solution)/shard_map/ppermute | solution.py:408
  348.9 3.3 collective-permute-start.17
  357.0 19.7 %collective-permute-done.18 = bf16[2304,256]{1,0:T(8,128)(2,1)} collective-permute-done((bf16[2304,256]{1,0:T(8,128)(2,1)S(1)}, bf16[2304,256]{1,0:T(8,128)(2,1)}, u32[]{:S(2)}, u32[]{:S(2)}) %collective-permute-start.18) | collective-permute-done | bytes 1179680 | tf_op jit(solution)/shard_map/ppermute | solution.py:408
  376.7 25.6 %collective-permute-done.17 = bf16[2304,256]{1,0:T(8,128)(2,1)} collective-permute-done((bf16[2304,256]{1,0:T(8,128)(2,1)S(1)}, bf16[2304,256]{1,0:T(8,128)(2,1)}, u32[]{:S(2)}, u32[]{:S(2)}) %collective-permute-start.17) | collective-permute-done | bytes 1179680 | tf_op jit(solution)/shard_map/ppermute | solution.py:408
  402.4 4.0 pad_maximum_fusion.packed_ref
  406.4 2.3 convert_element_type.204.data_ref
  408.7 11.5 %shard_map.94 = (f32[6,512,2048]{2,1,0:T(8,128)}, f32[4,1,64,2048]{3,2,1,0:T(8,128)}) custom-call(s32[4]{0:T(128)} %add_multiply_fusion.row_ref, f32[48]{0:T(128)} %div.47.scale_ref, f32[6]{0:T(128)} %get-tuple-element.38.keep_ref, f32[6]{0:T(128)} %compare_select_fusion.11.factor_ref, f32[8,1,64,2048]{3,2,1,0:T(8,128)} %convert_element_type.204.data_ref), custom_call_target="tpu_custom_call" | custom-call | flops 3489660928 | bytes 12582912 | tf_op jit(solution)/shard_map/pallas_call | solution.py:189
  420.2 1.7 convert.36
  421.9 4.6 all-to-all-start.2
  427.5 1.9 collective-permute-start.9
  429.4 77.3 %wide_solve.1 = f32[2048,512]{1,0:T(8,128)} custom-call(f32[3]{0:T(128)} %pad_maximum_fusion.5.coef_ref, s32[4]{0:T(128)} %and_select_fusion.turn_ref, f32[36]{0:T(128)} %constant.109.clone.table_ref, bf16[4,2304,256]{2,1,0:T(8,128)(2,1)} %pad_maximum_fusion.packed_ref, f32[2048,512]{1,0:T(8,128)} %get-tuple-element.31.merged_ref), custom_call_target="tpu_custom_call" | custom-call | flops 51539607552 | bytes 8388608 | tf_op jit(solution)/shard_map/wide_solve/pallas_call | solution.py:367
  508.9 1.9 collective-permute-start.10
  510.8 2.3 convert_element_type.195.data_ref
  513.1 2.4 collective-permute-done.11
  515.6 14.5 %collective-permute-done.10 = f16[1,64,2048]{2,1,0:T(8,128)(2,1)S(1)} collective-permute-done((f16[1,64,2048]{2,1,0:T(8,128)(2,1)S(1)}, f16[1,64,2048]{2,1,0:T(8,128)(2,1)S(1)}, u32[]{:S(2)}, u32[]{:S(2)}) %collective-permute-start.10) | collective-permute-done | bytes 262176 | tf_op jit(solution)/shard_map/ppermute | solution.py:408
  531.6 4.5 home.4.rest_0_
  536.1 6.5 convert_element_type.201.data_ref
  542.6 18.2 %shard_map.95 = (f32[6,512,2048]{2,1,0:T(8,128)}, f32[4,2,64,2048]{3,2,1,0:T(8,128)}) custom-call(s32[4]{0:T(128)} %add_multiply_fusion.row_ref, f32[48]{0:T(128)} %div.47.scale_ref, f32[6]{0:T(128)} %get-tuple-element.38.keep_ref, f32[6]{0:T(128)} %compare_select_fusion.11.factor_ref, ...), custom_call_target="tpu_custom_call", output_to_operand_aliasing={{0}: (5, {})} | custom-call | flops 6979321856 | bytes 25165824 | tf_op jit(solution)/shard_map/pallas_call | solution.py:189
  560.8 6.5 convert_element_type.198.data_ref
  567.2 18.2 %shard_map.96 = (f32[6,512,2048]{2,1,0:T(8,128)}, f32[4,2,64,2048]{3,2,1,0:T(8,128)}) custom-call(s32[4]{0:T(128)} %add_multiply_fusion.row_ref, f32[48]{0:T(128)} %div.47.scale_ref, f32[6]{0:T(128)} %get-tuple-element.38.keep_ref, f32[6]{0:T(128)} %compare_select_fusion.11.factor_ref, ...), custom_call_target="tpu_custom_call", output_to_operand_aliasing={{0}: (5, {})} | custom-call | flops 6979321856 | bytes 25165824 | tf_op jit(solution)/shard_map/pallas_call | solution.py:189
  585.5 11.6 %shard_map.97 = (f32[6,512,2048]{2,1,0:T(8,128)}, f32[4,1,64,2048]{3,2,1,0:T(8,128)}) custom-call(s32[4]{0:T(128)} %add_multiply_fusion.row_ref, f32[48]{0:T(128)} %div.47.scale_ref, f32[6]{0:T(128)} %get-tuple-element.38.keep_ref, f32[6]{0:T(128)} %compare_select_fusion.11.factor_ref, ...), custom_call_target="tpu_custom_call", output_to_operand_aliasing={{0}: (5, {})} | custom-call | flops 3489660928 | bytes 12582912 | tf_op jit(solution)/shard_map/pallas_call | solution.py:189
  598.3 1.9 convert.33
  600.7 1.8 copy-done.2
  603.1 2.9 collective-permute-start.2
  606.9 2.4 collective-permute-start.5
  609.6 5.8 collective-permute-done
  615.4 3.5 collective-permute-done.2
  619.0 3.0 collective-permute-start.8
  622.0 1.5 pad_maximum_fusion.3.data_ref
  623.5 14.3 %collective-permute-done.3 = f16[2,64,2048]{2,1,0:T(8,128)(2,1)S(1)} collective-permute-done((f16[2,64,2048]{2,1,0:T(8,128)(2,1)S(1)}, f16[2,64,2048]{2,1,0:T(8,128)(2,1)S(1)}, u32[]{:S(2)}, u32[]{:S(2)}) %collective-permute-start.3) | collective-permute-done | bytes 524320 | tf_op jit(solution)/shard_map/ppermute | solution.py:408
  637.9 3.5 collective-permute-done.5
  641.5 18.2 %collective-permute-done.6 = f16[2,64,2048]{2,1,0:T(8,128)(2,1)S(1)} collective-permute-done((f16[2,64,2048]{2,1,0:T(8,128)(2,1)S(1)}, f16[2,64,2048]{2,1,0:T(8,128)(2,1)S(1)}, u32[]{:S(2)}, u32[]{:S(2)}) %collective-permute-start.6) | collective-permute-done | bytes 524320 | tf_op jit(solution)/shard_map/ppermute | solution.py:408
  659.8 2.2 pad_maximum_fusion.1.data_ref
  662.3 2.3 pad_maximum_fusion.2.data_ref
  664.6 7.3 %home.5.rest_0_ = f32[24,64,2048]{2,1,0:T(8,128)} custom-call(s32[8]{0:T(128)} %reshape.310.ids_ref, f32[8]{0:T(128)} %reshape.311.factor_ref, f32[4,2,64,2048]{3,2,1,0:T(8,128)} %pad_maximum_fusion.2.data_ref, f32[24,64,2048]{2,1,0:T(8,128)} %home.4.rest_0_), custom_call_target="tpu_custom_call", output_to_operand_aliasing={{}: (3, {})} | custom-call | flops 100000000 | bytes 8388608 | tf_op jit(solution)/shard_map/home/pallas_call | solution.py:228
  671.9 7.3 %home.6.rest_0_ = f32[24,64,2048]{2,1,0:T(8,128)} custom-call(s32[8]{0:T(128)} %reshape.308.ids_ref, f32[8]{0:T(128)} %reshape.309.factor_ref, f32[4,2,64,2048]{3,2,1,0:T(8,128)} %pad_maximum_fusion.1.data_ref, f32[24,64,2048]{2,1,0:T(8,128)} %home.5.rest_0_), custom_call_target="tpu_custom_call", output_to_operand_aliasing={{}: (3, {})} | custom-call | flops 100000000 | bytes 8388608 | tf_op jit(solution)/shard_map/home/pallas_call | solution.py:228
  679.2 4.5 home.7
  (104 shorter events, 28.2 us)
Async XLA Ops:
  30.4 22.0 %all-to-all-start = ((f32[8,1,128]{2,1,0:T(1,128)}), f32[8,1,128]{2,1,0:T(1,128)S(1)}, u32[]{:S(2)}, u32[]{:S(2)}) async-start(f32[8,1,128]{2,1,0:T(1,128)} %broadcast_in_dim.80), calls=%async_computation | async-start | bytes 8192 | tf_op jit(solution)/shard_map/all_to_all | solution.py:401
  52.3 53.7 %all-to-all-start.4 = ((f16[8,1,64,2048]{3,2,1,0:T(8,128)(2,1)}), f16[8,1,64,2048]{3,2,1,0:T(8,128)(2,1)S(1)}, u32[]{:S(2)}, u32[]{:S(2)}) async-start(f16[8,1,64,2048]{3,2,1,0:T(8,128)(2,1)} %convert_bitcast_fusion), calls=%async_computation.4 | async-start | bytes 4194304 | tf_op jit(solution)/shard_map/all_to_all | solution.py:401
  106.0 1.4 copy-start
  107.4 52.1 %all-to-all-start.1 = ((f16[8,1,64,2048]{3,2,1,0:T(8,128)(2,1)}), f16[8,1,64,2048]{3,2,1,0:T(8,128)(2,1)S(1)}, u32[]{:S(2)}, u32[]{:S(2)}) async-start(f16[8,1,64,2048]{3,2,1,0:T(8,128)(2,1)} %convert_bitcast_fusion.1), calls=%async_computation.1 | async-start | bytes 4194304 | tf_op jit(solution)/shard_map/all_to_all | solution.py:401
  159.4 262.5 %all-to-all-start.3 = ((f16[8,2,64,2048]{3,2,1,0:T(8,128)(2,1)}), f16[8,2,64,2048]{3,2,1,0:T(8,128)(2,1)}, u32[]{:S(2)}, u32[]{:S(2)}) async-start(f16[8,2,64,2048]{3,2,1,0:T(8,128)(2,1)} %bitcast.106), calls=%async_computation.3 | async-start | bytes 8388608 | tf_op jit(solution)/shard_map/all_to_all | solution.py:401
  164.1 15.0 %copy-start.7 = (s32[96]{0:T(128)S(1)}, s32[96]{0:T(128)}, u32[]{:S(2)}) copy-start(s32[96]{0:T(128)} %param.12) | copy-start | bytes 1156
  174.3 84.4 %collective-permute-start.12 = (bf16[2304,256]{1,0:T(8,128)(2,1)}, bf16[2304,256]{1,0:T(8,128)(2,1)S(1)}, u32[]{:S(2)}, u32[]{:S(2)}) collective-permute-start(bf16[2304,256]{1,0:T(8,128)(2,1)} %get-tuple-element.41), channel_id=1, source_target_pairs={{0,1},{1,2},{2,3},{3,0},{4,5},{5,6},{6,7},{7,4},{8,9},{9,10},{10,1... | collective-permute-start | bytes 3538952 | tf_op jit(solution)/shard_map/ppermute | solution.py:408
  176.2 85.1 %collective-permute-start.14 = (bf16[2304,256]{1,0:T(8,128)(2,1)}, bf16[2304,256]{1,0:T(8,128)(2,1)}, u32[]{:S(2)}, u32[]{:S(2)}) collective-permute-start(bf16[2304,256]{1,0:T(8,128)(2,1)} %get-tuple-element.42), channel_id=1, source_target_pairs={{0,3},{1,0},{2,1},{3,2},{4,7},{5,4},{6,5},{7,6},{8,11},{9,8},{10,9... | collective-permute-start | bytes 3538952 | tf_op jit(solution)/shard_map/ppermute | solution.py:408
  177.2 106.6 %collective-permute-start.13 = (bf16[2304,256]{1,0:T(8,128)(2,1)}, bf16[2304,256]{1,0:T(8,128)(2,1)}, u32[]{:S(2)}, u32[]{:S(2)}) collective-permute-start(bf16[2304,256]{1,0:T(8,128)(2,1)} %get-tuple-element.43), channel_id=1, source_target_pairs={{0,2},{1,3},{2,0},{3,1},{4,6},{5,7},{6,4},{7,5},{8,10},{9,11},{10,... | collective-permute-start | bytes 3538952 | tf_op jit(solution)/shard_map/ppermute | solution.py:408
  190.2 7.3 %copy-start.8 = (s32[8]{0:T(128)S(1)}, s32[8]{0:T(128)}, u32[]{:S(2)}) copy-start(s32[8]{0:T(128)} %get-tuple-element.21) | copy-start | bytes 100
  258.7 2.6 copy-start.5
  286.7 6.2 copy-start.4
  286.7 52.3 %collective-permute-start.15 = (bf16[2304,256]{1,0:T(8,128)(2,1)S(1)}, bf16[2304,256]{1,0:T(8,128)(2,1)}, u32[]{:S(2)}, u32[]{:S(2)}) collective-permute-start(bf16[2304,256]{1,0:T(8,128)(2,1)S(1)} %fusion.2), channel_id=1, source_target_pairs={{0,4},{1,5},{2,6},{3,7},{4,0},{5,1},{6,2},{7,3},{8,12},{9,13},{10,... | collective-permute-start | bytes 3538952 | tf_op jit(solution)/shard_map/ppermute | solution.py:432
  341.0 35.7 %collective-permute-start.18 = (bf16[2304,256]{1,0:T(8,128)(2,1)S(1)}, bf16[2304,256]{1,0:T(8,128)(2,1)}, u32[]{:S(2)}, u32[]{:S(2)}) collective-permute-start(bf16[2304,256]{1,0:T(8,128)(2,1)S(1)} %add_convert_fusion), channel_id=1, source_target_pairs={{0,3},{1,0},{2,1},{3,2},{4,7},{5,4},{6,5},{7,6},{8,11},{9,8},{10,9... | collective-permute-start | bytes 3538952 | tf_op jit(solution)/shard_map/ppermute | solution.py:408
  348.9 53.5 %collective-permute-start.17 = (bf16[2304,256]{1,0:T(8,128)(2,1)S(1)}, bf16[2304,256]{1,0:T(8,128)(2,1)}, u32[]{:S(2)}, u32[]{:S(2)}) collective-permute-start(bf16[2304,256]{1,0:T(8,128)(2,1)S(1)} %add_convert_fusion), channel_id=1, source_target_pairs={{0,2},{1,3},{2,0},{3,1},{4,6},{5,7},{6,4},{7,5},{8,10},{9,11},{10,... | collective-permute-start | bytes 3538952 | tf_op jit(solution)/shard_map/ppermute | solution.py:408
  352.2 50.2 %collective-permute-start.16 = (bf16[2304,256]{1,0:T(8,128)(2,1)S(1)}, bf16[2304,256]{1,0:T(8,128)(2,1)}, u32[]{:S(2)}, u32[]{:S(2)}) collective-permute-start(bf16[2304,256]{1,0:T(8,128)(2,1)S(1)} %add_convert_fusion), channel_id=1, source_target_pairs={{0,1},{1,2},{2,3},{3,0},{4,5},{5,6},{6,7},{7,4},{8,9},{9,10},{10,1... | collective-permute-start | bytes 3538952 | tf_op jit(solution)/shard_map/ppermute | solution.py:408
  402.4 4.1 copy-start.1
  421.9 138.8 %all-to-all-start.2 = ((f16[8,2,64,2048]{3,2,1,0:T(8,128)(2,1)}), f16[8,2,64,2048]{3,2,1,0:T(8,128)(2,1)}, u32[]{:S(2)}, u32[]{:S(2)}) async-start(f16[8,2,64,2048]{3,2,1,0:T(8,128)(2,1)} %bitcast.107), calls=%async_computation.2 | async-start | bytes 8388608 | tf_op jit(solution)/shard_map/all_to_all | solution.py:401
  427.5 85.6 %collective-permute-start.9 = (f16[1,64,2048]{2,1,0:T(8,128)(2,1)}, f16[1,64,2048]{2,1,0:T(8,128)(2,1)S(1)}, u32[]{:S(2)}, u32[]{:S(2)}) collective-permute-start(f16[1,64,2048]{2,1,0:T(8,128)(2,1)} %get-tuple-element.50), channel_id=1, source_target_pairs={{0,1},{1,2},{2,3},{3,0},{4,5},{5,6},{6,7},{7,4},{8,9},{9,10},{10,1... | collective-permute-start | bytes 786440 | tf_op jit(solution)/shard_map/ppermute | solution.py:408
  429.4 78.4 %copy-start.6 = (f16[1,64,2048]{2,1,0:T(8,128)(2,1)S(1)}, f16[1,64,2048]{2,1,0:T(8,128)(2,1)}, u32[]{:S(2)}) copy-start(f16[1,64,2048]{2,1,0:T(8,128)(2,1)} %get-tuple-element.51) | copy-start | bytes 786436
  507.8 7.8 %collective-permute-start.11 = (f16[1,64,2048]{2,1,0:T(8,128)(2,1)S(1)}, f16[1,64,2048]{2,1,0:T(8,128)(2,1)S(1)}, u32[]{:S(2)}, u32[]{:S(2)}) collective-permute-start(f16[1,64,2048]{2,1,0:T(8,128)(2,1)S(1)} %copy-done.6), channel_id=1, source_target_pairs={{0,3},{1,0},{2,1},{3,2},{4,7},{5,4},{6,5},{7,6},{8,11},{9,8},{10,9... | collective-permute-start | bytes 786440 | tf_op jit(solution)/shard_map/ppermute | solution.py:408
  508.9 21.2 %collective-permute-start.10 = (f16[1,64,2048]{2,1,0:T(8,128)(2,1)S(1)}, f16[1,64,2048]{2,1,0:T(8,128)(2,1)S(1)}, u32[]{:S(2)}, u32[]{:S(2)}) collective-permute-start(f16[1,64,2048]{2,1,0:T(8,128)(2,1)S(1)} %get-tuple-element.52), channel_id=1, source_target_pairs={{0,2},{1,3},{2,0},{3,1},{4,6},{5,7},{6,4},{7,5},{8,10},{9,11},{10,... | collective-permute-start | bytes 786440 | tf_op jit(solution)/shard_map/ppermute | solution.py:408
  597.1 3.2 copy-start.3
  600.3 2.2 copy-start.2
  603.0 12.3 %collective-permute-start = (f16[1,64,2048]{2,1,0:T(8,128)(2,1)S(1)}, f16[1,64,2048]{2,1,0:T(8,128)(2,1)S(1)}, u32[]{:S(2)}, u32[]{:S(2)}) collective-permute-start(f16[1,64,2048]{2,1,0:T(8,128)(2,1)S(1)} %get-tuple-element.53), channel_id=1, source_target_pairs={{0,1},{1,2},{2,3},{3,0},{4,5},{5,6},{6,7},{7,4},{8,9},{9,10},{10,1... | collective-permute-start | bytes 786440 | tf_op jit(solution)/shard_map/ppermute | solution.py:408
  603.1 15.8 %collective-permute-start.2 = (f16[1,64,2048]{2,1,0:T(8,128)(2,1)S(1)}, f16[1,64,2048]{2,1,0:T(8,128)(2,1)S(1)}, u32[]{:S(2)}, u32[]{:S(2)}) collective-permute-start(f16[1,64,2048]{2,1,0:T(8,128)(2,1)S(1)} %get-tuple-element.54), channel_id=1, source_target_pairs={{0,3},{1,0},{2,1},{3,2},{4,7},{5,4},{6,5},{7,6},{8,11},{9,8},{10,9... | collective-permute-start | bytes 786440 | tf_op jit(solution)/shard_map/ppermute | solution.py:408
  606.0 12.9 %collective-permute-start.1 = (f16[1,64,2048]{2,1,0:T(8,128)(2,1)S(1)}, f16[1,64,2048]{2,1,0:T(8,128)(2,1)S(1)}, u32[]{:S(2)}, u32[]{:S(2)}) collective-permute-start(f16[1,64,2048]{2,1,0:T(8,128)(2,1)S(1)} %get-tuple-element.55), channel_id=1, source_target_pairs={{0,2},{1,3},{2,0},{3,1},{4,6},{5,7},{6,4},{7,5},{8,10},{9,11},{10,... | collective-permute-start | bytes 786440 | tf_op jit(solution)/shard_map/ppermute | solution.py:408
  606.3 31.5 %collective-permute-start.3 = (f16[2,64,2048]{2,1,0:T(8,128)(2,1)S(1)}, f16[2,64,2048]{2,1,0:T(8,128)(2,1)S(1)}, u32[]{:S(2)}, u32[]{:S(2)}) collective-permute-start(f16[2,64,2048]{2,1,0:T(8,128)(2,1)S(1)} %get-tuple-element.47), channel_id=1, source_target_pairs={{0,1},{1,2},{2,3},{3,0},{4,5},{5,6},{6,7},{7,4},{8,9},{9,10},{10,1... | collective-permute-start | bytes 1572872 | tf_op jit(solution)/shard_map/ppermute | solution.py:408
  606.9 34.4 %collective-permute-start.5 = (f16[2,64,2048]{2,1,0:T(8,128)(2,1)S(1)}, f16[2,64,2048]{2,1,0:T(8,128)(2,1)S(1)}, u32[]{:S(2)}, u32[]{:S(2)}) collective-permute-start(f16[2,64,2048]{2,1,0:T(8,128)(2,1)S(1)} %get-tuple-element.48), channel_id=1, source_target_pairs={{0,3},{1,0},{2,1},{3,2},{4,7},{5,4},{6,5},{7,6},{8,11},{9,8},{10,9... | collective-permute-start | bytes 1572872 | tf_op jit(solution)/shard_map/ppermute | solution.py:408
  615.4 26.1 %collective-permute-start.4 = (f16[2,64,2048]{2,1,0:T(8,128)(2,1)S(1)}, f16[2,64,2048]{2,1,0:T(8,128)(2,1)S(1)}, u32[]{:S(2)}, u32[]{:S(2)}) collective-permute-start(f16[2,64,2048]{2,1,0:T(8,128)(2,1)S(1)} %get-tuple-element.49), channel_id=1, source_target_pairs={{0,2},{1,3},{2,0},{3,1},{4,6},{5,7},{6,4},{7,5},{8,10},{9,11},{10,... | collective-permute-start | bytes 1572872 | tf_op jit(solution)/shard_map/ppermute | solution.py:408
  618.9 40.8 %collective-permute-start.6 = (f16[2,64,2048]{2,1,0:T(8,128)(2,1)S(1)}, f16[2,64,2048]{2,1,0:T(8,128)(2,1)S(1)}, u32[]{:S(2)}, u32[]{:S(2)}) collective-permute-start(f16[2,64,2048]{2,1,0:T(8,128)(2,1)S(1)} %get-tuple-element.44), channel_id=1, source_target_pairs={{0,1},{1,2},{2,3},{3,0},{4,5},{5,6},{6,7},{7,4},{8,9},{9,10},{10,1... | collective-permute-start | bytes 1572872 | tf_op jit(solution)/shard_map/ppermute | solution.py:408
  619.0 43.0 %collective-permute-start.8 = (f16[2,64,2048]{2,1,0:T(8,128)(2,1)S(1)}, f16[2,64,2048]{2,1,0:T(8,128)(2,1)S(1)}, u32[]{:S(2)}, u32[]{:S(2)}) collective-permute-start(f16[2,64,2048]{2,1,0:T(8,128)(2,1)S(1)} %get-tuple-element.45), channel_id=1, source_target_pairs={{0,3},{1,0},{2,1},{3,2},{4,7},{5,4},{6,5},{7,6},{8,11},{9,8},{10,9... | collective-permute-start | bytes 1572872 | tf_op jit(solution)/shard_map/ppermute | solution.py:408
  637.8 24.4 %collective-permute-start.7 = (f16[2,64,2048]{2,1,0:T(8,128)(2,1)S(1)}, f16[2,64,2048]{2,1,0:T(8,128)(2,1)S(1)}, u32[]{:S(2)}, u32[]{:S(2)}) collective-permute-start(f16[2,64,2048]{2,1,0:T(8,128)(2,1)S(1)} %get-tuple-element.46), channel_id=1, source_target_pairs={{0,2},{1,3},{2,0},{3,1},{4,6},{5,7},{6,4},{7,5},{8,10},{9,11},{10,... | collective-permute-start | bytes 1572872 | tf_op jit(solution)/shard_map/ppermute | solution.py:408

commit v3 on v2

--- a/solution.py
+++ b/solution.py
@@ -120,9 +120,9 @@
 
 def solve_kernel(
     members, half_members, first_slot,
-    row_ref, scale_ref, keep_ref, factor_ref, data_ref, *rest,
+    row_ref, scale_ref, keep_ref, factor_ref, ratio_ref, data_ref, *rest,
 ):
-    work_ref, back_ref, whole, low, held, mixed = rest[-6:]
+    work_ref, back_ref, whole, low = rest[-4:]
     rows = data_ref.shape[2]
     size, width = whole.shape
     slot = first_slot + pl.program_id(0)
@@ -133,15 +133,10 @@
         whole[pl.ds(member * rows, rows), :] = part
         low[pl.ds(member * rows, rows), :] = part.astype(BF16)
 
-    held[...] = jnp.zeros_like(held)
-
-    def add_gram(k, carry):
-        block = low[:, pl.ds(pl.multiple_of(k * tile, tile), tile)]
-        held[...] += dot_nt(block, block)
-        return carry
-
-    lax.fori_loop(0, width // tile, add_gram, 0)
-    gram = held[...]
+    gram = jnp.zeros((size, size), F32)
+    for k in range(width // tile):
+        block = low[:, k * tile:(k + 1) * tile]
+        gram = gram + dot_nt(block, block)
     row_ids = lax.broadcasted_iota(jnp.int32, (size, size), 0)
     col_ids = lax.broadcasted_iota(jnp.int32, (size, size), 1)
     norm_sq = jnp.sum(jnp.where(row_ids == col_ids, gram, 0.0), keepdims=True) + EPS
@@ -159,32 +154,28 @@
     mix = (COEF_A * (u + v) + dot(v.astype(BF16), u_low)).astype(BF16)
     factor = factor_ref[slot]
     keep = keep_ref[slot]
-    mixed[...] = mix
-
-    def apply(k, carry):
-        cols = pl.ds(pl.multiple_of(k * tile, tile), tile)
-        moved = dot(mixed[...], low[:, cols])
+    for k in range(width // tile):
+        cols = slice(k * tile, (k + 1) * tile)
+        moved = dot(mix, low[:, cols])
         result = ((COEF_A * COEF_A) * whole[:, cols] + moved) * inverse
         work_ref[0, :, cols] = result * factor
         whole[:, cols] = result * keep
-        return carry
-
-    lax.fori_loop(0, width // tile, apply, 0)
     for turn in range(half_members):
         start = pl.multiple_of(row_ref[turn], rows)
-        back_ref[turn, 0] = whole[pl.ds(start, rows), :]
-
-
-def solve(row_starts, scale, keep, factor, data, work, first_slot, most, half_members):
+        block = whole[pl.ds(start, rows), :]
+        back_ref[turn, 0] = block * ratio_ref[slot] if turn == 0 else block
+
+
+def solve(row_starts, scale, keep, factor, ratio, data, work, first_slot, most, half_members):
     members, chunk, rows, width = data.shape
     size = members * rows
-    inputs = [row_starts, scale, keep, factor, data]
-    specs = [SMEM_SPEC] * 4 + [pl.BlockSpec((members, 1, rows, width), lambda i: (0, i, 0, 0))]
+    inputs = [row_starts, scale, keep, factor, ratio, data]
+    specs = [SMEM_SPEC] * 5 + [pl.BlockSpec((members, 1, rows, width), lambda i: (0, i, 0, 0))]
     aliases = {}
     if work is not None:
         inputs.append(work)
         specs.append(ANY_SPEC)
-        aliases = {5: 0}
+        aliases = {6: 0}
     flops = chunk * (4 * size * size * width + 10 * size ** 3)
     return pl.pallas_call(
         functools.partial(solve_kernel, members, half_members, first_slot),
@@ -201,42 +192,52 @@
         scratch_shapes=[
             pltpu.VMEM((size, width), F32),
             pltpu.VMEM((size, width), BF16),
-            pltpu.VMEM((size, size), F32),
-            pltpu.VMEM((size, size), BF16),
         ],
         input_output_aliases=aliases,
         cost_estimate=cost(flops, data.size * 12),
     )(*inputs)
 
 
-def home_kernel(ids_ref, factor_ref, data_ref, *rest):
-    rest[-1][...] = data_ref[0] * factor_ref[pl.program_id(0)]
-
-
-def home(ids, factor, data, out, per_group):
-    half_members, chunk, rows, width = data.shape
-    inputs = [ids, factor, data]
-    specs = [
-        SMEM_SPEC,
-        pl.BlockSpec((1, 1, rows, width), lambda i, ids: (i // chunk, i % chunk, 0, 0)),
-    ]
+def home_kernel(half_members, ids_ref, local_ref, *rest):
+    received = rest[:half_members - 1]
+    out_ref, held, in_sem, out_sem = rest[-4:]
+    chunk = local_ref.shape[1]
+    loads, stores = [], []
+    for turn in range(half_members):
+        for slot in range(chunk):
+            i = turn * chunk + slot
+            source = received[turn - 1].at[slot] if turn else local_ref.at[0, slot]
+            loads.append(pltpu.make_async_copy(source, held.at[i], in_sem.at[i]))
+            loads[-1].start()
+    for i, load in enumerate(loads):
+        load.wait()
+        stores.append(pltpu.make_async_copy(held.at[i], out_ref.at[ids_ref[i]], out_sem.at[i]))
+        stores[-1].start()
+    for store in stores:
+        store.wait()
+
+
+def home(ids, local, received, out, per_group):
+    half_members, chunk, rows, width = local.shape
+    number = half_members * chunk
+    inputs = [ids, local] + received
     aliases = {}
     if out is not None:
+        aliases = {len(inputs): 0}
         inputs.append(out)
-        specs.append(ANY_SPEC)
-        aliases = {3: 0}
     return pl.pallas_call(
-        home_kernel,
-        grid_spec=pltpu.PrefetchScalarGridSpec(
-            num_scalar_prefetch=1,
-            grid=(half_members * chunk,),
-            in_specs=specs,
-            out_specs=pl.BlockSpec((1, rows, width), lambda i, ids: (ids[i], 0, 0)),
-        ),
+        functools.partial(home_kernel, half_members),
+        in_specs=[SMEM_SPEC] + [ANY_SPEC] * (len(inputs) - 1),
+        out_specs=ANY_SPEC,
         out_shape=jax.ShapeDtypeStruct((per_group, rows, width), F32),
+        scratch_shapes=[
+            pltpu.VMEM((number, rows, width), F32),
+            pltpu.SemaphoreType.DMA((number,)),
+            pltpu.SemaphoreType.DMA((number,)),
+        ],
         input_output_aliases=aliases,
         name="home",
-        cost_estimate=cost(1e8, data.size * 8),
+        cost_estimate=cost(2e9, number * rows * width * 8),
     )(*inputs)
 
 
@@ -253,15 +254,17 @@
 
     squares = jnp.square(rounded.astype(F32))
     sum_ref[...] += jnp.sum(squares, axis=(0, 1), keepdims=True)
-    for k in range(low.shape[0] // BLOCK):
-
-        @pl.when(i == k)
-        def _(k=k):
-            product = dot_nt(rounded, low[:(k + 1) * BLOCK, :]).astype(BF16)
-            start = k * (k + 1) // 2
-            for j in range(k + 1):
-                rows = slice((start + j) * BLOCK, (start + j + 1) * BLOCK)
-                packed_ref[rows, :] = product[:, j * BLOCK:(j + 1) * BLOCK]
+    start = i * (i + 1) // 2
+
+    def columns(j, carry):
+        other = low[pl.ds(pl.multiple_of(j * (2 * BLOCK), 2 * BLOCK), 2 * BLOCK), :]
+        product = dot_nt(rounded, other).astype(BF16)
+        for k in range(2):
+            place = pl.multiple_of((start + 2 * j + k) * BLOCK, BLOCK)
+            packed_ref[pl.ds(place, BLOCK), :] = product[:, k * BLOCK:(k + 1) * BLOCK]
+        return carry
+
+    lax.fori_loop(0, (i + 2) // 2, columns, 0)
 
 
 def wide_gram(momentum, grad):
@@ -290,12 +293,31 @@
 
 
 def wide_solve_kernel(
-    coef_ref, turn_ref, table_ref, packed_ref, merged_ref, out_ref, gram, first, second, low
+    coef_ref, turn_ref, table_ref, merged_ref, *rest
 ):
+    out_ref, packed_ref, gram, first, second, low, sem = rest[-7:]
     height, _ = out_ref.shape
     number = height // BLOCK
     pieces = packed_ref.shape[1] // PIECE
+    loads = [
+        pltpu.make_async_copy(piece, packed_ref.at[i], sem.at[i]) for i, piece in enumerate(rest[:-7])
+    ]
+    for load in loads:
+        load.start()
     inverse, inverse_sq, outer = coef_ref[0], coef_ref[1], coef_ref[2]
+
+    def prepare(i, carry):
+        rows = pl.ds(pl.multiple_of(i * BLOCK, BLOCK), BLOCK)
+        value = merged_ref[rows, :] * inverse
+        first[rows, :] = value
+        second[rows, :] = jnp.zeros_like(value)
+        low[0, rows, :] = value.astype(BF16)
+        return carry
+
+    lax.fori_loop(0, number, prepare, 0)
+
+    for load in loads:
+        load.wait()
 
     def assemble(i, carry):
         rows = pl.ds(pl.multiple_of(i * BLOCK, BLOCK), BLOCK)
@@ -316,16 +338,6 @@
 
     lax.fori_loop(0, number, assemble, 0)
 
-    def prepare(i, carry):
-        rows = pl.ds(pl.multiple_of(i * BLOCK, BLOCK), BLOCK)
-        value = merged_ref[rows, :] * inverse
-        first[rows, :] = value
-        second[rows, :] = jnp.zeros_like(value)
-        low[0, rows, :] = value.astype(BF16)
-        return carry
-
-    lax.fori_loop(0, number, prepare, 0)
-
     def sweep(step, carry):
         from_first, from_second, from_product = table_ref[step], table_ref[12 + step], table_ref[24 + step]
         now = step % 2
@@ -363,21 +375,24 @@
 
 def wide_solve(coef, turns, packed, merged):
     height, width = merged.shape
+    number = len(packed)
     table = jnp.asarray(SWEEP_FIRST + SWEEP_SECOND + SWEEP_PRODUCT, F32)
     return pl.pallas_call(
         wide_solve_kernel,
         out_shape=jax.ShapeDtypeStruct((height, width), F32),
-        in_specs=[SMEM_SPEC] * 3 + [pl.BlockSpec(memory_space=pltpu.VMEM)] * 2,
+        in_specs=[SMEM_SPEC] * 3 + [pl.BlockSpec(memory_space=pltpu.VMEM)] + [ANY_SPEC] * number,
         out_specs=pl.BlockSpec(memory_space=pltpu.VMEM),
         scratch_shapes=[
+            pltpu.VMEM((number,) + packed[0].shape, BF16),
             pltpu.VMEM((height, height), BF16),
             pltpu.VMEM((height, width), F32),
             pltpu.VMEM((height, width), F32),
             pltpu.VMEM((2, height, width), BF16),
+            pltpu.SemaphoreType.DMA((number,)),
         ],
         name="wide_solve",
         cost_estimate=cost(24 * height * height * width, height * width * 8),
-    )(coef, turns, table, packed, merged)
+    )(coef, turns, table, merged, *packed)
 
 
 def on_device(expert_momentum, expert_grad, wide_momentum, wide_grad, assignment, expert_tokens):
@@ -386,7 +401,7 @@
     per_group, rows, width = expert_momentum.shape
     _, wide_width = wide_momentum.shape[1:]
     most = 2 * -(-per_group // members)
-    sizes = [1] + [2] * ((most - 2) // 2) + [1]
+    sizes = [2, 1] * (most // 3) + [1] * (most % 3)
     starts = [sum(sizes[:i]) for i in range(len(sizes))]
     group_index = lax.axis_index("grp")
     me = lax.axis_index("fsdp")
@@ -417,9 +432,10 @@
     notes = jnp.pad(notes, (0, -notes.shape[0] % 128))
     notes = jnp.broadcast_to(notes[None, None, :], (members, 1, notes.shape[0]))
     notes = across(notes)[:, 0]
+    coded = lax.optimization_barrier(scaled.astype(jnp.float16))
     arrived = []
     for start, chunk in zip(starts, sizes):
-        picked = scaled[slots[:, start:start + chunk].reshape(-1)].astype(jnp.float16)
+        picked = coded[slots[:, start:start + chunk].reshape(-1)]
         arrived.append(across(picked.reshape(members, chunk, rows, width)))
 
     packed_rows = packed.shape[0] // half_members
@@ -431,7 +447,7 @@
     part = total.astype(BF16)
     other = lax.ppermute(part, "fsdp", mirror)
     part = (part.astype(F32) + other.astype(F32)).astype(BF16)
-    packed = jnp.stack([part] + [shifted(part, turn) for turn in range(1, half_members)])
+    packed = [part] + [shifted(part, turn) for turn in range(1, half_members)]
     wide_norm = jnp.sum(notes[:, per_group]) + EPS
     coef = jnp.stack(
         [lax.rsqrt(wide_norm), 1.0 / wide_norm, jnp.float32(math.sqrt(wide_width * members))]
@@ -451,6 +467,7 @@
     slot_scale = jnp.sum(jnp.where(own_pick[:, None, :], tops[None], 0.0), axis=2) / F16_TOP
     slot_keep = jnp.sum(jnp.where(own_pick, keep[None], 0.0), axis=1)
     slot_factor = jnp.sum(jnp.where(own_pick, factor[None], 0.0), axis=1)
+    slot_ratio = slot_factor / slot_keep
     slot_factor = jnp.where(jnp.arange(most) < own_count, slot_factor, 0.0)
     home_factor = jnp.sum(jnp.where(half_pick, (factor / keep)[None, None], 0.0), axis=2)
     slot_scale = slot_scale.reshape(-1)
@@ -461,18 +478,15 @@
     for index, piece in enumerate(arrived):
         start, chunk = starts[index], sizes[index]
         work, back = solve(
-            row_starts, slot_scale, slot_keep, slot_factor, piece.astype(F32), work,
+            row_starts, slot_scale, slot_keep, slot_factor, slot_ratio, piece.astype(F32), work,
             start, most, half_members,
         )
-        pieces = [back[0]]
+        received = []
         for turn in range(1, half_members):
-            pieces.append(shifted(back[turn].astype(jnp.float16), turn).astype(F32))
-        back = jnp.stack(pieces)
-        expert_out = home(
-            half_slots[:, start:start + chunk].reshape(-1),
-            home_factor[:, start:start + chunk].reshape(-1),
-            back, expert_out, per_group,
-        )
+            piece = shifted(back[turn].astype(jnp.float16), turn)
+            received.append(piece.astype(F32) * home_factor[turn, start:start + chunk, None, None])
+        ids = half_slots[:, start:start + chunk].reshape(-1)
+        expert_out = home(ids, back, received, expert_out, per_group)
     return (expert_out, wide_out[None], work[None])
 
 

time: 686 us -> 708 us (1.032)
  waiting for transfers between devices: 308 us -> 365 us
  Pallas kernels: 189 us -> 170 us
  local copies, waits for them, and re-layouts: 54.7 us -> 40.7 us
  other arithmetic: 65.1 us -> 57.7 us
    ppermute x1, waiting for transfers between devices: 46.1 us -> 78.9 us  [on_device(): other = lax.ppermute(part, 'fsdp', mirror)]
    mul x0 -> x12, other arithmetic: none -> 15.7 us  [on_device(): piece.astype(F32) * home_factor[turn, start:start + chunk, None, None]]
    another operation x21 -> x4, other arithmetic: 16.5 us -> 2.67 us  [the longest x16 8.19 us: on_device(): back = jnp.stack(pieces)]
    all_to_all x5, waiting for transfers between devices: 69.4 us -> 82.8 us  [across(): lax.all_to_all(value, 'fsdp', split_axis=0, concat_axis=0, tiled=True)]
    pallas_call x4, Pallas kernels: 59.5 us -> 47.6 us  [solve(): pl.pallas_call(functools.partial(solve_kernel, members, half_members, fir...]
    convert_element_type x4 -> x1, other arithmetic: 19.9 us -> 8.41 us  [on_device(): coded = lax.optimization_barrier(scaled.astype(jnp.float16))]
    ppermute x18, waiting for transfers between devices: 193 us -> 203 us  [shifted(): return lax.ppermute(value, 'fsdp', pairs)]
    pallas_call x4, Pallas kernels: 23.6 us -> 14.6 us  [home(): pl.pallas_call(functools.partial(home_kernel, half_members), in_specs=[SM...]
  transfers between devices with their start and end apart: 24 -> 24, of which waited for: 16 -> 15; matrix products, arithmetic and copies ran while one was open for 15% -> 12% of each run, Pallas kernels for 17% -> 16%
where the time goes in v3:
time: 708 us; the launch traced here: 707 us
  waiting for transfers between devices  365 us (52%)
  Pallas kernels  170 us (24%)
  starting transfers between devices  65.4 us (9%)
  other arithmetic  57.7 us (8%)
  local copies, waits for them, and re-layouts  40.7 us (6%)
  between operations  8 us (1%)
    ppermute x18, waiting for transfers between devices, shifted(): return lax.ppermute(value, 'fsdp', pairs)  203 us
    all_to_all x5, waiting for transfers between devices, across(): lax.all_to_all(value, 'fsdp', split_axis=0, concat_axis=0, tiled=True)  82.8 us
    ppermute x1, waiting for transfers between devices, on_device(): other = lax.ppermute(part, 'fsdp', mirror)  78.9 us
    pallas_call x1, Pallas kernels, wide_solve(): pl.pallas_call(wide_solve_kernel, out_shape=jax.ShapeDtypeStruct((height,...  77.5 us
    pallas_call x4, Pallas kernels, solve(): pl.pallas_call(functools.partial(solve_kernel, members, half_members, fir...  47.6 us
    all_to_all x5, starting transfers between devices, across(): lax.all_to_all(value, 'fsdp', split_axis=0, concat_axis=0, tiled=True)  34.2 us
    ppermute x18, starting transfers between devices, shifted(): return lax.ppermute(value, 'fsdp', pairs)  28.7 us
    gather x4, local copies, waits for them, and re-layouts, on_device(): picked = coded[slots[:, start:start + chunk].reshape(-1)]  24.7 us
  transfers between devices with their start and end apart: 24, of which 15 were waited for; matrix products, arithmetic and copies ran while one was open for 12% of the time, Pallas kernels for 16%

profile of v3, /device:TPU:0, one launch (start us, length us, event | category | flops | bytes accessed | tf_op | source)
XLA Modules:
  0.0 707.1 jit_solution(5719055113770677334)
XLA Ops:
  0.6 14.3 %wide_gram.1 = (f32[2048,512]{1,0:T(8,128)}, bf16[9216,256]{1,0:T(8,128)(2,1)}, f32[8,128]{1,0:T(8,128)}) custom-call(f32[2048,512]{1,0:T(8,128)} %bitcast.74, f32[2048,512]{1,0:T(8,128)} %bitcast.75), custom_call_target="tpu_custom_call" | custom-call | flops 2415919104 | bytes 17301504 | tf_op jit(solution)/shard_map/wide_gram/pallas_call | solution.py:275
  16.1 13.9 %merge.1 = (f32[24,64,2048]{2,1,0:T(8,128)}, f32[24,8,128]{2,1,0:T(8,128)}) custom-call(f32[24,64,2048]{2,1,0:T(8,128)} %momentum_ref.1, f32[24,64,2048]{2,1,0:T(8,128)} %grad_ref.1), custom_call_target="tpu_custom_call" | custom-call | flops 15728640 | bytes 37748736 | tf_op jit(solution)/shard_map/merge/pallas_call | solution.py:107
  32.5 7.3 %all-to-all-start = ((f32[8,1,128]{2,1,0:T(1,128)}), f32[8,1,128]{2,1,0:T(1,128)S(1)}, u32[]{:S(2)}, u32[]{:S(2)}) async-start(f32[8,1,128]{2,1,0:T(1,128)} %broadcast_in_dim.81), calls=%async_computation | async-start | bytes 8192 | tf_op jit(solution)/shard_map/all_to_all | solution.py:416
  39.9 2.5 route.1
  43.3 8.4 %convert_element_type.180 = f16[24,64,2048]{2,1,0:T(8,128)(2,1)} convert(f32[24,64,2048]{2,1,0:T(8,128)} %get-tuple-element.22) | non-fusion elementwise | flops 3145728 | bytes 18874368 | tf_op jit(solution)/shard_map/convert_element_type | solution.py:435
  51.7 5.5 gather_fusion.3
  57.2 6.0 all-to-all-start.3
  63.2 5.5 gather_fusion.1
  68.6 42.2 %all-to-all-done.3 = f16[8,1,64,2048]{3,2,1,0:T(8,128)(2,1)S(1)} async-done(((f16[8,1,64,2048]{3,2,1,0:T(8,128)(2,1)}), f16[8,1,64,2048]{3,2,1,0:T(8,128)(2,1)S(1)}, u32[]{:S(2)}, u32[]{:S(2)}) %all-to-all-start.3) | async-done | bytes 2097184 | tf_op jit(solution)/shard_map/all_to_all | solution.py:416
  110.8 4.3 all-to-all-start.1
  115.4 7.0 gather_fusion.4
  122.4 40.6 %all-to-all-done.1 = f16[8,1,64,2048]{3,2,1,0:T(8,128)(2,1)} async-done(((f16[8,1,64,2048]{3,2,1,0:T(8,128)(2,1)}), f16[8,1,64,2048]{3,2,1,0:T(8,128)(2,1)}, u32[]{:S(2)}, u32[]{:S(2)}) %all-to-all-start.1) | async-done | bytes 2097184 | tf_op jit(solution)/shard_map/all_to_all | solution.py:416
  163.0 4.6 all-to-all-start.4
  173.8 3.9 dynamic-slice_bitcast_fusion.2
  177.6 1.9 collective-permute-start.12
  180.6 1.9 collective-permute-start.13
  184.6 6.9 gather_fusion.2
  191.4 70.6 %collective-permute-done.12 = bf16[2304,256]{1,0:T(8,128)(2,1)S(1)} collective-permute-done((bf16[2304,256]{1,0:T(8,128)(2,1)}, bf16[2304,256]{1,0:T(8,128)(2,1)S(1)}, u32[]{:S(2)}, u32[]{:S(2)}) %collective-permute-start.12) | collective-permute-done | bytes 1179680 | tf_op jit(solution)/shard_map/ppermute | solution.py:423
  262.0 2.8 collective-permute-done.14
  264.8 22.6 %collective-permute-done.13 = bf16[2304,256]{1,0:T(8,128)(2,1)} collective-permute-done((bf16[2304,256]{1,0:T(8,128)(2,1)}, bf16[2304,256]{1,0:T(8,128)(2,1)}, u32[]{:S(2)}, u32[]{:S(2)}) %collective-permute-start.13) | collective-permute-done | bytes 1179680 | tf_op jit(solution)/shard_map/ppermute | solution.py:423
  287.3 2.9 fusion.2
  290.2 2.6 collective-permute-start.15
  298.2 12.0 %all-to-all-start.2 = ((f16[8,2,64,2048]{3,2,1,0:T(8,128)(2,1)}), f16[8,2,64,2048]{3,2,1,0:T(8,128)(2,1)}, u32[]{:S(2)}, u32[]{:S(2)}) async-start(f16[8,2,64,2048]{3,2,1,0:T(8,128)(2,1)} %bitcast.67), calls=%async_computation.2 | async-start | bytes 8388608 | tf_op jit(solution)/shard_map/all_to_all | solution.py:416
  310.2 78.9 %collective-permute-done.15 = bf16[2304,256]{1,0:T(8,128)(2,1)} collective-permute-done((bf16[2304,256]{1,0:T(8,128)(2,1)S(1)}, bf16[2304,256]{1,0:T(8,128)(2,1)}, u32[]{:S(2)}, u32[]{:S(2)}) %collective-permute-start.15) | collective-permute-done | bytes 1179680 | tf_op jit(solution)/shard_map/ppermute | solution.py:448
  389.1 2.6 add_convert_fusion.rest_0_
  391.6 8.3 %collective-permute-start.18 = (bf16[2304,256]{1,0:T(8,128)(2,1)}, bf16[2304,256]{1,0:T(8,128)(2,1)}, u32[]{:S(2)}, u32[]{:S(2)}) collective-permute-start(bf16[2304,256]{1,0:T(8,128)(2,1)} %add_convert_fusion.rest_0_), channel_id=1, source_target_pairs={{0,3},{1,0},{2,1},{3,2},{4,7},{5,4},{6,5},{7,6},{8,11},{9,8},{10,9... | collective-permute-start | bytes 3538952 | tf_op jit(solution)/shard_map/ppermute | solution.py:423
  399.9 2.6 collective-permute-start.17
  405.2 1.2 fusion.18
  406.4 26.8 %collective-permute-done.18.rest_3_ = bf16[2304,256]{1,0:T(8,128)(2,1)} collective-permute-done((bf16[2304,256]{1,0:T(8,128)(2,1)}, bf16[2304,256]{1,0:T(8,128)(2,1)}, u32[]{:S(2)}, u32[]{:S(2)}) %collective-permute-start.18) | collective-permute-done | bytes 1179680 | tf_op jit(solution)/shard_map/ppermute | solution.py:423
  433.2 40.8 %collective-permute-done.17.rest_2_ = bf16[2304,256]{1,0:T(8,128)(2,1)} collective-permute-done((bf16[2304,256]{1,0:T(8,128)(2,1)}, bf16[2304,256]{1,0:T(8,128)(2,1)}, u32[]{:S(2)}, u32[]{:S(2)}) %collective-permute-start.17) | collective-permute-done | bytes 1179680 | tf_op jit(solution)/shard_map/ppermute | solution.py:423
  474.0 77.5 %wide_solve.1 = f32[2048,512]{1,0:T(8,128)} custom-call(f32[3]{0:T(128)} %pad_maximum_fusion.coef_ref, s32[4]{0:T(128)} %and_select_fusion.turn_ref, f32[36]{0:T(128)} %constant.109.clone.table_ref, f32[2048,512]{1,0:T(8,128)} %get-tuple-element.30.merged_ref, bf16[2304,256]{1,0:T(8,128)(2,1)} %add_convert_fusion.rest_0_, ...), custom_call_target="tpu_custom_call" | custom-call | flops 51539607552 | bytes 8388608 | tf_op jit(solution)/shard_map/wide_solve/pallas_call | solution.py:380
  551.5 4.0 convert_element_type.181.data_ref
  555.5 2.4 convert_element_type.183.data_ref
  557.9 6.6 convert_element_type.184.data_ref
  564.5 14.3 %shard_map.94 = (f32[6,512,2048]{2,1,0:T(8,128)}, f32[4,2,64,2048]{3,2,1,0:T(8,128)}) custom-call(s32[4]{0:T(128)} %add_multiply_fusion.row_ref, f32[48]{0:T(128)} %div.46.scale_ref, f32[6]{0:T(128)} %copy-done.4, f32[6]{0:T(128)} %get-tuple-element.78.factor_ref, f32[6]{0:T(128)} %get-tuple-element.77.ratio_ref, ...), custom_call_target="tpu_custom_call" | custom-call | flops 6979321856 | bytes 25165824 | tf_op jit(solution)/shard_map/pallas_call | solution.py:180
  578.8 9.5 %shard_map.95 = (f32[6,512,2048]{2,1,0:T(8,128)}, f32[4,1,64,2048]{3,2,1,0:T(8,128)}) custom-call(s32[4]{0:T(128)} %add_multiply_fusion.row_ref, f32[48]{0:T(128)} %div.46.scale_ref, f32[6]{0:T(128)} %copy-done.4, f32[6]{0:T(128)} %get-tuple-element.78.factor_ref, f32[6]{0:T(128)} %get-tuple-element.77.ratio_ref, ...), custom_call_target="tpu_custom_call", output_to_operand_aliasing={{0}: (6, {})} | custom-call | flops 3489660928 | bytes 12582912 | tf_op jit(solution)/shard_map/pallas_call | solution.py:180
  588.3 6.6 convert_element_type.182.data_ref
  594.9 14.3 %shard_map.96 = (f32[6,512,2048]{2,1,0:T(8,128)}, f32[4,2,64,2048]{3,2,1,0:T(8,128)}) custom-call(s32[4]{0:T(128)} %add_multiply_fusion.row_ref, f32[48]{0:T(128)} %div.46.scale_ref, f32[6]{0:T(128)} %copy-done.4, f32[6]{0:T(128)} %get-tuple-element.78.factor_ref, f32[6]{0:T(128)} %get-tuple-element.77.ratio_ref, ...), custom_call_target="tpu_custom_call", output_to_operand_aliasing={{0}: (6, {})} | custom-call | flops 6979321856 | bytes 25165824 | tf_op jit(solution)/shard_map/pallas_call | solution.py:180
  609.2 9.4 %shard_map.97 = (f32[6,512,2048]{2,1,0:T(8,128)}, f32[4,1,64,2048]{3,2,1,0:T(8,128)}) custom-call(s32[4]{0:T(128)} %add_multiply_fusion.row_ref, f32[48]{0:T(128)} %div.46.scale_ref, f32[6]{0:T(128)} %copy-done.4, f32[6]{0:T(128)} %get-tuple-element.78.factor_ref, f32[6]{0:T(128)} %get-tuple-element.77.ratio_ref, ...), custom_call_target="tpu_custom_call", output_to_operand_aliasing={{0}: (6, {})} | custom-call | flops 3489660928 | bytes 12582912 | tf_op jit(solution)/shard_map/pallas_call | solution.py:180
  618.6 1.9 convert.21
  620.9 1.9 collective-permute-start
  623.2 1.5 collective-permute-start.8
  624.7 1.5 collective-permute-start.7
  626.9 1.5 copy-done.1
  629.0 4.7 collective-permute-done.2
  633.7 1.5 convert_multiply_fusion.9.rest_2_
  635.2 2.9 collective-permute-start.5
  638.1 1.5 convert_multiply_fusion.10.rest_1_
  639.5 1.5 convert_multiply_fusion.11.rest_0_
  641.1 3.8 collective-permute-done.8
  644.9 1.4 convert_multiply_fusion.6.rest_2_
  646.3 2.9 collective-permute-start.11
  649.2 1.5 convert_multiply_fusion.7.rest_1_
  651.4 2.0 collective-permute-start.10
  653.4 1.5 convert_multiply_fusion.8.rest_0_
  654.9 12.5 %collective-permute-done.5 = f16[2,64,2048]{2,1,0:T(8,128)(2,1)S(1)} collective-permute-done((f16[2,64,2048]{2,1,0:T(8,128)(2,1)S(1)}, f16[2,64,2048]{2,1,0:T(8,128)(2,1)S(1)}, u32[]{:S(2)}, u32[]{:S(2)}) %collective-permute-start.5) | collective-permute-done | bytes 524320 | tf_op jit(solution)/shard_map/ppermute | solution.py:423
  667.3 1.2 convert_multiply_fusion.3.rest_2_
  668.6 10.9 %collective-permute-done.11 = f16[2,64,2048]{2,1,0:T(8,128)(2,1)S(1)} collective-permute-done((f16[2,64,2048]{2,1,0:T(8,128)(2,1)S(1)}, f16[2,64,2048]{2,1,0:T(8,128)(2,1)S(1)}, u32[]{:S(2)}, u32[]{:S(2)}) %collective-permute-start.11) | collective-permute-done | bytes 524320 | tf_op jit(solution)/shard_map/ppermute | solution.py:423
  680.6 4.8 collective-permute-done.10
  686.6 2.2 collective-permute-done.9
  689.9 4.2 home.4.rest_3_
  694.2 3.1 home.5.rest_3_
  699.6 4.2 home.6.rest_3_
  703.8 3.1 home.7
  (84 shorter events, 23.7 us)
Async XLA Ops:
  32.5 24.6 %all-to-all-start = ((f32[8,1,128]{2,1,0:T(1,128)}), f32[8,1,128]{2,1,0:T(1,128)S(1)}, u32[]{:S(2)}, u32[]{:S(2)}) async-start(f32[8,1,128]{2,1,0:T(1,128)} %broadcast_in_dim.81), calls=%async_computation | async-start | bytes 8192 | tf_op jit(solution)/shard_map/all_to_all | solution.py:416
  57.2 53.7 %all-to-all-start.3 = ((f16[8,1,64,2048]{3,2,1,0:T(8,128)(2,1)}), f16[8,1,64,2048]{3,2,1,0:T(8,128)(2,1)S(1)}, u32[]{:S(2)}, u32[]{:S(2)}) async-start(f16[8,1,64,2048]{3,2,1,0:T(8,128)(2,1)} %bitcast.69), calls=%async_computation.3 | async-start | bytes 4194304 | tf_op jit(solution)/shard_map/all_to_all | solution.py:416
  110.8 52.2 %all-to-all-start.1 = ((f16[8,1,64,2048]{3,2,1,0:T(8,128)(2,1)}), f16[8,1,64,2048]{3,2,1,0:T(8,128)(2,1)}, u32[]{:S(2)}, u32[]{:S(2)}) async-start(f16[8,1,64,2048]{3,2,1,0:T(8,128)(2,1)} %bitcast.68), calls=%async_computation.1 | async-start | bytes 4194304 | tf_op jit(solution)/shard_map/all_to_all | solution.py:416
  163.0 135.2 %all-to-all-start.4 = ((f16[8,2,64,2048]{3,2,1,0:T(8,128)(2,1)}), f16[8,2,64,2048]{3,2,1,0:T(8,128)(2,1)}, u32[]{:S(2)}, u32[]{:S(2)}) async-start(f16[8,2,64,2048]{3,2,1,0:T(8,128)(2,1)} %bitcast.66), calls=%async_computation.4 | async-start | bytes 8388608 | tf_op jit(solution)/shard_map/all_to_all | solution.py:416
  173.8 8.7 %copy-start.5 = (s32[96]{0:T(128)S(1)}, s32[96]{0:T(128)}, u32[]{:S(2)}) copy-start(s32[96]{0:T(128)} %param.12) | copy-start | bytes 1156
  177.6 84.3 %collective-permute-start.12 = (bf16[2304,256]{1,0:T(8,128)(2,1)}, bf16[2304,256]{1,0:T(8,128)(2,1)S(1)}, u32[]{:S(2)}, u32[]{:S(2)}) collective-permute-start(bf16[2304,256]{1,0:T(8,128)(2,1)} %get-tuple-element.47), channel_id=1, source_target_pairs={{0,1},{1,2},{2,3},{3,0},{4,5},{5,6},{6,7},{7,4},{8,9},{9,10},{10,1... | collective-permute-start | bytes 3538952 | tf_op jit(solution)/shard_map/ppermute | solution.py:423
  179.5 85.3 %collective-permute-start.14 = (bf16[2304,256]{1,0:T(8,128)(2,1)}, bf16[2304,256]{1,0:T(8,128)(2,1)}, u32[]{:S(2)}, u32[]{:S(2)}) collective-permute-start(bf16[2304,256]{1,0:T(8,128)(2,1)} %get-tuple-element.48), channel_id=1, source_target_pairs={{0,3},{1,0},{2,1},{3,2},{4,7},{5,4},{6,5},{7,6},{8,11},{9,8},{10,9... | collective-permute-start | bytes 3538952 | tf_op jit(solution)/shard_map/ppermute | solution.py:423
  180.6 106.8 %collective-permute-start.13 = (bf16[2304,256]{1,0:T(8,128)(2,1)}, bf16[2304,256]{1,0:T(8,128)(2,1)}, u32[]{:S(2)}, u32[]{:S(2)}) collective-permute-start(bf16[2304,256]{1,0:T(8,128)(2,1)} %get-tuple-element.49), channel_id=1, source_target_pairs={{0,2},{1,3},{2,0},{3,1},{4,6},{5,7},{6,4},{7,5},{8,10},{9,11},{10,... | collective-permute-start | bytes 3538952 | tf_op jit(solution)/shard_map/ppermute | solution.py:423
  191.4 102.7 %copy-start.6 = (s32[8]{0:T(128)S(1)}, s32[8]{0:T(128)}, u32[]{:S(2)}) copy-start(s32[8]{0:T(128)} %get-tuple-element.21) | copy-start | bytes 100
  262.0 2.8 copy-start.3
  290.2 98.8 %collective-permute-start.15 = (bf16[2304,256]{1,0:T(8,128)(2,1)S(1)}, bf16[2304,256]{1,0:T(8,128)(2,1)}, u32[]{:S(2)}, u32[]{:S(2)}) collective-permute-start(bf16[2304,256]{1,0:T(8,128)(2,1)S(1)} %fusion.2), channel_id=1, source_target_pairs={{0,4},{1,5},{2,6},{3,7},{4,0},{5,1},{6,2},{7,3},{8,12},{9,13},{10,... | collective-permute-start | bytes 3538952 | tf_op jit(solution)/shard_map/ppermute | solution.py:448
  298.2 290.1 %all-to-all-start.2 = ((f16[8,2,64,2048]{3,2,1,0:T(8,128)(2,1)}), f16[8,2,64,2048]{3,2,1,0:T(8,128)(2,1)}, u32[]{:S(2)}, u32[]{:S(2)}) async-start(f16[8,2,64,2048]{3,2,1,0:T(8,128)(2,1)} %bitcast.67), calls=%async_computation.2 | async-start | bytes 8388608 | tf_op jit(solution)/shard_map/all_to_all | solution.py:416
  391.6 41.6 %collective-permute-start.18 = (bf16[2304,256]{1,0:T(8,128)(2,1)}, bf16[2304,256]{1,0:T(8,128)(2,1)}, u32[]{:S(2)}, u32[]{:S(2)}) collective-permute-start(bf16[2304,256]{1,0:T(8,128)(2,1)} %add_convert_fusion.rest_0_), channel_id=1, source_target_pairs={{0,3},{1,0},{2,1},{3,2},{4,7},{5,4},{6,5},{7,6},{8,11},{9,8},{10,9... | collective-permute-start | bytes 3538952 | tf_op jit(solution)/shard_map/ppermute | solution.py:423
  399.9 74.1 %collective-permute-start.17 = (bf16[2304,256]{1,0:T(8,128)(2,1)}, bf16[2304,256]{1,0:T(8,128)(2,1)}, u32[]{:S(2)}, u32[]{:S(2)}) collective-permute-start(bf16[2304,256]{1,0:T(8,128)(2,1)} %add_convert_fusion.rest_0_), channel_id=1, source_target_pairs={{0,2},{1,3},{2,0},{3,1},{4,6},{5,7},{6,4},{7,5},{8,10},{9,11},{10,... | collective-permute-start | bytes 3538952 | tf_op jit(solution)/shard_map/ppermute | solution.py:423
  402.5 71.5 %collective-permute-start.16 = (bf16[2304,256]{1,0:T(8,128)(2,1)}, bf16[2304,256]{1,0:T(8,128)(2,1)}, u32[]{:S(2)}, u32[]{:S(2)}) collective-permute-start(bf16[2304,256]{1,0:T(8,128)(2,1)} %add_convert_fusion.rest_0_), channel_id=1, source_target_pairs={{0,1},{1,2},{2,3},{3,0},{4,5},{5,6},{6,7},{7,4},{8,9},{9,10},{10,1... | collective-permute-start | bytes 3538952 | tf_op jit(solution)/shard_map/ppermute | solution.py:423
  405.2 146.4 %copy-start.4 = (f32[6]{0:T(128)}, f32[6]{0:T(128)S(1)}, u32[]{:S(2)}) copy-start(f32[6]{0:T(128)S(1)} %get-tuple-element.44.keep_ref) | copy-start | bytes 76
  618.6 4.2 copy-start.2
  620.7 13.0 %collective-permute-start.2 = (f16[1,64,2048]{2,1,0:T(8,128)(2,1)S(1)}, f16[1,64,2048]{2,1,0:T(8,128)(2,1)S(1)}, u32[]{:S(2)}, u32[]{:S(2)}) collective-permute-start(f16[1,64,2048]{2,1,0:T(8,128)(2,1)S(1)} %get-tuple-element.59), channel_id=1, source_target_pairs={{0,3},{1,0},{2,1},{3,2},{4,7},{5,4},{6,5},{7,6},{8,11},{9,8},{10,9... | collective-permute-start | bytes 786440 | tf_op jit(solution)/shard_map/ppermute | solution.py:423
  620.8 14.4 %collective-permute-start.1 = (f16[1,64,2048]{2,1,0:T(8,128)(2,1)S(1)}, f16[1,64,2048]{2,1,0:T(8,128)(2,1)S(1)}, u32[]{:S(2)}, u32[]{:S(2)}) collective-permute-start(f16[1,64,2048]{2,1,0:T(8,128)(2,1)S(1)} %get-tuple-element.60), channel_id=1, source_target_pairs={{0,2},{1,3},{2,0},{3,1},{4,6},{5,7},{6,4},{7,5},{8,10},{9,11},{10,... | collective-permute-start | bytes 786440 | tf_op jit(solution)/shard_map/ppermute | solution.py:423
  620.9 18.7 %collective-permute-start = (f16[1,64,2048]{2,1,0:T(8,128)(2,1)S(1)}, f16[1,64,2048]{2,1,0:T(8,128)(2,1)S(1)}, u32[]{:S(2)}, u32[]{:S(2)}) collective-permute-start(f16[1,64,2048]{2,1,0:T(8,128)(2,1)S(1)} %get-tuple-element.61), channel_id=1, source_target_pairs={{0,1},{1,2},{2,3},{3,0},{4,5},{5,6},{6,7},{7,4},{8,9},{9,10},{10,1... | collective-permute-start | bytes 786440 | tf_op jit(solution)/shard_map/ppermute | solution.py:423
  622.8 3.4 copy-start
  623.2 21.7 %collective-permute-start.8 = (f16[1,64,2048]{2,1,0:T(8,128)(2,1)S(1)}, f16[1,64,2048]{2,1,0:T(8,128)(2,1)S(1)}, u32[]{:S(2)}, u32[]{:S(2)}) collective-permute-start(f16[1,64,2048]{2,1,0:T(8,128)(2,1)S(1)} %get-tuple-element.56), channel_id=1, source_target_pairs={{0,3},{1,0},{2,1},{3,2},{4,7},{5,4},{6,5},{7,6},{8,11},{9,8},{10,9... | collective-permute-start | bytes 786440 | tf_op jit(solution)/shard_map/ppermute | solution.py:423
  624.7 21.6 %collective-permute-start.7 = (f16[1,64,2048]{2,1,0:T(8,128)(2,1)S(1)}, f16[1,64,2048]{2,1,0:T(8,128)(2,1)S(1)}, u32[]{:S(2)}, u32[]{:S(2)}) collective-permute-start(f16[1,64,2048]{2,1,0:T(8,128)(2,1)S(1)} %get-tuple-element.57), channel_id=1, source_target_pairs={{0,2},{1,3},{2,0},{3,1},{4,6},{5,7},{6,4},{7,5},{8,10},{9,11},{10,... | collective-permute-start | bytes 786440 | tf_op jit(solution)/shard_map/ppermute | solution.py:423
  626.2 2.2 copy-start.1
  633.7 17.7 %collective-permute-start.6 = (f16[1,64,2048]{2,1,0:T(8,128)(2,1)S(1)}, f16[1,64,2048]{2,1,0:T(8,128)(2,1)S(1)}, u32[]{:S(2)}, u32[]{:S(2)}) collective-permute-start(f16[1,64,2048]{2,1,0:T(8,128)(2,1)S(1)} %get-tuple-element.58), channel_id=1, source_target_pairs={{0,1},{1,2},{2,3},{3,0},{4,5},{5,6},{6,7},{7,4},{8,9},{9,10},{10,1... | collective-permute-start | bytes 786440 | tf_op jit(solution)/shard_map/ppermute | solution.py:423
  635.2 32.2 %collective-permute-start.5 = (f16[2,64,2048]{2,1,0:T(8,128)(2,1)S(1)}, f16[2,64,2048]{2,1,0:T(8,128)(2,1)S(1)}, u32[]{:S(2)}, u32[]{:S(2)}) collective-permute-start(f16[2,64,2048]{2,1,0:T(8,128)(2,1)S(1)} %get-tuple-element.53), channel_id=1, source_target_pairs={{0,3},{1,0},{2,1},{3,2},{4,7},{5,4},{6,5},{7,6},{8,11},{9,8},{10,9... | collective-permute-start | bytes 1572872 | tf_op jit(solution)/shard_map/ppermute | solution.py:423
  639.5 57.7 %collective-permute-start.4 = (f16[2,64,2048]{2,1,0:T(8,128)(2,1)S(1)}, f16[2,64,2048]{2,1,0:T(8,128)(2,1)S(1)}, u32[]{:S(2)}, u32[]{:S(2)}) collective-permute-start(f16[2,64,2048]{2,1,0:T(8,128)(2,1)S(1)} %get-tuple-element.54), channel_id=1, source_target_pairs={{0,2},{1,3},{2,0},{3,1},{4,6},{5,7},{6,4},{7,5},{8,10},{9,11},{10,... | collective-permute-start | bytes 1572872 | tf_op jit(solution)/shard_map/ppermute | solution.py:423
  644.9 53.5 %collective-permute-start.3 = (f16[2,64,2048]{2,1,0:T(8,128)(2,1)S(1)}, f16[2,64,2048]{2,1,0:T(8,128)(2,1)S(1)}, u32[]{:S(2)}, u32[]{:S(2)}) collective-permute-start(f16[2,64,2048]{2,1,0:T(8,128)(2,1)S(1)} %get-tuple-element.55), channel_id=1, source_target_pairs={{0,1},{1,2},{2,3},{3,0},{4,5},{5,6},{6,7},{7,4},{8,9},{9,10},{10,1... | collective-permute-start | bytes 1572872 | tf_op jit(solution)/shard_map/ppermute | solution.py:423
  646.3 33.1 %collective-permute-start.11 = (f16[2,64,2048]{2,1,0:T(8,128)(2,1)S(1)}, f16[2,64,2048]{2,1,0:T(8,128)(2,1)S(1)}, u32[]{:S(2)}, u32[]{:S(2)}) collective-permute-start(f16[2,64,2048]{2,1,0:T(8,128)(2,1)S(1)} %get-tuple-element.50), channel_id=1, source_target_pairs={{0,3},{1,0},{2,1},{3,2},{4,7},{5,4},{6,5},{7,6},{8,11},{9,8},{10,9... | collective-permute-start | bytes 1572872 | tf_op jit(solution)/shard_map/ppermute | solution.py:423
  651.4 34.0 %collective-permute-start.10 = (f16[2,64,2048]{2,1,0:T(8,128)(2,1)S(1)}, f16[2,64,2048]{2,1,0:T(8,128)(2,1)S(1)}, u32[]{:S(2)}, u32[]{:S(2)}) collective-permute-start(f16[2,64,2048]{2,1,0:T(8,128)(2,1)S(1)} %get-tuple-element.51), channel_id=1, source_target_pairs={{0,2},{1,3},{2,0},{3,1},{4,6},{5,7},{6,4},{7,5},{8,10},{9,11},{10,... | collective-permute-start | bytes 1572872 | tf_op jit(solution)/shard_map/ppermute | solution.py:423
  667.3 21.4 %collective-permute-start.9 = (f16[2,64,2048]{2,1,0:T(8,128)(2,1)S(1)}, f16[2,64,2048]{2,1,0:T(8,128)(2,1)S(1)}, u32[]{:S(2)}, u32[]{:S(2)}) collective-permute-start(f16[2,64,2048]{2,1,0:T(8,128)(2,1)S(1)} %get-tuple-element.52), channel_id=1, source_target_pairs={{0,1},{1,2},{2,3},{3,0},{4,5},{5,6},{6,7},{7,4},{8,9},{9,10},{10,1... | collective-permute-start | bytes 1572872 | tf_op jit(solution)/shard_map/ppermute | solution.py:423

commit v4 on v3

--- a/solution.py
+++ b/solution.py
@@ -116,6 +116,33 @@
         name="merge",
         cost_estimate=cost(5 * momentum.size, momentum.size * 12),
     )(momentum, grad)
+
+
+def pick_kernel(table_ref, momentum_ref, grad_ref, scaled_ref):
+    merged = BETA * momentum_ref[0] + grad_ref[0]
+    top = jnp.maximum(jnp.max(jnp.abs(merged), keepdims=True), SMALLEST)
+    scaled_ref[0, 0] = merged * (F16_TOP / top)
+
+
+def pick_first(table, momentum, grad, members, most, chunk):
+    rows, width = momentum.shape[1:]
+    source = pl.BlockSpec(
+        (1, rows, width), lambda i, table: (table[i // chunk * most + i % chunk], 0, 0)
+    )
+    return pl.pallas_call(
+        pick_kernel,
+        grid_spec=pltpu.PrefetchScalarGridSpec(
+            num_scalar_prefetch=1,
+            grid=(members * chunk,),
+            in_specs=[source, source],
+            out_specs=pl.BlockSpec(
+                (1, 1, rows, width), lambda i, table: (i // chunk, i % chunk, 0, 0)
+            ),
+        ),
+        out_shape=jax.ShapeDtypeStruct((members, chunk, rows, width), F32),
+        name="pick_first",
+        cost_estimate=cost(2e9, members * chunk * rows * width * 12),
+    )(table, momentum, grad)
 
 
 def solve_kernel(
@@ -243,10 +270,11 @@
 
 def wide_gram_kernel(momentum_ref, grad_ref, merged_ref, packed_ref, sum_ref, low):
     i = pl.program_id(0)
+    step = 2 * BLOCK
     merged = BETA * momentum_ref[...] + grad_ref[...]
     merged_ref[...] = merged
     rounded = merged.astype(BF16)
-    low[pl.ds(pl.multiple_of(i * BLOCK, BLOCK), BLOCK), :] = rounded
+    low[pl.ds(pl.multiple_of(i * step, step), step), :] = rounded
 
     @pl.when(i == 0)
     def _():
@@ -254,27 +282,34 @@
 
     squares = jnp.square(rounded.astype(F32))
     sum_ref[...] += jnp.sum(squares, axis=(0, 1), keepdims=True)
-    start = i * (i + 1) // 2
-
-    def columns(j, carry):
-        other = low[pl.ds(pl.multiple_of(j * (2 * BLOCK), 2 * BLOCK), 2 * BLOCK), :]
+
+    def columns(turn, carry):
+        j = i - turn
+        other = low[pl.ds(pl.multiple_of(j * step, step), step), :]
         product = dot_nt(rounded, other).astype(BF16)
-        for k in range(2):
-            place = pl.multiple_of((start + 2 * j + k) * BLOCK, BLOCK)
-            packed_ref[pl.ds(place, BLOCK), :] = product[:, k * BLOCK:(k + 1) * BLOCK]
+        for a in range(2):
+            row = 2 * i + a
+            for b in range(2):
+                place = pl.multiple_of((row * (row + 1) // 2 + 2 * j + b) * BLOCK, BLOCK)
+
+                @pl.when(jnp.logical_or(turn > 0, b <= a))
+                def _():
+                    packed_ref[pl.ds(place, BLOCK), :] = product[
+                        a * BLOCK:(a + 1) * BLOCK, b * BLOCK:(b + 1) * BLOCK
+                    ]
         return carry
 
-    lax.fori_loop(0, (i + 2) // 2, columns, 0)
+    lax.fori_loop(0, i + 1, columns, 0)
 
 
 def wide_gram(momentum, grad):
     height, width = momentum.shape
     number = height // BLOCK
     packed = number * (number + 1) // 2 * BLOCK
-    row_spec = pl.BlockSpec((BLOCK, width), lambda i: (i, 0))
+    row_spec = pl.BlockSpec((2 * BLOCK, width), lambda i: (i, 0))
     return pl.pallas_call(
         wide_gram_kernel,
-        grid=(number,),
+        grid=(number // 2,),
         out_shape=(
             jax.ShapeDtypeStruct((height, width), F32),
             jax.ShapeDtypeStruct((packed, BLOCK), BF16),
@@ -434,8 +469,12 @@
     notes = across(notes)[:, 0]
     coded = lax.optimization_barrier(scaled.astype(jnp.float16))
     arrived = []
-    for start, chunk in zip(starts, sizes):
-        picked = coded[slots[:, start:start + chunk].reshape(-1)]
+    for index, (start, chunk) in enumerate(zip(starts, sizes)):
+        if index == 0:
+            picked = pick_first(table, expert_momentum, expert_grad, members, most, chunk)
+            picked = picked.astype(jnp.float16)
+        else:
+            picked = coded[slots[:, start:start + chunk].reshape(-1)]
         arrived.append(across(picked.reshape(members, chunk, rows, width)))
 
     packed_rows = packed.shape[0] // half_members

time: 708 us -> 706 us (level)
  waiting for transfers between devices: 365 us -> 350 us
  Pallas kernels: 170 us -> 183 us
  local copies, waits for them, and re-layouts: 40.7 us -> 33.5 us
    all_to_all x5, waiting for transfers between devices: 82.8 us -> 68.2 us  [across(): lax.all_to_all(value, 'fsdp', split_axis=0, concat_axis=0, tiled=True)]
    pallas_call x1 -> x2, Pallas kernels: 14.3 us -> 27.4 us  [the longest x1 15.6 us: pick_first(): pl.pallas_call(pick_kernel, grid_spec=pltpu.PrefetchScalarGridSpec(num_sc...]
    gather x4 -> x3, local copies, waits for them, and re-layouts: 24.7 us -> 17.8 us  [on_device(): picked = coded[slots[:, start:start + chunk].reshape(-1)]]
  transfers between devices with their start and end apart: 24 -> 24, of which waited for: 15 -> 15; matrix products, arithmetic and copies ran while one was open for 12% -> 12% of each run, Pallas kernels for 16% -> 18%
where the time goes in v4:
time: 706 us; the launch traced here: 704 us
  waiting for transfers between devices  350 us (50%)
  Pallas kernels  183 us (26%)
  starting transfers between devices  65.4 us (9%)
  other arithmetic  63.8 us (9%)
  local copies, waits for them, and re-layouts  33.5 us (5%)
  between operations  8.13 us (1%)
    ppermute x18, waiting for transfers between devices, shifted(): return lax.ppermute(value, 'fsdp', pairs)  203 us
    ppermute x1, waiting for transfers between devices, on_device(): other = lax.ppermute(part, 'fsdp', mirror)  79 us
    pallas_call x1, Pallas kernels, wide_solve(): pl.pallas_call(wide_solve_kernel, out_shape=jax.ShapeDtypeStruct((height,...  77.5 us
    all_to_all x5, waiting for transfers between devices, across(): lax.all_to_all(value, 'fsdp', split_axis=0, concat_axis=0, tiled=True)  68.2 us
    pallas_call x4, Pallas kernels, solve(): pl.pallas_call(functools.partial(solve_kernel, members, half_members, fir...  47.6 us
    all_to_all x5, starting transfers between devices, across(): lax.all_to_all(value, 'fsdp', split_axis=0, concat_axis=0, tiled=True)  34.2 us
    ppermute x18, starting transfers between devices, shifted(): return lax.ppermute(value, 'fsdp', pairs)  28.6 us
    convert_element_type x4, other arithmetic, on_device(): piece.astype(F32)  19.5 us
  transfers between devices with their start and end apart: 24, of which 15 were waited for; matrix products, arithmetic and copies ran while one was open for 12% of the time, Pallas kernels for 18%

profile of v4, /device:TPU:0, one launch (start us, length us, event | category | flops | bytes accessed | tf_op | source)
XLA Modules:
  0.0 704.4 jit_solution(7295302639228147573)
XLA Ops:
  0.6 11.7 %wide_gram.1 = (f32[2048,512]{1,0:T(8,128)}, bf16[9216,256]{1,0:T(8,128)(2,1)}, f32[8,128]{1,0:T(8,128)}) custom-call(f32[2048,512]{1,0:T(8,128)} %bitcast.70, f32[2048,512]{1,0:T(8,128)} %bitcast.71), custom_call_target="tpu_custom_call" | custom-call | flops 2415919104 | bytes 17301504 | tf_op jit(solution)/shard_map/wide_gram/pallas_call | solution.py:310
  13.6 13.9 %merge.1 = (f32[24,64,2048]{2,1,0:T(8,128)}, f32[24,8,128]{2,1,0:T(8,128)}) custom-call(f32[24,64,2048]{2,1,0:T(8,128)} %momentum_ref.3, f32[24,64,2048]{2,1,0:T(8,128)} %grad_ref.3), custom_call_target="tpu_custom_call" | custom-call | flops 15728640 | bytes 37748736 | tf_op jit(solution)/shard_map/merge/pallas_call | solution.py:107
  30.0 7.3 %all-to-all-start = ((f32[8,1,128]{2,1,0:T(1,128)}), f32[8,1,128]{2,1,0:T(1,128)S(1)}, u32[]{:S(2)}, u32[]{:S(2)}) async-start(f32[8,1,128]{2,1,0:T(1,128)} %broadcast_in_dim.80), calls=%async_computation | async-start | bytes 8192 | tf_op jit(solution)/shard_map/all_to_all | solution.py:451
  37.3 2.5 route.1
  40.7 8.4 %convert_element_type.183 = f16[24,64,2048]{2,1,0:T(8,128)(2,1)} convert(f32[24,64,2048]{2,1,0:T(8,128)} %get-tuple-element.22) | non-fusion elementwise | flops 3145728 | bytes 18874368 | tf_op jit(solution)/shard_map/convert_element_type | solution.py:470
  49.1 5.5 gather_fusion.3
  54.6 6.0 all-to-all-start.3
  60.6 5.5 gather_fusion.1
  66.1 42.2 %all-to-all-done.3 = f16[8,1,64,2048]{3,2,1,0:T(8,128)(2,1)S(1)} async-done(((f16[8,1,64,2048]{3,2,1,0:T(8,128)(2,1)}), f16[8,1,64,2048]{3,2,1,0:T(8,128)(2,1)S(1)}, u32[]{:S(2)}, u32[]{:S(2)}) %all-to-all-start.3) | async-done | bytes 2097184 | tf_op jit(solution)/shard_map/all_to_all | solution.py:451
  108.2 4.4 all-to-all-start.1
  112.6 15.6 %pick_first.1 = f32[8,2,64,2048]{3,2,1,0:T(8,128)} custom-call(s32[48]{0:T(128)} %get-tuple-element.18.table_ref, f32[24,64,2048]{2,1,0:T(8,128)} %momentum_ref.3, f32[24,64,2048]{2,1,0:T(8,128)} %grad_ref.3), custom_call_target="tpu_custom_call" | custom-call | flops 2000000000 | bytes 25165824 | tf_op jit(solution)/shard_map/pick_first/pallas_call | solution.py:132
  128.2 6.1 convert_element_type.187
  134.3 26.1 %all-to-all-done.1 = f16[8,1,64,2048]{3,2,1,0:T(8,128)(2,1)} async-done(((f16[8,1,64,2048]{3,2,1,0:T(8,128)(2,1)}), f16[8,1,64,2048]{3,2,1,0:T(8,128)(2,1)}, u32[]{:S(2)}, u32[]{:S(2)}) %all-to-all-start.1) | async-done | bytes 2097184 | tf_op jit(solution)/shard_map/all_to_all | solution.py:451
  160.4 4.6 all-to-all-start.4
  171.3 3.9 dynamic-slice_bitcast_fusion.2
  175.2 1.9 collective-permute-start.12
  178.1 1.9 collective-permute-start.13
  182.1 6.9 gather_fusion.2
  189.0 70.3 %collective-permute-done.12 = bf16[2304,256]{1,0:T(8,128)(2,1)S(1)} collective-permute-done((bf16[2304,256]{1,0:T(8,128)(2,1)}, bf16[2304,256]{1,0:T(8,128)(2,1)S(1)}, u32[]{:S(2)}, u32[]{:S(2)}) %collective-permute-start.12) | collective-permute-done | bytes 1179680 | tf_op jit(solution)/shard_map/ppermute | solution.py:458
  259.3 2.8 collective-permute-done.14
  262.2 22.6 %collective-permute-done.13 = bf16[2304,256]{1,0:T(8,128)(2,1)} collective-permute-done((bf16[2304,256]{1,0:T(8,128)(2,1)}, bf16[2304,256]{1,0:T(8,128)(2,1)}, u32[]{:S(2)}, u32[]{:S(2)}) %collective-permute-start.13) | collective-permute-done | bytes 1179680 | tf_op jit(solution)/shard_map/ppermute | solution.py:458
  284.7 2.9 fusion.2
  287.6 2.6 collective-permute-start.15
  295.6 11.9 %all-to-all-start.2 = ((f16[8,2,64,2048]{3,2,1,0:T(8,128)(2,1)}), f16[8,2,64,2048]{3,2,1,0:T(8,128)(2,1)}, u32[]{:S(2)}, u32[]{:S(2)}) async-start(f16[8,2,64,2048]{3,2,1,0:T(8,128)(2,1)} %bitcast.63), calls=%async_computation.2 | async-start | bytes 8388608 | tf_op jit(solution)/shard_map/all_to_all | solution.py:451
  307.5 79.0 %collective-permute-done.15 = bf16[2304,256]{1,0:T(8,128)(2,1)} collective-permute-done((bf16[2304,256]{1,0:T(8,128)(2,1)S(1)}, bf16[2304,256]{1,0:T(8,128)(2,1)}, u32[]{:S(2)}, u32[]{:S(2)}) %collective-permute-start.15) | collective-permute-done | bytes 1179680 | tf_op jit(solution)/shard_map/ppermute | solution.py:487
  386.5 2.6 add_convert_fusion.rest_0_
  389.0 8.2 %collective-permute-start.18 = (bf16[2304,256]{1,0:T(8,128)(2,1)}, bf16[2304,256]{1,0:T(8,128)(2,1)}, u32[]{:S(2)}, u32[]{:S(2)}) collective-permute-start(bf16[2304,256]{1,0:T(8,128)(2,1)} %add_convert_fusion.rest_0_), channel_id=1, source_target_pairs={{0,3},{1,0},{2,1},{3,2},{4,7},{5,4},{6,5},{7,6},{8,11},{9,8},{10,9... | collective-permute-start | bytes 3538952 | tf_op jit(solution)/shard_map/ppermute | solution.py:458
  397.3 2.6 collective-permute-start.17
  402.4 1.2 fusion.16
  403.6 26.9 %collective-permute-done.18.rest_3_ = bf16[2304,256]{1,0:T(8,128)(2,1)} collective-permute-done((bf16[2304,256]{1,0:T(8,128)(2,1)}, bf16[2304,256]{1,0:T(8,128)(2,1)}, u32[]{:S(2)}, u32[]{:S(2)}) %collective-permute-start.18) | collective-permute-done | bytes 1179680 | tf_op jit(solution)/shard_map/ppermute | solution.py:458
  430.5 40.8 %collective-permute-done.17.rest_2_ = bf16[2304,256]{1,0:T(8,128)(2,1)} collective-permute-done((bf16[2304,256]{1,0:T(8,128)(2,1)}, bf16[2304,256]{1,0:T(8,128)(2,1)}, u32[]{:S(2)}, u32[]{:S(2)}) %collective-permute-start.17) | collective-permute-done | bytes 1179680 | tf_op jit(solution)/shard_map/ppermute | solution.py:458
  471.3 77.5 %wide_solve.1 = f32[2048,512]{1,0:T(8,128)} custom-call(f32[3]{0:T(128)} %pad_maximum_fusion.coef_ref, s32[4]{0:T(128)} %and_select_fusion.turn_ref, f32[36]{0:T(128)} %constant.109.clone.table_ref, f32[2048,512]{1,0:T(8,128)} %get-tuple-element.30.merged_ref, bf16[2304,256]{1,0:T(8,128)(2,1)} %add_convert_fusion.rest_0_, ...), custom_call_target="tpu_custom_call" | custom-call | flops 51539607552 | bytes 8388608 | tf_op jit(solution)/shard_map/wide_solve/pallas_call | solution.py:415
  548.9 4.0 convert_element_type.184.data_ref
  552.8 2.4 convert_element_type.186.data_ref
  555.2 6.6 convert_element_type.188.data_ref
  561.8 14.3 %shard_map.94 = (f32[6,512,2048]{2,1,0:T(8,128)}, f32[4,2,64,2048]{3,2,1,0:T(8,128)}) custom-call(s32[4]{0:T(128)} %add_multiply_fusion.row_ref, f32[48]{0:T(128)} %div.46.scale_ref, f32[6]{0:T(128)} %copy-done.4, f32[6]{0:T(128)} %get-tuple-element.76.factor_ref, f32[6]{0:T(128)} %get-tuple-element.75.ratio_ref, ...), custom_call_target="tpu_custom_call" | custom-call | flops 6979321856 | bytes 25165824 | tf_op jit(solution)/shard_map/pallas_call | solution.py:207
  576.1 9.5 %shard_map.95 = (f32[6,512,2048]{2,1,0:T(8,128)}, f32[4,1,64,2048]{3,2,1,0:T(8,128)}) custom-call(s32[4]{0:T(128)} %add_multiply_fusion.row_ref, f32[48]{0:T(128)} %div.46.scale_ref, f32[6]{0:T(128)} %copy-done.4, f32[6]{0:T(128)} %get-tuple-element.76.factor_ref, f32[6]{0:T(128)} %get-tuple-element.75.ratio_ref, ...), custom_call_target="tpu_custom_call", output_to_operand_aliasing={{0}: (6, {})} | custom-call | flops 3489660928 | bytes 12582912 | tf_op jit(solution)/shard_map/pallas_call | solution.py:207
  585.6 6.6 convert_element_type.185.data_ref
  592.2 14.3 %shard_map.96 = (f32[6,512,2048]{2,1,0:T(8,128)}, f32[4,2,64,2048]{3,2,1,0:T(8,128)}) custom-call(s32[4]{0:T(128)} %add_multiply_fusion.row_ref, f32[48]{0:T(128)} %div.46.scale_ref, f32[6]{0:T(128)} %copy-done.4, f32[6]{0:T(128)} %get-tuple-element.76.factor_ref, f32[6]{0:T(128)} %get-tuple-element.75.ratio_ref, ...), custom_call_target="tpu_custom_call", output_to_operand_aliasing={{0}: (6, {})} | custom-call | flops 6979321856 | bytes 25165824 | tf_op jit(solution)/shard_map/pallas_call | solution.py:207
  606.5 9.5 %shard_map.97 = (f32[6,512,2048]{2,1,0:T(8,128)}, f32[4,1,64,2048]{3,2,1,0:T(8,128)}) custom-call(s32[4]{0:T(128)} %add_multiply_fusion.row_ref, f32[48]{0:T(128)} %div.46.scale_ref, f32[6]{0:T(128)} %copy-done.4, f32[6]{0:T(128)} %get-tuple-element.76.factor_ref, f32[6]{0:T(128)} %get-tuple-element.75.ratio_ref, ...), custom_call_target="tpu_custom_call", output_to_operand_aliasing={{0}: (6, {})} | custom-call | flops 3489660928 | bytes 12582912 | tf_op jit(solution)/shard_map/pallas_call | solution.py:207
  616.0 1.9 convert.21
  618.2 1.9 collective-permute-start
  620.5 1.5 collective-permute-start.8
  622.0 1.5 collective-permute-start.7
  624.2 1.5 copy-done.1
  626.3 4.7 collective-permute-done.2
  631.0 1.4 convert_multiply_fusion.9.rest_2_
  632.5 2.9 collective-permute-start.5
  635.4 1.4 convert_multiply_fusion.10.rest_1_
  636.8 1.5 convert_multiply_fusion.11.rest_0_
  638.2 4.0 collective-permute-done.8
  642.2 1.5 convert_multiply_fusion.6.rest_2_
  643.7 2.9 collective-permute-start.11
  646.7 1.4 convert_multiply_fusion.7.rest_1_
  648.7 2.0 collective-permute-start.10
  650.7 1.5 convert_multiply_fusion.8.rest_0_
  652.3 12.4 %collective-permute-done.5 = f16[2,64,2048]{2,1,0:T(8,128)(2,1)S(1)} collective-permute-done((f16[2,64,2048]{2,1,0:T(8,128)(2,1)S(1)}, f16[2,64,2048]{2,1,0:T(8,128)(2,1)S(1)}, u32[]{:S(2)}, u32[]{:S(2)}) %collective-permute-start.5) | collective-permute-done | bytes 524320 | tf_op jit(solution)/shard_map/ppermute | solution.py:458
  665.9 10.9 %collective-permute-done.11 = f16[2,64,2048]{2,1,0:T(8,128)(2,1)S(1)} collective-permute-done((f16[2,64,2048]{2,1,0:T(8,128)(2,1)S(1)}, f16[2,64,2048]{2,1,0:T(8,128)(2,1)S(1)}, u32[]{:S(2)}, u32[]{:S(2)}) %collective-permute-start.11) | collective-permute-done | bytes 524320 | tf_op jit(solution)/shard_map/ppermute | solution.py:458
  677.9 4.8 collective-permute-done.10
  683.9 2.2 collective-permute-done.9
  687.3 4.2 home.4.rest_3_
  691.5 3.1 home.5.rest_3_
  696.9 4.2 home.6.rest_3_
  701.2 3.1 home.7
  (83 shorter events, 24.5 us)
Async XLA Ops:
  30.0 24.6 %all-to-all-start = ((f32[8,1,128]{2,1,0:T(1,128)}), f32[8,1,128]{2,1,0:T(1,128)S(1)}, u32[]{:S(2)}, u32[]{:S(2)}) async-start(f32[8,1,128]{2,1,0:T(1,128)} %broadcast_in_dim.80), calls=%async_computation | async-start | bytes 8192 | tf_op jit(solution)/shard_map/all_to_all | solution.py:451
  54.6 53.7 %all-to-all-start.3 = ((f16[8,1,64,2048]{3,2,1,0:T(8,128)(2,1)}), f16[8,1,64,2048]{3,2,1,0:T(8,128)(2,1)S(1)}, u32[]{:S(2)}, u32[]{:S(2)}) async-start(f16[8,1,64,2048]{3,2,1,0:T(8,128)(2,1)} %bitcast.65), calls=%async_computation.3 | async-start | bytes 4194304 | tf_op jit(solution)/shard_map/all_to_all | solution.py:451
  108.2 52.2 %all-to-all-start.1 = ((f16[8,1,64,2048]{3,2,1,0:T(8,128)(2,1)}), f16[8,1,64,2048]{3,2,1,0:T(8,128)(2,1)}, u32[]{:S(2)}, u32[]{:S(2)}) async-start(f16[8,1,64,2048]{3,2,1,0:T(8,128)(2,1)} %bitcast.64), calls=%async_computation.1 | async-start | bytes 4194304 | tf_op jit(solution)/shard_map/all_to_all | solution.py:451
  160.4 135.2 %all-to-all-start.4 = ((f16[8,2,64,2048]{3,2,1,0:T(8,128)(2,1)}), f16[8,2,64,2048]{3,2,1,0:T(8,128)(2,1)}, u32[]{:S(2)}, u32[]{:S(2)}) async-start(f16[8,2,64,2048]{3,2,1,0:T(8,128)(2,1)} %convert_element_type.187), calls=%async_computation.4 | async-start | bytes 8388608 | tf_op jit(solution)/shard_map/all_to_all | solution.py:451
  171.3 8.8 %copy-start.5 = (s32[96]{0:T(128)S(1)}, s32[96]{0:T(128)}, u32[]{:S(2)}) copy-start(s32[96]{0:T(128)} %param.12) | copy-start | bytes 1156
  175.2 84.1 %collective-permute-start.12 = (bf16[2304,256]{1,0:T(8,128)(2,1)}, bf16[2304,256]{1,0:T(8,128)(2,1)S(1)}, u32[]{:S(2)}, u32[]{:S(2)}) collective-permute-start(bf16[2304,256]{1,0:T(8,128)(2,1)} %get-tuple-element.47), channel_id=1, source_target_pairs={{0,1},{1,2},{2,3},{3,0},{4,5},{5,6},{6,7},{7,4},{8,9},{9,10},{10,1... | collective-permute-start | bytes 3538952 | tf_op jit(solution)/shard_map/ppermute | solution.py:458
  177.1 85.1 %collective-permute-start.14 = (bf16[2304,256]{1,0:T(8,128)(2,1)}, bf16[2304,256]{1,0:T(8,128)(2,1)}, u32[]{:S(2)}, u32[]{:S(2)}) collective-permute-start(bf16[2304,256]{1,0:T(8,128)(2,1)} %get-tuple-element.48), channel_id=1, source_target_pairs={{0,3},{1,0},{2,1},{3,2},{4,7},{5,4},{6,5},{7,6},{8,11},{9,8},{10,9... | collective-permute-start | bytes 3538952 | tf_op jit(solution)/shard_map/ppermute | solution.py:458
  178.1 106.6 %collective-permute-start.13 = (bf16[2304,256]{1,0:T(8,128)(2,1)}, bf16[2304,256]{1,0:T(8,128)(2,1)}, u32[]{:S(2)}, u32[]{:S(2)}) collective-permute-start(bf16[2304,256]{1,0:T(8,128)(2,1)} %get-tuple-element.49), channel_id=1, source_target_pairs={{0,2},{1,3},{2,0},{3,1},{4,6},{5,7},{6,4},{7,5},{8,10},{9,11},{10,... | collective-permute-start | bytes 3538952 | tf_op jit(solution)/shard_map/ppermute | solution.py:458
  189.0 102.5 %copy-start.6 = (s32[8]{0:T(128)S(1)}, s32[8]{0:T(128)}, u32[]{:S(2)}) copy-start(s32[8]{0:T(128)} %get-tuple-element.21) | copy-start | bytes 100
  259.3 2.8 copy-start.3
  287.6 98.8 %collective-permute-start.15 = (bf16[2304,256]{1,0:T(8,128)(2,1)S(1)}, bf16[2304,256]{1,0:T(8,128)(2,1)}, u32[]{:S(2)}, u32[]{:S(2)}) collective-permute-start(bf16[2304,256]{1,0:T(8,128)(2,1)S(1)} %fusion.2), channel_id=1, source_target_pairs={{0,4},{1,5},{2,6},{3,7},{4,0},{5,1},{6,2},{7,3},{8,12},{9,13},{10,... | collective-permute-start | bytes 3538952 | tf_op jit(solution)/shard_map/ppermute | solution.py:487
  295.6 290.0 %all-to-all-start.2 = ((f16[8,2,64,2048]{3,2,1,0:T(8,128)(2,1)}), f16[8,2,64,2048]{3,2,1,0:T(8,128)(2,1)}, u32[]{:S(2)}, u32[]{:S(2)}) async-start(f16[8,2,64,2048]{3,2,1,0:T(8,128)(2,1)} %bitcast.63), calls=%async_computation.2 | async-start | bytes 8388608 | tf_op jit(solution)/shard_map/all_to_all | solution.py:451
  389.0 41.5 %collective-permute-start.18 = (bf16[2304,256]{1,0:T(8,128)(2,1)}, bf16[2304,256]{1,0:T(8,128)(2,1)}, u32[]{:S(2)}, u32[]{:S(2)}) collective-permute-start(bf16[2304,256]{1,0:T(8,128)(2,1)} %add_convert_fusion.rest_0_), channel_id=1, source_target_pairs={{0,3},{1,0},{2,1},{3,2},{4,7},{5,4},{6,5},{7,6},{8,11},{9,8},{10,9... | collective-permute-start | bytes 3538952 | tf_op jit(solution)/shard_map/ppermute | solution.py:458
  397.3 74.1 %collective-permute-start.17 = (bf16[2304,256]{1,0:T(8,128)(2,1)}, bf16[2304,256]{1,0:T(8,128)(2,1)}, u32[]{:S(2)}, u32[]{:S(2)}) collective-permute-start(bf16[2304,256]{1,0:T(8,128)(2,1)} %add_convert_fusion.rest_0_), channel_id=1, source_target_pairs={{0,2},{1,3},{2,0},{3,1},{4,6},{5,7},{6,4},{7,5},{8,10},{9,11},{10,... | collective-permute-start | bytes 3538952 | tf_op jit(solution)/shard_map/ppermute | solution.py:458
  399.8 71.5 %collective-permute-start.16 = (bf16[2304,256]{1,0:T(8,128)(2,1)}, bf16[2304,256]{1,0:T(8,128)(2,1)}, u32[]{:S(2)}, u32[]{:S(2)}) collective-permute-start(bf16[2304,256]{1,0:T(8,128)(2,1)} %add_convert_fusion.rest_0_), channel_id=1, source_target_pairs={{0,1},{1,2},{2,3},{3,0},{4,5},{5,6},{6,7},{7,4},{8,9},{9,10},{10,1... | collective-permute-start | bytes 3538952 | tf_op jit(solution)/shard_map/ppermute | solution.py:458
  402.4 146.5 %copy-start.4 = (f32[6]{0:T(128)}, f32[6]{0:T(128)S(1)}, u32[]{:S(2)}) copy-start(f32[6]{0:T(128)S(1)} %get-tuple-element.44.keep_ref) | copy-start | bytes 76
  616.0 4.2 copy-start.2
  618.0 13.0 %collective-permute-start.2 = (f16[1,64,2048]{2,1,0:T(8,128)(2,1)S(1)}, f16[1,64,2048]{2,1,0:T(8,128)(2,1)S(1)}, u32[]{:S(2)}, u32[]{:S(2)}) collective-permute-start(f16[1,64,2048]{2,1,0:T(8,128)(2,1)S(1)} %get-tuple-element.59), channel_id=1, source_target_pairs={{0,3},{1,0},{2,1},{3,2},{4,7},{5,4},{6,5},{7,6},{8,11},{9,8},{10,9... | collective-permute-start | bytes 786440 | tf_op jit(solution)/shard_map/ppermute | solution.py:458
  618.1 14.3 %collective-permute-start.1 = (f16[1,64,2048]{2,1,0:T(8,128)(2,1)S(1)}, f16[1,64,2048]{2,1,0:T(8,128)(2,1)S(1)}, u32[]{:S(2)}, u32[]{:S(2)}) collective-permute-start(f16[1,64,2048]{2,1,0:T(8,128)(2,1)S(1)} %get-tuple-element.60), channel_id=1, source_target_pairs={{0,2},{1,3},{2,0},{3,1},{4,6},{5,7},{6,4},{7,5},{8,10},{9,11},{10,... | collective-permute-start | bytes 786440 | tf_op jit(solution)/shard_map/ppermute | solution.py:458
  618.2 18.6 %collective-permute-start = (f16[1,64,2048]{2,1,0:T(8,128)(2,1)S(1)}, f16[1,64,2048]{2,1,0:T(8,128)(2,1)S(1)}, u32[]{:S(2)}, u32[]{:S(2)}) collective-permute-start(f16[1,64,2048]{2,1,0:T(8,128)(2,1)S(1)} %get-tuple-element.61), channel_id=1, source_target_pairs={{0,1},{1,2},{2,3},{3,0},{4,5},{5,6},{6,7},{7,4},{8,9},{9,10},{10,1... | collective-permute-start | bytes 786440 | tf_op jit(solution)/shard_map/ppermute | solution.py:458
  620.1 3.4 copy-start
  620.5 21.7 %collective-permute-start.8 = (f16[1,64,2048]{2,1,0:T(8,128)(2,1)S(1)}, f16[1,64,2048]{2,1,0:T(8,128)(2,1)S(1)}, u32[]{:S(2)}, u32[]{:S(2)}) collective-permute-start(f16[1,64,2048]{2,1,0:T(8,128)(2,1)S(1)} %get-tuple-element.56), channel_id=1, source_target_pairs={{0,3},{1,0},{2,1},{3,2},{4,7},{5,4},{6,5},{7,6},{8,11},{9,8},{10,9... | collective-permute-start | bytes 786440 | tf_op jit(solution)/shard_map/ppermute | solution.py:458
  622.0 21.8 %collective-permute-start.7 = (f16[1,64,2048]{2,1,0:T(8,128)(2,1)S(1)}, f16[1,64,2048]{2,1,0:T(8,128)(2,1)S(1)}, u32[]{:S(2)}, u32[]{:S(2)}) collective-permute-start(f16[1,64,2048]{2,1,0:T(8,128)(2,1)S(1)} %get-tuple-element.57), channel_id=1, source_target_pairs={{0,2},{1,3},{2,0},{3,1},{4,6},{5,7},{6,4},{7,5},{8,10},{9,11},{10,... | collective-permute-start | bytes 786440 | tf_op jit(solution)/shard_map/ppermute | solution.py:458
  623.5 2.2 copy-start.1
  631.0 17.7 %collective-permute-start.6 = (f16[1,64,2048]{2,1,0:T(8,128)(2,1)S(1)}, f16[1,64,2048]{2,1,0:T(8,128)(2,1)S(1)}, u32[]{:S(2)}, u32[]{:S(2)}) collective-permute-start(f16[1,64,2048]{2,1,0:T(8,128)(2,1)S(1)} %get-tuple-element.58), channel_id=1, source_target_pairs={{0,1},{1,2},{2,3},{3,0},{4,5},{5,6},{6,7},{7,4},{8,9},{9,10},{10,1... | collective-permute-start | bytes 786440 | tf_op jit(solution)/shard_map/ppermute | solution.py:458
  632.5 32.2 %collective-permute-start.5 = (f16[2,64,2048]{2,1,0:T(8,128)(2,1)S(1)}, f16[2,64,2048]{2,1,0:T(8,128)(2,1)S(1)}, u32[]{:S(2)}, u32[]{:S(2)}) collective-permute-start(f16[2,64,2048]{2,1,0:T(8,128)(2,1)S(1)} %get-tuple-element.53), channel_id=1, source_target_pairs={{0,3},{1,0},{2,1},{3,2},{4,7},{5,4},{6,5},{7,6},{8,11},{9,8},{10,9... | collective-permute-start | bytes 1572872 | tf_op jit(solution)/shard_map/ppermute | solution.py:458
  636.8 57.9 %collective-permute-start.4 = (f16[2,64,2048]{2,1,0:T(8,128)(2,1)S(1)}, f16[2,64,2048]{2,1,0:T(8,128)(2,1)S(1)}, u32[]{:S(2)}, u32[]{:S(2)}) collective-permute-start(f16[2,64,2048]{2,1,0:T(8,128)(2,1)S(1)} %get-tuple-element.54), channel_id=1, source_target_pairs={{0,2},{1,3},{2,0},{3,1},{4,6},{5,7},{6,4},{7,5},{8,10},{9,11},{10,... | collective-permute-start | bytes 1572872 | tf_op jit(solution)/shard_map/ppermute | solution.py:458
  642.2 53.5 %collective-permute-start.3 = (f16[2,64,2048]{2,1,0:T(8,128)(2,1)S(1)}, f16[2,64,2048]{2,1,0:T(8,128)(2,1)S(1)}, u32[]{:S(2)}, u32[]{:S(2)}) collective-permute-start(f16[2,64,2048]{2,1,0:T(8,128)(2,1)S(1)} %get-tuple-element.55), channel_id=1, source_target_pairs={{0,1},{1,2},{2,3},{3,0},{4,5},{5,6},{6,7},{7,4},{8,9},{9,10},{10,1... | collective-permute-start | bytes 1572872 | tf_op jit(solution)/shard_map/ppermute | solution.py:458
  643.7 33.0 %collective-permute-start.11 = (f16[2,64,2048]{2,1,0:T(8,128)(2,1)S(1)}, f16[2,64,2048]{2,1,0:T(8,128)(2,1)S(1)}, u32[]{:S(2)}, u32[]{:S(2)}) collective-permute-start(f16[2,64,2048]{2,1,0:T(8,128)(2,1)S(1)} %get-tuple-element.50), channel_id=1, source_target_pairs={{0,3},{1,0},{2,1},{3,2},{4,7},{5,4},{6,5},{7,6},{8,11},{9,8},{10,9... | collective-permute-start | bytes 1572872 | tf_op jit(solution)/shard_map/ppermute | solution.py:458
  648.7 34.0 %collective-permute-start.10 = (f16[2,64,2048]{2,1,0:T(8,128)(2,1)S(1)}, f16[2,64,2048]{2,1,0:T(8,128)(2,1)S(1)}, u32[]{:S(2)}, u32[]{:S(2)}) collective-permute-start(f16[2,64,2048]{2,1,0:T(8,128)(2,1)S(1)} %get-tuple-element.51), channel_id=1, source_target_pairs={{0,2},{1,3},{2,0},{3,1},{4,6},{5,7},{6,4},{7,5},{8,10},{9,11},{10,... | collective-permute-start | bytes 1572872 | tf_op jit(solution)/shard_map/ppermute | solution.py:458
  664.7 21.4 %collective-permute-start.9 = (f16[2,64,2048]{2,1,0:T(8,128)(2,1)S(1)}, f16[2,64,2048]{2,1,0:T(8,128)(2,1)S(1)}, u32[]{:S(2)}, u32[]{:S(2)}) collective-permute-start(f16[2,64,2048]{2,1,0:T(8,128)(2,1)S(1)} %get-tuple-element.52), channel_id=1, source_target_pairs={{0,1},{1,2},{2,3},{3,0},{4,5},{5,6},{6,7},{7,4},{8,9},{9,10},{10,1... | collective-permute-start | bytes 1572872 | tf_op jit(solution)/shard_map/ppermute | solution.py:458

commit v5 on v3

--- a/solution.py
+++ b/solution.py
@@ -243,10 +243,11 @@
 
 def wide_gram_kernel(momentum_ref, grad_ref, merged_ref, packed_ref, sum_ref, low):
     i = pl.program_id(0)
+    step = 2 * BLOCK
     merged = BETA * momentum_ref[...] + grad_ref[...]
     merged_ref[...] = merged
     rounded = merged.astype(BF16)
-    low[pl.ds(pl.multiple_of(i * BLOCK, BLOCK), BLOCK), :] = rounded
+    low[pl.ds(pl.multiple_of(i * step, step), step), :] = rounded
 
     @pl.when(i == 0)
     def _():
@@ -254,27 +255,34 @@
 
     squares = jnp.square(rounded.astype(F32))
     sum_ref[...] += jnp.sum(squares, axis=(0, 1), keepdims=True)
-    start = i * (i + 1) // 2
-
-    def columns(j, carry):
-        other = low[pl.ds(pl.multiple_of(j * (2 * BLOCK), 2 * BLOCK), 2 * BLOCK), :]
+
+    def columns(turn, carry):
+        j = i - turn
+        other = low[pl.ds(pl.multiple_of(j * step, step), step), :]
         product = dot_nt(rounded, other).astype(BF16)
-        for k in range(2):
-            place = pl.multiple_of((start + 2 * j + k) * BLOCK, BLOCK)
-            packed_ref[pl.ds(place, BLOCK), :] = product[:, k * BLOCK:(k + 1) * BLOCK]
+        for a in range(2):
+            row = 2 * i + a
+            for b in range(2):
+                place = pl.multiple_of((row * (row + 1) // 2 + 2 * j + b) * BLOCK, BLOCK)
+
+                @pl.when(jnp.logical_or(turn > 0, b <= a))
+                def _():
+                    packed_ref[pl.ds(place, BLOCK), :] = product[
+                        a * BLOCK:(a + 1) * BLOCK, b * BLOCK:(b + 1) * BLOCK
+                    ]
         return carry
 
-    lax.fori_loop(0, (i + 2) // 2, columns, 0)
+    lax.fori_loop(0, i + 1, columns, 0)
 
 
 def wide_gram(momentum, grad):
     height, width = momentum.shape
     number = height // BLOCK
     packed = number * (number + 1) // 2 * BLOCK
-    row_spec = pl.BlockSpec((BLOCK, width), lambda i: (i, 0))
+    row_spec = pl.BlockSpec((2 * BLOCK, width), lambda i: (i, 0))
     return pl.pallas_call(
         wide_gram_kernel,
-        grid=(number,),
+        grid=(number // 2,),
         out_shape=(
             jax.ShapeDtypeStruct((height, width), F32),
             jax.ShapeDtypeStruct((packed, BLOCK), BF16),
@@ -401,7 +409,7 @@
     per_group, rows, width = expert_momentum.shape
     _, wide_width = wide_momentum.shape[1:]
     most = 2 * -(-per_group // members)
-    sizes = [2, 1] * (most // 3) + [1] * (most % 3)
+    sizes = [1] + [2] * ((most - 2) // 2) + [1]
     starts = [sum(sizes[:i]) for i in range(len(sizes))]
     group_index = lax.axis_index("grp")
     me = lax.axis_index("fsdp")
@@ -440,11 +448,13 @@
 
     packed_rows = packed.shape[0] // half_members
     packed = packed.reshape(half_members, packed_rows, BLOCK)
-    total = lax.dynamic_index_in_dim(packed, place, 0, keepdims=False).astype(F32)
-    for turn in range(1, half_members):
-        part = lax.dynamic_index_in_dim(packed, onward[turn], 0, keepdims=False)
-        total = total + shifted(part, turn).astype(F32)
-    part = total.astype(BF16)
+    parts = lax.all_to_all(
+        packed, "fsdp", split_axis=0, concat_axis=0, tiled=True,
+        axis_index_groups=[
+            list(range(half_members)), list(range(half_members, members))
+        ],
+    )
+    part = jnp.sum(parts.astype(F32), axis=0).astype(BF16)
     other = lax.ppermute(part, "fsdp", mirror)
     part = (part.astype(F32) + other.astype(F32)).astype(BF16)
     packed = [part] + [shifted(part, turn) for turn in range(1, half_members)]

time: 708 us -> 667 us (0.942)
  waiting for transfers between devices: 365 us -> 288 us
  blocking collectives: 0 us -> 52 us
    ppermute x18 -> x15, waiting for transfers between devices: 203 us -> 115 us  [shifted(): return lax.ppermute(value, 'fsdp', pairs)]
    ppermute x1, waiting for transfers between devices: 78.9 us -> 0.01 us  [on_device(): other = lax.ppermute(part, 'fsdp', mirror)]
    all_to_all x0 -> x1, blocking collectives: none -> 52 us  [across(): lax.all_to_all(value, 'fsdp', split_axis=0, concat_axis=0, tiled=True)]
    all_to_all x5 -> x4, waiting for transfers between devices: 82.8 us -> 128 us  [across(): lax.all_to_all(value, 'fsdp', split_axis=0, concat_axis=0, tiled=True)]
    all_to_all x0 -> x1, waiting for transfers between devices: none -> 44.9 us  [on_device(): lax.all_to_all(packed, 'fsdp', split_axis=0, concat_axis=0, tiled=True, a...]
    all_to_all x5 -> x4, starting transfers between devices: 34.2 us -> 22.7 us  [across(): lax.all_to_all(value, 'fsdp', split_axis=0, concat_axis=0, tiled=True)]
    ppermute x18 -> x15, starting transfers between devices: 28.7 us -> 24.6 us  [shifted(): return lax.ppermute(value, 'fsdp', pairs)]
  transfers between devices with their start and end apart: 24 -> 21, of which waited for: 15 -> 14; matrix products, arithmetic and copies ran while one was open for 12% -> 14% of each run, Pallas kernels for 16% -> 10%
where the time goes in v5:
time: 667 us; the launch traced here: 665 us
  waiting for transfers between devices  288 us (43%)
  Pallas kernels  168 us (25%)
  starting transfers between devices  60 us (9%)
  other arithmetic  58.5 us (9%)
  blocking collectives  52 us (8%)
  local copies, waits for them, and re-layouts  36.6 us (5%)
    all_to_all x4, waiting for transfers between devices, across(): lax.all_to_all(value, 'fsdp', split_axis=0, concat_axis=0, tiled=True)  128 us
    ppermute x15, waiting for transfers between devices, shifted(): return lax.ppermute(value, 'fsdp', pairs)  115 us
    pallas_call x1, Pallas kernels, wide_solve(): pl.pallas_call(wide_solve_kernel, out_shape=jax.ShapeDtypeStruct((height,...  77.5 us
    all_to_all x1, blocking collectives, across(): lax.all_to_all(value, 'fsdp', split_axis=0, concat_axis=0, tiled=True)  52 us
    pallas_call x4, Pallas kernels, solve(): pl.pallas_call(functools.partial(solve_kernel, members, half_members, fir...  47.6 us
    all_to_all x1, waiting for transfers between devices, on_device(): lax.all_to_all(packed, 'fsdp', split_axis=0, concat_axis=0, tiled=True, a...  44.9 us
    gather x4, local copies, waits for them, and re-layouts, on_device(): picked = coded[slots[:, start:start + chunk].reshape(-1)]  24.8 us
    ppermute x15, starting transfers between devices, shifted(): return lax.ppermute(value, 'fsdp', pairs)  24.6 us
  transfers between devices with their start and end apart: 21, of which 14 were waited for; matrix products, arithmetic and copies ran while one was open for 14% of the time, Pallas kernels for 10%

profile of v5, /device:TPU:0, one launch (start us, length us, event | category | flops | bytes accessed | tf_op | source)
XLA Modules:
  0.0 665.4 jit_solution(10348197175673343397)
XLA Ops:
  0.6 11.7 %wide_gram.1 = (f32[2048,512]{1,0:T(8,128)}, bf16[9216,256]{1,0:T(8,128)(2,1)}, f32[8,128]{1,0:T(8,128)}) custom-call(f32[2048,512]{1,0:T(8,128)} %bitcast.61, f32[2048,512]{1,0:T(8,128)} %bitcast.62), custom_call_target="tpu_custom_call" | custom-call | flops 2415919104 | bytes 17301504 | tf_op jit(solution)/shard_map/wide_gram/pallas_call | solution.py:283
  12.4 1.2 slice.122
  13.6 13.9 %merge.1 = (f32[24,64,2048]{2,1,0:T(8,128)}, f32[24,8,128]{2,1,0:T(8,128)}) custom-call(f32[24,64,2048]{2,1,0:T(8,128)} %momentum_ref.1, f32[24,64,2048]{2,1,0:T(8,128)} %grad_ref.1), custom_call_target="tpu_custom_call" | custom-call | flops 15728640 | bytes 37748736 | tf_op jit(solution)/shard_map/merge/pallas_call | solution.py:107
  27.5 1.2 slice_reduce_fusion
  30.0 7.3 %all-to-all-start = ((f32[8,1,128]{2,1,0:T(1,128)}), f32[8,1,128]{2,1,0:T(1,128)S(1)}, u32[]{:S(2)}, u32[]{:S(2)}) async-start(f32[8,1,128]{2,1,0:T(1,128)} %broadcast_in_dim.81), calls=%async_computation | async-start | bytes 8192 | tf_op jit(solution)/shard_map/all_to_all | solution.py:424
  37.3 2.5 route.1
  40.7 8.4 %convert_element_type.164 = f16[24,64,2048]{2,1,0:T(8,128)(2,1)} convert(f32[24,64,2048]{2,1,0:T(8,128)} %get-tuple-element.22) | non-fusion elementwise | flops 3145728 | bytes 18874368 | tf_op jit(solution)/shard_map/convert_element_type | solution.py:443
  49.1 5.5 gather_fusion.4
  54.5 6.0 all-to-all-start.4
  60.5 5.5 gather_fusion.1
  66.0 42.2 %all-to-all-done.4 = f16[8,1,64,2048]{3,2,1,0:T(8,128)(2,1)S(1)} async-done(((f16[8,1,64,2048]{3,2,1,0:T(8,128)(2,1)}), f16[8,1,64,2048]{3,2,1,0:T(8,128)(2,1)S(1)}, u32[]{:S(2)}, u32[]{:S(2)}) %all-to-all-start.4) | async-done | bytes 2097184 | tf_op jit(solution)/shard_map/all_to_all | solution.py:424
  108.2 1.3 copy-done.2
  109.5 52.0 %all_to_all.30 = f16[8,1,64,2048]{3,2,1,0:T(8,128)(2,1)S(1)} all-to-all(f16[8,1,64,2048]{3,2,1,0:T(8,128)(2,1)} %bitcast.57), channel_id=1, replica_groups=mesh['grp'=4,'fsdp'=8] {'fsdp'}, dimensions={0} | all-to-all | bytes 4194304 | tf_op jit(solution)/shard_map/all_to_all | solution.py:424
  161.6 4.9 all-to-all-start.5
  166.7 7.0 %gather_fusion.3 = f16[16,64,2048]{2,1,0:T(8,128)(2,1)} fusion(f16[24,64,2048]{2,1,0:T(8,128)(2,1)} %convert_element_type.164, s32[1024]{0:T(1024)S(1)} %pad_clamp_fusion.1), kind=kCustom, calls=%fused_computation.3 | custom fusion | bytes 8388672 | tf_op jit(solution)/shard_map/gather | solution.py:446
  173.6 44.9 %all-to-all-done.5 = bf16[4,2304,256]{2,1,0:T(8,128)(2,1)} async-done(((bf16[4,2304,256]{2,1,0:T(8,128)(2,1)}), bf16[4,2304,256]{2,1,0:T(8,128)(2,1)}, u32[]{:S(2)}, u32[]{:S(2)}) %all-to-all-start.5) | async-done | bytes 4718624 | tf_op jit(solution)/shard_map/all_to_all | solution.py:451
  218.5 4.6 all-to-all-start.3
  223.2 6.9 %gather_fusion.2 = f16[16,64,2048]{2,1,0:T(8,128)(2,1)} fusion(f16[24,64,2048]{2,1,0:T(8,128)(2,1)} %convert_element_type.164, s32[1024]{0:T(1024)S(1)} %pad_clamp_fusion.2), kind=kCustom, calls=%fused_computation.2 | custom fusion | bytes 8388672 | tf_op jit(solution)/shard_map/gather | solution.py:446
  230.1 85.6 %all-to-all-done.3 = f16[8,2,64,2048]{3,2,1,0:T(8,128)(2,1)} async-done(((f16[8,2,64,2048]{3,2,1,0:T(8,128)(2,1)}), f16[8,2,64,2048]{3,2,1,0:T(8,128)(2,1)}, u32[]{:S(2)}, u32[]{:S(2)}) %all-to-all-start.3) | async-done | bytes 4194336 | tf_op jit(solution)/shard_map/all_to_all | solution.py:424
  315.8 4.8 all-to-all-start.2
  329.0 1.2 fusion.15
  330.2 4.0 convert_element_type.168.data_ref
  334.2 9.5 %shard_map.94 = (f32[6,512,2048]{2,1,0:T(8,128)}, f32[4,1,64,2048]{3,2,1,0:T(8,128)}) custom-call(s32[4]{0:T(128)} %fusion.5.row_ref, f32[48]{0:T(128)} %div.46.scale_ref, f32[6]{0:T(128)} %copy-done.4, f32[6]{0:T(128)} %get-tuple-element.72.factor_ref, f32[6]{0:T(128)} %get-tuple-element.71.ratio_ref, f32[8,1,64,2048]{3,2,1,0:T(8,128)} %convert_element_type.168.data_ref), custom_call_target="tpu_custom_call" | custom-call | flops 3489660928 | bytes 12582912 | tf_op jit(solution)/shard_map/pallas_call | solution.py:180
  343.7 1.7 convert.24
  345.6 2.6 collective-permute-start.11
  351.0 2.4 convert_element_type.165.data_ref
  353.4 42.4 %collective-permute-done.11 = f16[1,64,2048]{2,1,0:T(8,128)(2,1)S(1)} collective-permute-done((f16[1,64,2048]{2,1,0:T(8,128)(2,1)S(1)}, f16[1,64,2048]{2,1,0:T(8,128)(2,1)S(1)}, u32[]{:S(2)}, u32[]{:S(2)}) %collective-permute-start.11) | collective-permute-done | bytes 262176 | tf_op jit(solution)/shard_map/ppermute | solution.py:431
  395.7 1.5 convert_multiply_fusion.6.rest_2_
  397.2 2.2 collective-permute-done.10
  399.4 1.5 convert_multiply_fusion.7.rest_1_
  400.9 1.4 convert_multiply_fusion.8.rest_0_
  402.3 3.1 home.4.rest_3_
  405.4 3.8 reduce_sum.72
  409.2 7.8 %collective-permute-start.12 = (bf16[2304,256]{1,0:T(8,128)(2,1)S(1)}, bf16[2304,256]{1,0:T(8,128)(2,1)S(1)}, u32[]{:S(2)}, u32[]{:S(2)}) collective-permute-start(bf16[2304,256]{1,0:T(8,128)(2,1)S(1)} %reduce_sum.72), channel_id=1, source_target_pairs={{0,4},{1,5},{2,6},{3,7},{4,0},{5,1},{6,2},{7,3},{8,12},{9,13},{10,... | collective-permute-start | bytes 3538952 | tf_op jit(solution)/shard_map/ppermute | solution.py:458
  417.0 6.4 convert_element_type.167.data_ref
  423.4 14.3 %shard_map.95 = (f32[6,512,2048]{2,1,0:T(8,128)}, f32[4,2,64,2048]{3,2,1,0:T(8,128)}) custom-call(s32[4]{0:T(128)} %fusion.5.row_ref, f32[48]{0:T(128)} %div.46.scale_ref, f32[6]{0:T(128)} %copy-done.4, f32[6]{0:T(128)} %get-tuple-element.72.factor_ref, f32[6]{0:T(128)} %get-tuple-element.71.ratio_ref, ...), custom_call_target="tpu_custom_call", output_to_operand_aliasing={{0}: (6, {})} | custom-call | flops 6979321856 | bytes 25165824 | tf_op jit(solution)/shard_map/pallas_call | solution.py:180
  437.7 6.4 convert_element_type.166.data_ref
  444.1 14.3 %shard_map.96 = (f32[6,512,2048]{2,1,0:T(8,128)}, f32[4,2,64,2048]{3,2,1,0:T(8,128)}) custom-call(s32[4]{0:T(128)} %fusion.5.row_ref, f32[48]{0:T(128)} %div.46.scale_ref, f32[6]{0:T(128)} %copy-done.4, f32[6]{0:T(128)} %get-tuple-element.72.factor_ref, f32[6]{0:T(128)} %get-tuple-element.71.ratio_ref, ...), custom_call_target="tpu_custom_call", output_to_operand_aliasing={{0}: (6, {})} | custom-call | flops 6979321856 | bytes 25165824 | tf_op jit(solution)/shard_map/pallas_call | solution.py:180
  458.4 9.5 %shard_map.97 = (f32[6,512,2048]{2,1,0:T(8,128)}, f32[4,1,64,2048]{3,2,1,0:T(8,128)}) custom-call(s32[4]{0:T(128)} %fusion.5.row_ref, f32[48]{0:T(128)} %div.46.scale_ref, f32[6]{0:T(128)} %copy-done.4, f32[6]{0:T(128)} %get-tuple-element.72.factor_ref, f32[6]{0:T(128)} %get-tuple-element.71.ratio_ref, ...), custom_call_target="tpu_custom_call", output_to_operand_aliasing={{0}: (6, {})} | custom-call | flops 3489660928 | bytes 12582912 | tf_op jit(solution)/shard_map/pallas_call | solution.py:180
  467.9 1.9 convert.21
  470.0 5.0 collective-permute-start.2
  475.0 4.5 collective-permute-start.1
  481.0 2.9 collective-permute-start.5
  484.5 2.6 collective-permute-done.2
  487.1 1.5 convert_multiply_fusion.9.rest_2_
  488.7 3.6 collective-permute-done.1
  492.3 1.4 convert_multiply_fusion.10.rest_1_
  493.7 6.2 collective-permute-start.8
  500.0 1.4 convert_multiply_fusion.11.rest_0_
  501.4 8.2 %collective-permute-done.5 = f16[2,64,2048]{2,1,0:T(8,128)(2,1)S(1)} collective-permute-done((f16[2,64,2048]{2,1,0:T(8,128)(2,1)S(1)}, f16[2,64,2048]{2,1,0:T(8,128)(2,1)S(1)}, u32[]{:S(2)}, u32[]{:S(2)}) %collective-permute-start.5) | collective-permute-done | bytes 524320 | tf_op jit(solution)/shard_map/ppermute | solution.py:431
  509.6 1.2 convert_multiply_fusion.3.rest_2_
  510.7 4.0 collective-permute-done.4
  514.8 1.2 convert_multiply_fusion.4.rest_1_
  516.0 7.6 %collective-permute-done.8 = f16[2,64,2048]{2,1,0:T(8,128)(2,1)S(1)} collective-permute-done((f16[2,64,2048]{2,1,0:T(8,128)(2,1)S(1)}, f16[2,64,2048]{2,1,0:T(8,128)(2,1)S(1)}, u32[]{:S(2)}, u32[]{:S(2)}) %collective-permute-start.8) | collective-permute-done | bytes 524320 | tf_op jit(solution)/shard_map/ppermute | solution.py:431
  524.7 9.8 %collective-permute-done.7 = f16[2,64,2048]{2,1,0:T(8,128)(2,1)S(1)} collective-permute-done((f16[2,64,2048]{2,1,0:T(8,128)(2,1)S(1)}, f16[2,64,2048]{2,1,0:T(8,128)(2,1)S(1)}, u32[]{:S(2)}, u32[]{:S(2)}) %collective-permute-start.7) | collective-permute-done | bytes 524320 | tf_op jit(solution)/shard_map/ppermute | solution.py:431
  536.1 1.9 collective-permute-start.13
  539.2 4.2 home.5.rest_3_
  543.4 2.2 convert_multiply_fusion.5.rest_0_
  545.6 4.2 home.6.rest_3_
  549.9 3.1 home.7
  553.0 11.0 %collective-permute-done.15.rest_3_ = bf16[2304,256]{1,0:T(8,128)(2,1)S(1)} collective-permute-done((bf16[2304,256]{1,0:T(8,128)(2,1)S(1)}, bf16[2304,256]{1,0:T(8,128)(2,1)S(1)}, u32[]{:S(2)}, u32[]{:S(2)}) %collective-permute-start.15) | collective-permute-done | bytes 1179680 | tf_op jit(solution)/shard_map/ppermute | solution.py:431
  563.9 21.6 %collective-permute-done.14.rest_2_ = bf16[2304,256]{1,0:T(8,128)(2,1)S(1)} collective-permute-done((bf16[2304,256]{1,0:T(8,128)(2,1)S(1)}, bf16[2304,256]{1,0:T(8,128)(2,1)S(1)}, u32[]{:S(2)}, u32[]{:S(2)}) %collective-permute-start.14) | collective-permute-done | bytes 1179680 | tf_op jit(solution)/shard_map/ppermute | solution.py:431
  585.6 2.2 collective-permute-done.13.rest_1_
  587.7 77.5 %wide_solve.1 = f32[2048,512]{1,0:T(8,128)} custom-call(f32[3]{0:T(128)} %pad_maximum_fusion.coef_ref, s32[4]{0:T(128)} %and_select_fusion.turn_ref, f32[36]{0:T(128)} %constant.101.clone.table_ref, f32[2048,512]{1,0:T(8,128)} %get-tuple-element.30.merged_ref, bf16[2304,256]{1,0:T(8,128)(2,1)} %copy-done.3, ...), custom_call_target="tpu_custom_call" | custom-call | flops 51539607552 | bytes 8388608 | tf_op jit(solution)/shard_map/wide_solve/pallas_call | solution.py:388
  (81 shorter events, 18.4 us)
Async XLA Ops:
  30.0 24.6 %all-to-all-start = ((f32[8,1,128]{2,1,0:T(1,128)}), f32[8,1,128]{2,1,0:T(1,128)S(1)}, u32[]{:S(2)}, u32[]{:S(2)}) async-start(f32[8,1,128]{2,1,0:T(1,128)} %broadcast_in_dim.81), calls=%async_computation | async-start | bytes 8192 | tf_op jit(solution)/shard_map/all_to_all | solution.py:424
  54.5 53.7 %all-to-all-start.4 = ((f16[8,1,64,2048]{3,2,1,0:T(8,128)(2,1)}), f16[8,1,64,2048]{3,2,1,0:T(8,128)(2,1)S(1)}, u32[]{:S(2)}, u32[]{:S(2)}) async-start(f16[8,1,64,2048]{3,2,1,0:T(8,128)(2,1)} %bitcast.56), calls=%async_computation.4 | async-start | bytes 4194304 | tf_op jit(solution)/shard_map/all_to_all | solution.py:424
  108.2 1.3 copy-start.2
  161.6 57.0 %all-to-all-start.5 = ((bf16[4,2304,256]{2,1,0:T(8,128)(2,1)}), bf16[4,2304,256]{2,1,0:T(8,128)(2,1)}, u32[]{:S(2)}, u32[]{:S(2)}) async-start(bf16[4,2304,256]{2,1,0:T(8,128)(2,1)} %bitcast.58), calls=%async_computation.5 | async-start | bytes 9437184 | tf_op jit(solution)/shard_map/all_to_all | solution.py:451
  218.5 97.2 %all-to-all-start.3 = ((f16[8,2,64,2048]{3,2,1,0:T(8,128)(2,1)}), f16[8,2,64,2048]{3,2,1,0:T(8,128)(2,1)}, u32[]{:S(2)}, u32[]{:S(2)}) async-start(f16[8,2,64,2048]{3,2,1,0:T(8,128)(2,1)} %bitcast.55), calls=%async_computation.3 | async-start | bytes 8388608 | tf_op jit(solution)/shard_map/all_to_all | solution.py:424
  315.8 4.9 copy-start.7
  315.8 8.2 %copy-start.8 = (s32[8]{0:T(128)S(1)}, s32[8]{0:T(128)}, u32[]{:S(2)}) copy-start(s32[8]{0:T(128)} %get-tuple-element.21) | copy-start | bytes 100
  315.8 121.9 %all-to-all-start.2 = ((f16[8,2,64,2048]{3,2,1,0:T(8,128)(2,1)}), f16[8,2,64,2048]{3,2,1,0:T(8,128)(2,1)}, u32[]{:S(2)}, u32[]{:S(2)}) async-start(f16[8,2,64,2048]{3,2,1,0:T(8,128)(2,1)} %bitcast.54), calls=%async_computation.2 | async-start | bytes 8388608 | tf_op jit(solution)/shard_map/all_to_all | solution.py:424
  328.9 5.4 copy-start.4
  345.6 50.1 %collective-permute-start.11 = (f16[1,64,2048]{2,1,0:T(8,128)(2,1)S(1)}, f16[1,64,2048]{2,1,0:T(8,128)(2,1)S(1)}, u32[]{:S(2)}, u32[]{:S(2)}) collective-permute-start(f16[1,64,2048]{2,1,0:T(8,128)(2,1)S(1)} %get-tuple-element.53), channel_id=1, source_target_pairs={{0,3},{1,0},{2,1},{3,2},{4,7},{5,4},{6,5},{7,6},{8,11},{9,8},{10,9... | collective-permute-start | bytes 786440 | tf_op jit(solution)/shard_map/ppermute | solution.py:431
  349.8 49.6 %collective-permute-start.10 = (f16[1,64,2048]{2,1,0:T(8,128)(2,1)S(1)}, f16[1,64,2048]{2,1,0:T(8,128)(2,1)S(1)}, u32[]{:S(2)}, u32[]{:S(2)}) collective-permute-start(f16[1,64,2048]{2,1,0:T(8,128)(2,1)S(1)} %get-tuple-element.54), channel_id=1, source_target_pairs={{0,2},{1,3},{2,0},{3,1},{4,6},{5,7},{6,4},{7,5},{8,10},{9,11},{10,... | collective-permute-start | bytes 786440 | tf_op jit(solution)/shard_map/ppermute | solution.py:431
  350.4 50.5 %collective-permute-start.9 = (f16[1,64,2048]{2,1,0:T(8,128)(2,1)S(1)}, f16[1,64,2048]{2,1,0:T(8,128)(2,1)S(1)}, u32[]{:S(2)}, u32[]{:S(2)}) collective-permute-start(f16[1,64,2048]{2,1,0:T(8,128)(2,1)S(1)} %get-tuple-element.55), channel_id=1, source_target_pairs={{0,1},{1,2},{2,3},{3,0},{4,5},{5,6},{6,7},{7,4},{8,9},{9,10},{10,1... | collective-permute-start | bytes 786440 | tf_op jit(solution)/shard_map/ppermute | solution.py:431
  409.2 126.4 %collective-permute-start.12 = (bf16[2304,256]{1,0:T(8,128)(2,1)S(1)}, bf16[2304,256]{1,0:T(8,128)(2,1)S(1)}, u32[]{:S(2)}, u32[]{:S(2)}) collective-permute-start(bf16[2304,256]{1,0:T(8,128)(2,1)S(1)} %reduce_sum.72), channel_id=1, source_target_pairs={{0,4},{1,5},{2,6},{3,7},{4,0},{5,1},{6,2},{7,3},{8,12},{9,13},{10,... | collective-permute-start | bytes 3538952 | tf_op jit(solution)/shard_map/ppermute | solution.py:458
  467.9 11.6 %copy-start = (f32[4,2,64,2048]{3,2,1,0:T(8,128)S(1)}, f32[4,2,64,2048]{3,2,1,0:T(8,128)}, u32[]{:S(2)}) copy-start(f32[4,2,64,2048]{3,2,1,0:T(8,128)} %get-tuple-element.27.local_ref) | copy-start | bytes 12582916
  470.0 17.1 %collective-permute-start.2 = (f16[1,64,2048]{2,1,0:T(8,128)(2,1)S(1)}, f16[1,64,2048]{2,1,0:T(8,128)(2,1)S(1)}, u32[]{:S(2)}, u32[]{:S(2)}) collective-permute-start(f16[1,64,2048]{2,1,0:T(8,128)(2,1)S(1)} %get-tuple-element.56), channel_id=1, source_target_pairs={{0,3},{1,0},{2,1},{3,2},{4,7},{5,4},{6,5},{7,6},{8,11},{9,8},{10,9... | collective-permute-start | bytes 786440 | tf_op jit(solution)/shard_map/ppermute | solution.py:431
  475.0 17.2 %collective-permute-start.1 = (f16[1,64,2048]{2,1,0:T(8,128)(2,1)S(1)}, f16[1,64,2048]{2,1,0:T(8,128)(2,1)S(1)}, u32[]{:S(2)}, u32[]{:S(2)}) collective-permute-start(f16[1,64,2048]{2,1,0:T(8,128)(2,1)S(1)} %get-tuple-element.57), channel_id=1, source_target_pairs={{0,2},{1,3},{2,0},{3,1},{4,6},{5,7},{6,4},{7,5},{8,10},{9,11},{10,... | collective-permute-start | bytes 786440 | tf_op jit(solution)/shard_map/ppermute | solution.py:431
  479.5 14.2 %collective-permute-start = (f16[1,64,2048]{2,1,0:T(8,128)(2,1)S(1)}, f16[1,64,2048]{2,1,0:T(8,128)(2,1)S(1)}, u32[]{:S(2)}, u32[]{:S(2)}) collective-permute-start(f16[1,64,2048]{2,1,0:T(8,128)(2,1)S(1)} %get-tuple-element.58), channel_id=1, source_target_pairs={{0,1},{1,2},{2,3},{3,0},{4,5},{5,6},{6,7},{7,4},{8,9},{9,10},{10,1... | collective-permute-start | bytes 786440 | tf_op jit(solution)/shard_map/ppermute | solution.py:431
  479.5 4.4 copy-start.1
  481.0 28.6 %collective-permute-start.5 = (f16[2,64,2048]{2,1,0:T(8,128)(2,1)S(1)}, f16[2,64,2048]{2,1,0:T(8,128)(2,1)S(1)}, u32[]{:S(2)}, u32[]{:S(2)}) collective-permute-start(f16[2,64,2048]{2,1,0:T(8,128)(2,1)S(1)} %get-tuple-element.50), channel_id=1, source_target_pairs={{0,3},{1,0},{2,1},{3,2},{4,7},{5,4},{6,5},{7,6},{8,11},{9,8},{10,9... | collective-permute-start | bytes 1572872 | tf_op jit(solution)/shard_map/ppermute | solution.py:431
  487.1 27.6 %collective-permute-start.4 = (f16[2,64,2048]{2,1,0:T(8,128)(2,1)S(1)}, f16[2,64,2048]{2,1,0:T(8,128)(2,1)S(1)}, u32[]{:S(2)}, u32[]{:S(2)}) collective-permute-start(f16[2,64,2048]{2,1,0:T(8,128)(2,1)S(1)} %get-tuple-element.51), channel_id=1, source_target_pairs={{0,2},{1,3},{2,0},{3,1},{4,6},{5,7},{6,4},{7,5},{8,10},{9,11},{10,... | collective-permute-start | bytes 1572872 | tf_op jit(solution)/shard_map/ppermute | solution.py:431
  492.3 51.1 %collective-permute-start.3 = (f16[2,64,2048]{2,1,0:T(8,128)(2,1)}, f16[2,64,2048]{2,1,0:T(8,128)(2,1)}, u32[]{:S(2)}, u32[]{:S(2)}) collective-permute-start(f16[2,64,2048]{2,1,0:T(8,128)(2,1)} %get-tuple-element.52), channel_id=1, source_target_pairs={{0,1},{1,2},{2,3},{3,0},{4,5},{5,6},{6,7},{7,4},{8,9},{9,10},{10,1... | collective-permute-start | bytes 1572872 | tf_op jit(solution)/shard_map/ppermute | solution.py:431
  493.7 29.8 %collective-permute-start.8 = (f16[2,64,2048]{2,1,0:T(8,128)(2,1)S(1)}, f16[2,64,2048]{2,1,0:T(8,128)(2,1)S(1)}, u32[]{:S(2)}, u32[]{:S(2)}) collective-permute-start(f16[2,64,2048]{2,1,0:T(8,128)(2,1)S(1)} %get-tuple-element.47), channel_id=1, source_target_pairs={{0,3},{1,0},{2,1},{3,2},{4,7},{5,4},{6,5},{7,6},{8,11},{9,8},{10,9... | collective-permute-start | bytes 1572872 | tf_op jit(solution)/shard_map/ppermute | solution.py:431
  509.6 24.9 %collective-permute-start.7 = (f16[2,64,2048]{2,1,0:T(8,128)(2,1)S(1)}, f16[2,64,2048]{2,1,0:T(8,128)(2,1)S(1)}, u32[]{:S(2)}, u32[]{:S(2)}) collective-permute-start(f16[2,64,2048]{2,1,0:T(8,128)(2,1)S(1)} %get-tuple-element.48), channel_id=1, source_target_pairs={{0,2},{1,3},{2,0},{3,1},{4,6},{5,7},{6,4},{7,5},{8,10},{9,11},{10,... | collective-permute-start | bytes 1572872 | tf_op jit(solution)/shard_map/ppermute | solution.py:431
  514.8 23.3 %collective-permute-start.6 = (f16[2,64,2048]{2,1,0:T(8,128)(2,1)S(1)}, f16[2,64,2048]{2,1,0:T(8,128)(2,1)S(1)}, u32[]{:S(2)}, u32[]{:S(2)}) collective-permute-start(f16[2,64,2048]{2,1,0:T(8,128)(2,1)S(1)} %get-tuple-element.49), channel_id=1, source_target_pairs={{0,1},{1,2},{2,3},{3,0},{4,5},{5,6},{6,7},{7,4},{8,9},{9,10},{10,1... | collective-permute-start | bytes 1572872 | tf_op jit(solution)/shard_map/ppermute | solution.py:431
  535.9 7.5 %copy-start.3 = (bf16[2304,256]{1,0:T(8,128)(2,1)}, bf16[2304,256]{1,0:T(8,128)(2,1)S(1)}, u32[]{:S(2)}) copy-start(bf16[2304,256]{1,0:T(8,128)(2,1)S(1)} %add_convert_fusion.rest_0_) | copy-start | bytes 3538948
  535.9 28.0 %collective-permute-start.15 = (bf16[2304,256]{1,0:T(8,128)(2,1)S(1)}, bf16[2304,256]{1,0:T(8,128)(2,1)S(1)}, u32[]{:S(2)}, u32[]{:S(2)}) collective-permute-start(bf16[2304,256]{1,0:T(8,128)(2,1)S(1)} %add_convert_fusion.rest_0_), channel_id=1, source_target_pairs={{0,3},{1,0},{2,1},{3,2},{4,7},{5,4},{6,5},{7,6},{8,11},{9,8},{10,9... | collective-permute-start | bytes 3538952 | tf_op jit(solution)/shard_map/ppermute | solution.py:431
  536.0 49.6 %collective-permute-start.14 = (bf16[2304,256]{1,0:T(8,128)(2,1)S(1)}, bf16[2304,256]{1,0:T(8,128)(2,1)S(1)}, u32[]{:S(2)}, u32[]{:S(2)}) collective-permute-start(bf16[2304,256]{1,0:T(8,128)(2,1)S(1)} %add_convert_fusion.rest_0_), channel_id=1, source_target_pairs={{0,2},{1,3},{2,0},{3,1},{4,6},{5,7},{6,4},{7,5},{8,10},{9,11},{10,... | collective-permute-start | bytes 3538952 | tf_op jit(solution)/shard_map/ppermute | solution.py:431
  536.1 51.6 %collective-permute-start.13 = (bf16[2304,256]{1,0:T(8,128)(2,1)S(1)}, bf16[2304,256]{1,0:T(8,128)(2,1)}, u32[]{:S(2)}, u32[]{:S(2)}) collective-permute-start(bf16[2304,256]{1,0:T(8,128)(2,1)S(1)} %add_convert_fusion.rest_0_), channel_id=1, source_target_pairs={{0,1},{1,2},{2,3},{3,0},{4,5},{5,6},{6,7},{7,4},{8,9},{9,10},{10,1... | collective-permute-start | bytes 3538952 | tf_op jit(solution)/shard_map/ppermute | solution.py:431
  563.9 23.8 %copy-start.5 = (bf16[2304,256]{1,0:T(8,128)(2,1)}, bf16[2304,256]{1,0:T(8,128)(2,1)S(1)}, u32[]{:S(2)}) copy-start(bf16[2304,256]{1,0:T(8,128)(2,1)S(1)} %collective-permute-done.15.rest_3_) | copy-start | bytes 3538948
  585.6 2.2 copy-start.6

commit v6 on v4

--- a/solution.py
+++ b/solution.py
@@ -19,7 +19,7 @@
 SMALLEST = 1e-30
 BLOCK = 256
 PIECE = 128
-SWEEP = 512
+SWEEP = 1024
 
 F32 = jnp.float32
 BF16 = jnp.bfloat16
@@ -118,31 +118,32 @@
     )(momentum, grad)
 
 
-def pick_kernel(table_ref, momentum_ref, grad_ref, scaled_ref):
-    merged = BETA * momentum_ref[0] + grad_ref[0]
-    top = jnp.maximum(jnp.max(jnp.abs(merged), keepdims=True), SMALLEST)
-    scaled_ref[0, 0] = merged * (F16_TOP / top)
+def pick_kernel(table_ref, *refs):
+    scaled_ref = refs[-1]
+    for slot in range(scaled_ref.shape[1]):
+        merged = BETA * refs[2 * slot][0] + refs[2 * slot + 1][0]
+        top = jnp.maximum(jnp.max(jnp.abs(merged), keepdims=True), SMALLEST)
+        scaled_ref[0, slot] = merged * (F16_TOP / top)
 
 
 def pick_first(table, momentum, grad, members, most, chunk):
     rows, width = momentum.shape[1:]
-    source = pl.BlockSpec(
-        (1, rows, width), lambda i, table: (table[i // chunk * most + i % chunk], 0, 0)
-    )
+
+    def source(slot):
+        return pl.BlockSpec((1, rows, width), lambda i, table: (table[i * most + slot], 0, 0))
+
     return pl.pallas_call(
         pick_kernel,
         grid_spec=pltpu.PrefetchScalarGridSpec(
             num_scalar_prefetch=1,
-            grid=(members * chunk,),
-            in_specs=[source, source],
-            out_specs=pl.BlockSpec(
-                (1, 1, rows, width), lambda i, table: (i // chunk, i % chunk, 0, 0)
-            ),
+            grid=(members,),
+            in_specs=[source(slot) for slot in range(chunk) for _ in range(2)],
+            out_specs=pl.BlockSpec((1, chunk, rows, width), lambda i, table: (i, 0, 0, 0)),
         ),
         out_shape=jax.ShapeDtypeStruct((members, chunk, rows, width), F32),
         name="pick_first",
         cost_estimate=cost(2e9, members * chunk * rows * width * 12),
-    )(table, momentum, grad)
+    )(table, *([momentum, grad] * chunk))
 
 
 def solve_kernel(

time: 706 us -> 702 us (level)
  transfers between devices with their start and end apart: 24 -> 24, of which waited for: 15 -> 15; matrix products, arithmetic and copies ran while one was open for 12% -> 12% of each run, Pallas kernels for 18% -> 17%
where the time goes in v6:
time: 702 us; the launch traced here: 700 us
  waiting for transfers between devices  354 us (50%)
  Pallas kernels  176 us (25%)
  starting transfers between devices  65.4 us (9%)
  other arithmetic  63.8 us (9%)
  local copies, waits for them, and re-layouts  33.5 us (5%)
  between operations  8.15 us (1%)
    ppermute x18, waiting for transfers between devices, shifted(): return lax.ppermute(value, 'fsdp', pairs)  203 us
    ppermute x1, waiting for transfers between devices, on_device(): other = lax.ppermute(part, 'fsdp', mirror)  79 us
    pallas_call x1, Pallas kernels, wide_solve(): pl.pallas_call(wide_solve_kernel, out_shape=jax.ShapeDtypeStruct((height,...  73.5 us
    all_to_all x5, waiting for transfers between devices, across(): lax.all_to_all(value, 'fsdp', split_axis=0, concat_axis=0, tiled=True)  71.7 us
    pallas_call x4, Pallas kernels, solve(): pl.pallas_call(functools.partial(solve_kernel, members, half_members, fir...  47.6 us
    all_to_all x5, starting transfers between devices, across(): lax.all_to_all(value, 'fsdp', split_axis=0, concat_axis=0, tiled=True)  34.2 us
    ppermute x18, starting transfers between devices, shifted(): return lax.ppermute(value, 'fsdp', pairs)  28.6 us
    convert_element_type x4, other arithmetic, on_device(): piece.astype(F32)  19.5 us
  transfers between devices with their start and end apart: 24, of which 15 were waited for; matrix products, arithmetic and copies ran while one was open for 12% of the time, Pallas kernels for 17%

profile of v6, /device:TPU:0, one launch (start us, length us, event | category | flops | bytes accessed | tf_op | source)
XLA Modules:
  0.0 700.5 jit_solution(13303167512040213451)
XLA Ops:
  0.6 11.7 %wide_gram.1 = (f32[2048,512]{1,0:T(8,128)}, bf16[9216,256]{1,0:T(8,128)(2,1)}, f32[8,128]{1,0:T(8,128)}) custom-call(f32[2048,512]{1,0:T(8,128)} %bitcast.70, f32[2048,512]{1,0:T(8,128)} %bitcast.71), custom_call_target="tpu_custom_call" | custom-call | flops 2415919104 | bytes 17301504 | tf_op jit(solution)/shard_map/wide_gram/pallas_call | solution.py:311
  13.6 13.9 %merge.1 = (f32[24,64,2048]{2,1,0:T(8,128)}, f32[24,8,128]{2,1,0:T(8,128)}) custom-call(f32[24,64,2048]{2,1,0:T(8,128)} %refs_2_.1, f32[24,64,2048]{2,1,0:T(8,128)} %refs_3_.1), custom_call_target="tpu_custom_call" | custom-call | flops 15728640 | bytes 37748736 | tf_op jit(solution)/shard_map/merge/pallas_call | solution.py:107
  30.0 7.3 %all-to-all-start = ((f32[8,1,128]{2,1,0:T(1,128)}), f32[8,1,128]{2,1,0:T(1,128)S(1)}, u32[]{:S(2)}, u32[]{:S(2)}) async-start(f32[8,1,128]{2,1,0:T(1,128)} %broadcast_in_dim.80), calls=%async_computation | async-start | bytes 8192 | tf_op jit(solution)/shard_map/all_to_all | solution.py:452
  37.3 2.5 route.1
  40.7 8.4 %convert_element_type.183 = f16[24,64,2048]{2,1,0:T(8,128)(2,1)} convert(f32[24,64,2048]{2,1,0:T(8,128)} %get-tuple-element.22) | non-fusion elementwise | flops 3145728 | bytes 18874368 | tf_op jit(solution)/shard_map/convert_element_type | solution.py:471
  49.1 5.5 gather_fusion.3
  54.6 6.0 all-to-all-start.3
  60.6 5.5 gather_fusion.1
  66.1 42.2 %all-to-all-done.3 = f16[8,1,64,2048]{3,2,1,0:T(8,128)(2,1)S(1)} async-done(((f16[8,1,64,2048]{3,2,1,0:T(8,128)(2,1)}), f16[8,1,64,2048]{3,2,1,0:T(8,128)(2,1)S(1)}, u32[]{:S(2)}, u32[]{:S(2)}) %all-to-all-start.3) | async-done | bytes 2097184 | tf_op jit(solution)/shard_map/all_to_all | solution.py:452
  108.2 4.4 all-to-all-start.1
  112.6 12.1 %pick_first.1 = f32[8,2,64,2048]{3,2,1,0:T(8,128)} custom-call(s32[48]{0:T(128)} %get-tuple-element.18.table_ref, f32[24,64,2048]{2,1,0:T(8,128)} %refs_2_.1, f32[24,64,2048]{2,1,0:T(8,128)} %refs_3_.1, f32[24,64,2048]{2,1,0:T(8,128)} %refs_2_.1, f32[24,64,2048]{2,1,0:T(8,128)} %refs_3_.1), custom_call_target="tpu_custom_call" | custom-call | flops 2000000000 | bytes 25165824 | tf_op jit(solution)/shard_map/pick_first/pallas_call | solution.py:135
  124.7 6.1 convert_element_type.187
  130.9 29.6 %all-to-all-done.1 = f16[8,1,64,2048]{3,2,1,0:T(8,128)(2,1)} async-done(((f16[8,1,64,2048]{3,2,1,0:T(8,128)(2,1)}), f16[8,1,64,2048]{3,2,1,0:T(8,128)(2,1)}, u32[]{:S(2)}, u32[]{:S(2)}) %all-to-all-start.1) | async-done | bytes 2097184 | tf_op jit(solution)/shard_map/all_to_all | solution.py:452
  160.4 4.6 all-to-all-start.4
  171.3 3.9 dynamic-slice_bitcast_fusion.2
  175.2 1.9 collective-permute-start.12
  178.1 1.9 collective-permute-start.13
  182.1 6.9 gather_fusion.2
  189.0 70.3 %collective-permute-done.12 = bf16[2304,256]{1,0:T(8,128)(2,1)S(1)} collective-permute-done((bf16[2304,256]{1,0:T(8,128)(2,1)}, bf16[2304,256]{1,0:T(8,128)(2,1)S(1)}, u32[]{:S(2)}, u32[]{:S(2)}) %collective-permute-start.12) | collective-permute-done | bytes 1179680 | tf_op jit(solution)/shard_map/ppermute | solution.py:459
  259.3 2.8 collective-permute-done.14
  262.2 22.6 %collective-permute-done.13 = bf16[2304,256]{1,0:T(8,128)(2,1)} collective-permute-done((bf16[2304,256]{1,0:T(8,128)(2,1)}, bf16[2304,256]{1,0:T(8,128)(2,1)}, u32[]{:S(2)}, u32[]{:S(2)}) %collective-permute-start.13) | collective-permute-done | bytes 1179680 | tf_op jit(solution)/shard_map/ppermute | solution.py:459
  284.7 2.9 fusion.2
  287.6 2.6 collective-permute-start.15
  295.6 11.9 %all-to-all-start.2 = ((f16[8,2,64,2048]{3,2,1,0:T(8,128)(2,1)}), f16[8,2,64,2048]{3,2,1,0:T(8,128)(2,1)}, u32[]{:S(2)}, u32[]{:S(2)}) async-start(f16[8,2,64,2048]{3,2,1,0:T(8,128)(2,1)} %bitcast.63), calls=%async_computation.2 | async-start | bytes 8388608 | tf_op jit(solution)/shard_map/all_to_all | solution.py:452
  307.5 79.0 %collective-permute-done.15 = bf16[2304,256]{1,0:T(8,128)(2,1)} collective-permute-done((bf16[2304,256]{1,0:T(8,128)(2,1)S(1)}, bf16[2304,256]{1,0:T(8,128)(2,1)}, u32[]{:S(2)}, u32[]{:S(2)}) %collective-permute-start.15) | collective-permute-done | bytes 1179680 | tf_op jit(solution)/shard_map/ppermute | solution.py:488
  386.5 2.6 add_convert_fusion.rest_0_
  389.0 8.2 %collective-permute-start.18 = (bf16[2304,256]{1,0:T(8,128)(2,1)}, bf16[2304,256]{1,0:T(8,128)(2,1)}, u32[]{:S(2)}, u32[]{:S(2)}) collective-permute-start(bf16[2304,256]{1,0:T(8,128)(2,1)} %add_convert_fusion.rest_0_), channel_id=1, source_target_pairs={{0,3},{1,0},{2,1},{3,2},{4,7},{5,4},{6,5},{7,6},{8,11},{9,8},{10,9... | collective-permute-start | bytes 3538952 | tf_op jit(solution)/shard_map/ppermute | solution.py:459
  397.3 2.6 collective-permute-start.17
  402.4 1.2 fusion.16
  403.6 26.9 %collective-permute-done.18.rest_3_ = bf16[2304,256]{1,0:T(8,128)(2,1)} collective-permute-done((bf16[2304,256]{1,0:T(8,128)(2,1)}, bf16[2304,256]{1,0:T(8,128)(2,1)}, u32[]{:S(2)}, u32[]{:S(2)}) %collective-permute-start.18) | collective-permute-done | bytes 1179680 | tf_op jit(solution)/shard_map/ppermute | solution.py:459
  430.5 40.8 %collective-permute-done.17.rest_2_ = bf16[2304,256]{1,0:T(8,128)(2,1)} collective-permute-done((bf16[2304,256]{1,0:T(8,128)(2,1)}, bf16[2304,256]{1,0:T(8,128)(2,1)}, u32[]{:S(2)}, u32[]{:S(2)}) %collective-permute-start.17) | collective-permute-done | bytes 1179680 | tf_op jit(solution)/shard_map/ppermute | solution.py:459
  471.3 73.5 %wide_solve.1 = f32[2048,512]{1,0:T(8,128)} custom-call(f32[3]{0:T(128)} %pad_maximum_fusion.coef_ref, s32[4]{0:T(128)} %and_select_fusion.turn_ref, f32[36]{0:T(128)} %constant.109.clone.table_ref, f32[2048,512]{1,0:T(8,128)} %get-tuple-element.30.merged_ref, bf16[2304,256]{1,0:T(8,128)(2,1)} %add_convert_fusion.rest_0_, ...), custom_call_target="tpu_custom_call" | custom-call | flops 51539607552 | bytes 8388608 | tf_op jit(solution)/shard_map/wide_solve/pallas_call | solution.py:416
  544.9 4.0 convert_element_type.184.data_ref
  548.8 2.4 convert_element_type.186.data_ref
  551.2 6.6 convert_element_type.188.data_ref
  557.8 14.3 %shard_map.94 = (f32[6,512,2048]{2,1,0:T(8,128)}, f32[4,2,64,2048]{3,2,1,0:T(8,128)}) custom-call(s32[4]{0:T(128)} %add_multiply_fusion.row_ref, f32[48]{0:T(128)} %div.46.scale_ref, f32[6]{0:T(128)} %copy-done.4, f32[6]{0:T(128)} %get-tuple-element.76.factor_ref, f32[6]{0:T(128)} %get-tuple-element.75.ratio_ref, ...), custom_call_target="tpu_custom_call" | custom-call | flops 6979321856 | bytes 25165824 | tf_op jit(solution)/shard_map/pallas_call | solution.py:208
  572.1 9.5 %shard_map.95 = (f32[6,512,2048]{2,1,0:T(8,128)}, f32[4,1,64,2048]{3,2,1,0:T(8,128)}) custom-call(s32[4]{0:T(128)} %add_multiply_fusion.row_ref, f32[48]{0:T(128)} %div.46.scale_ref, f32[6]{0:T(128)} %copy-done.4, f32[6]{0:T(128)} %get-tuple-element.76.factor_ref, f32[6]{0:T(128)} %get-tuple-element.75.ratio_ref, ...), custom_call_target="tpu_custom_call", output_to_operand_aliasing={{0}: (6, {})} | custom-call | flops 3489660928 | bytes 12582912 | tf_op jit(solution)/shard_map/pallas_call | solution.py:208
  581.6 6.6 convert_element_type.185.data_ref
  588.2 14.3 %shard_map.96 = (f32[6,512,2048]{2,1,0:T(8,128)}, f32[4,2,64,2048]{3,2,1,0:T(8,128)}) custom-call(s32[4]{0:T(128)} %add_multiply_fusion.row_ref, f32[48]{0:T(128)} %div.46.scale_ref, f32[6]{0:T(128)} %copy-done.4, f32[6]{0:T(128)} %get-tuple-element.76.factor_ref, f32[6]{0:T(128)} %get-tuple-element.75.ratio_ref, ...), custom_call_target="tpu_custom_call", output_to_operand_aliasing={{0}: (6, {})} | custom-call | flops 6979321856 | bytes 25165824 | tf_op jit(solution)/shard_map/pallas_call | solution.py:208
  602.5 9.5 %shard_map.97 = (f32[6,512,2048]{2,1,0:T(8,128)}, f32[4,1,64,2048]{3,2,1,0:T(8,128)}) custom-call(s32[4]{0:T(128)} %add_multiply_fusion.row_ref, f32[48]{0:T(128)} %div.46.scale_ref, f32[6]{0:T(128)} %copy-done.4, f32[6]{0:T(128)} %get-tuple-element.76.factor_ref, f32[6]{0:T(128)} %get-tuple-element.75.ratio_ref, ...), custom_call_target="tpu_custom_call", output_to_operand_aliasing={{0}: (6, {})} | custom-call | flops 3489660928 | bytes 12582912 | tf_op jit(solution)/shard_map/pallas_call | solution.py:208
  612.0 1.9 convert.21
  614.2 1.9 collective-permute-start
  616.5 1.5 collective-permute-start.8
  618.0 1.5 collective-permute-start.7
  620.2 1.5 copy-done.1
  622.3 4.7 collective-permute-done.2
  627.0 1.4 convert_multiply_fusion.9.rest_2_
  628.4 2.9 collective-permute-start.5
  631.4 1.4 convert_multiply_fusion.10.rest_1_
  632.7 1.5 convert_multiply_fusion.11.rest_0_
  634.2 4.0 collective-permute-done.8
  638.2 1.5 convert_multiply_fusion.6.rest_2_
  639.7 2.9 collective-permute-start.11
  642.7 1.4 convert_multiply_fusion.7.rest_1_
  644.7 2.0 collective-permute-start.10
  646.7 1.5 convert_multiply_fusion.8.rest_0_
  648.3 12.4 %collective-permute-done.5 = f16[2,64,2048]{2,1,0:T(8,128)(2,1)S(1)} collective-permute-done((f16[2,64,2048]{2,1,0:T(8,128)(2,1)S(1)}, f16[2,64,2048]{2,1,0:T(8,128)(2,1)S(1)}, u32[]{:S(2)}, u32[]{:S(2)}) %collective-permute-start.5) | collective-permute-done | bytes 524320 | tf_op jit(solution)/shard_map/ppermute | solution.py:459
  661.8 10.9 %collective-permute-done.11 = f16[2,64,2048]{2,1,0:T(8,128)(2,1)S(1)} collective-permute-done((f16[2,64,2048]{2,1,0:T(8,128)(2,1)S(1)}, f16[2,64,2048]{2,1,0:T(8,128)(2,1)S(1)}, u32[]{:S(2)}, u32[]{:S(2)}) %collective-permute-start.11) | collective-permute-done | bytes 524320 | tf_op jit(solution)/shard_map/ppermute | solution.py:459
  673.9 4.8 collective-permute-done.10
  679.9 2.2 collective-permute-done.9
  683.3 4.2 home.4.rest_3_
  687.5 3.1 home.5.rest_3_
  692.9 4.2 home.6.rest_3_
  697.2 3.1 home.7
  (83 shorter events, 24.5 us)
Async XLA Ops:
  30.0 24.6 %all-to-all-start = ((f32[8,1,128]{2,1,0:T(1,128)}), f32[8,1,128]{2,1,0:T(1,128)S(1)}, u32[]{:S(2)}, u32[]{:S(2)}) async-start(f32[8,1,128]{2,1,0:T(1,128)} %broadcast_in_dim.80), calls=%async_computation | async-start | bytes 8192 | tf_op jit(solution)/shard_map/all_to_all | solution.py:452
  54.6 53.7 %all-to-all-start.3 = ((f16[8,1,64,2048]{3,2,1,0:T(8,128)(2,1)}), f16[8,1,64,2048]{3,2,1,0:T(8,128)(2,1)S(1)}, u32[]{:S(2)}, u32[]{:S(2)}) async-start(f16[8,1,64,2048]{3,2,1,0:T(8,128)(2,1)} %bitcast.65), calls=%async_computation.3 | async-start | bytes 4194304 | tf_op jit(solution)/shard_map/all_to_all | solution.py:452
  108.2 52.2 %all-to-all-start.1 = ((f16[8,1,64,2048]{3,2,1,0:T(8,128)(2,1)}), f16[8,1,64,2048]{3,2,1,0:T(8,128)(2,1)}, u32[]{:S(2)}, u32[]{:S(2)}) async-start(f16[8,1,64,2048]{3,2,1,0:T(8,128)(2,1)} %bitcast.64), calls=%async_computation.1 | async-start | bytes 4194304 | tf_op jit(solution)/shard_map/all_to_all | solution.py:452
  160.4 135.2 %all-to-all-start.4 = ((f16[8,2,64,2048]{3,2,1,0:T(8,128)(2,1)}), f16[8,2,64,2048]{3,2,1,0:T(8,128)(2,1)}, u32[]{:S(2)}, u32[]{:S(2)}) async-start(f16[8,2,64,2048]{3,2,1,0:T(8,128)(2,1)} %convert_element_type.187), calls=%async_computation.4 | async-start | bytes 8388608 | tf_op jit(solution)/shard_map/all_to_all | solution.py:452
  171.3 8.8 %copy-start.5 = (s32[96]{0:T(128)S(1)}, s32[96]{0:T(128)}, u32[]{:S(2)}) copy-start(s32[96]{0:T(128)} %param.12) | copy-start | bytes 1156
  175.2 84.1 %collective-permute-start.12 = (bf16[2304,256]{1,0:T(8,128)(2,1)}, bf16[2304,256]{1,0:T(8,128)(2,1)S(1)}, u32[]{:S(2)}, u32[]{:S(2)}) collective-permute-start(bf16[2304,256]{1,0:T(8,128)(2,1)} %get-tuple-element.47), channel_id=1, source_target_pairs={{0,1},{1,2},{2,3},{3,0},{4,5},{5,6},{6,7},{7,4},{8,9},{9,10},{10,1... | collective-permute-start | bytes 3538952 | tf_op jit(solution)/shard_map/ppermute | solution.py:459
  177.1 85.1 %collective-permute-start.14 = (bf16[2304,256]{1,0:T(8,128)(2,1)}, bf16[2304,256]{1,0:T(8,128)(2,1)}, u32[]{:S(2)}, u32[]{:S(2)}) collective-permute-start(bf16[2304,256]{1,0:T(8,128)(2,1)} %get-tuple-element.48), channel_id=1, source_target_pairs={{0,3},{1,0},{2,1},{3,2},{4,7},{5,4},{6,5},{7,6},{8,11},{9,8},{10,9... | collective-permute-start | bytes 3538952 | tf_op jit(solution)/shard_map/ppermute | solution.py:459
  178.1 106.6 %collective-permute-start.13 = (bf16[2304,256]{1,0:T(8,128)(2,1)}, bf16[2304,256]{1,0:T(8,128)(2,1)}, u32[]{:S(2)}, u32[]{:S(2)}) collective-permute-start(bf16[2304,256]{1,0:T(8,128)(2,1)} %get-tuple-element.49), channel_id=1, source_target_pairs={{0,2},{1,3},{2,0},{3,1},{4,6},{5,7},{6,4},{7,5},{8,10},{9,11},{10,... | collective-permute-start | bytes 3538952 | tf_op jit(solution)/shard_map/ppermute | solution.py:459
  189.0 102.5 %copy-start.6 = (s32[8]{0:T(128)S(1)}, s32[8]{0:T(128)}, u32[]{:S(2)}) copy-start(s32[8]{0:T(128)} %get-tuple-element.21) | copy-start | bytes 100
  259.3 2.8 copy-start.3
  287.6 98.8 %collective-permute-start.15 = (bf16[2304,256]{1,0:T(8,128)(2,1)S(1)}, bf16[2304,256]{1,0:T(8,128)(2,1)}, u32[]{:S(2)}, u32[]{:S(2)}) collective-permute-start(bf16[2304,256]{1,0:T(8,128)(2,1)S(1)} %fusion.2), channel_id=1, source_target_pairs={{0,4},{1,5},{2,6},{3,7},{4,0},{5,1},{6,2},{7,3},{8,12},{9,13},{10,... | collective-permute-start | bytes 3538952 | tf_op jit(solution)/shard_map/ppermute | solution.py:488
  295.6 286.0 %all-to-all-start.2 = ((f16[8,2,64,2048]{3,2,1,0:T(8,128)(2,1)}), f16[8,2,64,2048]{3,2,1,0:T(8,128)(2,1)}, u32[]{:S(2)}, u32[]{:S(2)}) async-start(f16[8,2,64,2048]{3,2,1,0:T(8,128)(2,1)} %bitcast.63), calls=%async_computation.2 | async-start | bytes 8388608 | tf_op jit(solution)/shard_map/all_to_all | solution.py:452
  389.0 41.5 %collective-permute-start.18 = (bf16[2304,256]{1,0:T(8,128)(2,1)}, bf16[2304,256]{1,0:T(8,128)(2,1)}, u32[]{:S(2)}, u32[]{:S(2)}) collective-permute-start(bf16[2304,256]{1,0:T(8,128)(2,1)} %add_convert_fusion.rest_0_), channel_id=1, source_target_pairs={{0,3},{1,0},{2,1},{3,2},{4,7},{5,4},{6,5},{7,6},{8,11},{9,8},{10,9... | collective-permute-start | bytes 3538952 | tf_op jit(solution)/shard_map/ppermute | solution.py:459
  397.3 74.1 %collective-permute-start.17 = (bf16[2304,256]{1,0:T(8,128)(2,1)}, bf16[2304,256]{1,0:T(8,128)(2,1)}, u32[]{:S(2)}, u32[]{:S(2)}) collective-permute-start(bf16[2304,256]{1,0:T(8,128)(2,1)} %add_convert_fusion.rest_0_), channel_id=1, source_target_pairs={{0,2},{1,3},{2,0},{3,1},{4,6},{5,7},{6,4},{7,5},{8,10},{9,11},{10,... | collective-permute-start | bytes 3538952 | tf_op jit(solution)/shard_map/ppermute | solution.py:459
  399.8 71.5 %collective-permute-start.16 = (bf16[2304,256]{1,0:T(8,128)(2,1)}, bf16[2304,256]{1,0:T(8,128)(2,1)}, u32[]{:S(2)}, u32[]{:S(2)}) collective-permute-start(bf16[2304,256]{1,0:T(8,128)(2,1)} %add_convert_fusion.rest_0_), channel_id=1, source_target_pairs={{0,1},{1,2},{2,3},{3,0},{4,5},{5,6},{6,7},{7,4},{8,9},{9,10},{10,1... | collective-permute-start | bytes 3538952 | tf_op jit(solution)/shard_map/ppermute | solution.py:459
  402.4 142.5 %copy-start.4 = (f32[6]{0:T(128)}, f32[6]{0:T(128)S(1)}, u32[]{:S(2)}) copy-start(f32[6]{0:T(128)S(1)} %get-tuple-element.44.keep_ref) | copy-start | bytes 76
  612.0 4.2 copy-start.2
  614.1 12.9 %collective-permute-start.2 = (f16[1,64,2048]{2,1,0:T(8,128)(2,1)S(1)}, f16[1,64,2048]{2,1,0:T(8,128)(2,1)S(1)}, u32[]{:S(2)}, u32[]{:S(2)}) collective-permute-start(f16[1,64,2048]{2,1,0:T(8,128)(2,1)S(1)} %get-tuple-element.59), channel_id=1, source_target_pairs={{0,3},{1,0},{2,1},{3,2},{4,7},{5,4},{6,5},{7,6},{8,11},{9,8},{10,9... | collective-permute-start | bytes 786440 | tf_op jit(solution)/shard_map/ppermute | solution.py:459
  614.1 14.3 %collective-permute-start.1 = (f16[1,64,2048]{2,1,0:T(8,128)(2,1)S(1)}, f16[1,64,2048]{2,1,0:T(8,128)(2,1)S(1)}, u32[]{:S(2)}, u32[]{:S(2)}) collective-permute-start(f16[1,64,2048]{2,1,0:T(8,128)(2,1)S(1)} %get-tuple-element.60), channel_id=1, source_target_pairs={{0,2},{1,3},{2,0},{3,1},{4,6},{5,7},{6,4},{7,5},{8,10},{9,11},{10,... | collective-permute-start | bytes 786440 | tf_op jit(solution)/shard_map/ppermute | solution.py:459
  614.2 18.5 %collective-permute-start = (f16[1,64,2048]{2,1,0:T(8,128)(2,1)S(1)}, f16[1,64,2048]{2,1,0:T(8,128)(2,1)S(1)}, u32[]{:S(2)}, u32[]{:S(2)}) collective-permute-start(f16[1,64,2048]{2,1,0:T(8,128)(2,1)S(1)} %get-tuple-element.61), channel_id=1, source_target_pairs={{0,1},{1,2},{2,3},{3,0},{4,5},{5,6},{6,7},{7,4},{8,9},{9,10},{10,1... | collective-permute-start | bytes 786440 | tf_op jit(solution)/shard_map/ppermute | solution.py:459
  616.1 3.4 copy-start
  616.5 21.7 %collective-permute-start.8 = (f16[1,64,2048]{2,1,0:T(8,128)(2,1)S(1)}, f16[1,64,2048]{2,1,0:T(8,128)(2,1)S(1)}, u32[]{:S(2)}, u32[]{:S(2)}) collective-permute-start(f16[1,64,2048]{2,1,0:T(8,128)(2,1)S(1)} %get-tuple-element.56), channel_id=1, source_target_pairs={{0,3},{1,0},{2,1},{3,2},{4,7},{5,4},{6,5},{7,6},{8,11},{9,8},{10,9... | collective-permute-start | bytes 786440 | tf_op jit(solution)/shard_map/ppermute | solution.py:459
  618.0 21.7 %collective-permute-start.7 = (f16[1,64,2048]{2,1,0:T(8,128)(2,1)S(1)}, f16[1,64,2048]{2,1,0:T(8,128)(2,1)S(1)}, u32[]{:S(2)}, u32[]{:S(2)}) collective-permute-start(f16[1,64,2048]{2,1,0:T(8,128)(2,1)S(1)} %get-tuple-element.57), channel_id=1, source_target_pairs={{0,2},{1,3},{2,0},{3,1},{4,6},{5,7},{6,4},{7,5},{8,10},{9,11},{10,... | collective-permute-start | bytes 786440 | tf_op jit(solution)/shard_map/ppermute | solution.py:459
  619.5 2.2 copy-start.1
  627.0 17.7 %collective-permute-start.6 = (f16[1,64,2048]{2,1,0:T(8,128)(2,1)S(1)}, f16[1,64,2048]{2,1,0:T(8,128)(2,1)S(1)}, u32[]{:S(2)}, u32[]{:S(2)}) collective-permute-start(f16[1,64,2048]{2,1,0:T(8,128)(2,1)S(1)} %get-tuple-element.58), channel_id=1, source_target_pairs={{0,1},{1,2},{2,3},{3,0},{4,5},{5,6},{6,7},{7,4},{8,9},{9,10},{10,1... | collective-permute-start | bytes 786440 | tf_op jit(solution)/shard_map/ppermute | solution.py:459
  628.4 32.2 %collective-permute-start.5 = (f16[2,64,2048]{2,1,0:T(8,128)(2,1)S(1)}, f16[2,64,2048]{2,1,0:T(8,128)(2,1)S(1)}, u32[]{:S(2)}, u32[]{:S(2)}) collective-permute-start(f16[2,64,2048]{2,1,0:T(8,128)(2,1)S(1)} %get-tuple-element.53), channel_id=1, source_target_pairs={{0,3},{1,0},{2,1},{3,2},{4,7},{5,4},{6,5},{7,6},{8,11},{9,8},{10,9... | collective-permute-start | bytes 1572872 | tf_op jit(solution)/shard_map/ppermute | solution.py:459
  632.7 57.9 %collective-permute-start.4 = (f16[2,64,2048]{2,1,0:T(8,128)(2,1)S(1)}, f16[2,64,2048]{2,1,0:T(8,128)(2,1)S(1)}, u32[]{:S(2)}, u32[]{:S(2)}) collective-permute-start(f16[2,64,2048]{2,1,0:T(8,128)(2,1)S(1)} %get-tuple-element.54), channel_id=1, source_target_pairs={{0,2},{1,3},{2,0},{3,1},{4,6},{5,7},{6,4},{7,5},{8,10},{9,11},{10,... | collective-permute-start | bytes 1572872 | tf_op jit(solution)/shard_map/ppermute | solution.py:459
  638.2 53.6 %collective-permute-start.3 = (f16[2,64,2048]{2,1,0:T(8,128)(2,1)S(1)}, f16[2,64,2048]{2,1,0:T(8,128)(2,1)S(1)}, u32[]{:S(2)}, u32[]{:S(2)}) collective-permute-start(f16[2,64,2048]{2,1,0:T(8,128)(2,1)S(1)} %get-tuple-element.55), channel_id=1, source_target_pairs={{0,1},{1,2},{2,3},{3,0},{4,5},{5,6},{6,7},{7,4},{8,9},{9,10},{10,1... | collective-permute-start | bytes 1572872 | tf_op jit(solution)/shard_map/ppermute | solution.py:459
  639.7 33.0 %collective-permute-start.11 = (f16[2,64,2048]{2,1,0:T(8,128)(2,1)S(1)}, f16[2,64,2048]{2,1,0:T(8,128)(2,1)S(1)}, u32[]{:S(2)}, u32[]{:S(2)}) collective-permute-start(f16[2,64,2048]{2,1,0:T(8,128)(2,1)S(1)} %get-tuple-element.50), channel_id=1, source_target_pairs={{0,3},{1,0},{2,1},{3,2},{4,7},{5,4},{6,5},{7,6},{8,11},{9,8},{10,9... | collective-permute-start | bytes 1572872 | tf_op jit(solution)/shard_map/ppermute | solution.py:459
  644.7 34.0 %collective-permute-start.10 = (f16[2,64,2048]{2,1,0:T(8,128)(2,1)S(1)}, f16[2,64,2048]{2,1,0:T(8,128)(2,1)S(1)}, u32[]{:S(2)}, u32[]{:S(2)}) collective-permute-start(f16[2,64,2048]{2,1,0:T(8,128)(2,1)S(1)} %get-tuple-element.51), channel_id=1, source_target_pairs={{0,2},{1,3},{2,0},{3,1},{4,6},{5,7},{6,4},{7,5},{8,10},{9,11},{10,... | collective-permute-start | bytes 1572872 | tf_op jit(solution)/shard_map/ppermute | solution.py:459
  660.6 21.5 %collective-permute-start.9 = (f16[2,64,2048]{2,1,0:T(8,128)(2,1)S(1)}, f16[2,64,2048]{2,1,0:T(8,128)(2,1)S(1)}, u32[]{:S(2)}, u32[]{:S(2)}) collective-permute-start(f16[2,64,2048]{2,1,0:T(8,128)(2,1)S(1)} %get-tuple-element.52), channel_id=1, source_target_pairs={{0,1},{1,2},{2,3},{3,0},{4,5},{5,6},{6,7},{7,4},{8,9},{9,10},{10,1... | collective-permute-start | bytes 1572872 | tf_op jit(solution)/shard_map/ppermute | solution.py:459
